TPU v7x, 256 devices: a whole 4x4x8 slice. The times are simulated.
256 devices in a mesh: dp: 128 (over y, x, z), rep: 2 (over core).
Axes of the slice: x: 4, y: 4, z: 8, core: 2. Of those that a mesh axis runs over, the one named last changes fastest.
Arguments:
- tokens: bfloat16 [2, 1024, 4096], P('rep'), may hold values from -6 to 6
- cotangent: bfloat16 [2, 1024, 4096], P('rep'), may hold values from -6 to 6
- lengths: int32 [2, 2], P('rep'), may hold values from 1 to 512
- w_in: bfloat16 [4096, 2, 14336], P(None, None, 'dp'), may hold values from -0.09375 to 0.09375
- w_down: bfloat16 [14336, 4096], P('dp'), may hold values from -0.046875 to 0.046875
Outputs:
- d_tokens: float32 [2, 1024, 4096], P('rep', 'dp')
- weight_grads: float32 [4096, 3, 14336], P('rep', None, 'dp')
All inputs are finite; a program needn't handle non-finite values.
Results may differ from a plain program's by a relative error of at most 0.0029.
Values sent between devices are 32-bit elements; how exact they have to be, the bound alone decides.
No kernel may reach another device: no remote copies, remote signals or barrier semaphores. Data moves between devices by JAX's collectives and lax.ppermute only.
A program may use at most 192 MiB of HBM per device.

v0:
```python
import jax
import jax.numpy as jnp
from jax import lax
from jax.sharding import Mesh
from jax.sharding import PartitionSpec as P

DP = ("dp_0", "dp_1", "dp_2")


GRAD_SCALE = 0.03125


def in_blocks(value, dim, length):
    dims = value.shape
    tiles = value.reshape(*dims[:dim], length, dims[dim] // length, *dims[dim + 1 :])
    return jnp.moveaxis(tiles, dim, 0)


def cut_rows(length, count):
    step = length // count
    if step >= 8:
        step -= step % 8
    return [step * k for k in range(1, count)]


def own_block(tiles, axes, order):
    dims = [lax.axis_size(a) for a in axes]
    tiles = tiles.reshape(*dims, *tiles.shape[1:])
    tiles = tiles.transpose(*order, *range(len(axes), tiles.ndim))
    tiles = tiles.reshape(-1, *tiles.shape[len(axes) :])
    for k in order:
        tiles = lax.psum_scatter(tiles, axes[k], scatter_dimension=0, tiled=True)
    return tiles[0]


def sum_at_once(value, axes, dim):
    tiles = in_blocks(value, dim, lax.axis_size(axes))
    split_at = max(range(1, max(2, tiles.ndim - 1)), key=lambda d: tiles.shape[d])
    count, gathered = (len(axes), [])
    for leading, share in enumerate(
        jnp.split(tiles, cut_rows(tiles.shape[split_at], count), axis=split_at)
    ):
        if share.size:
            order = [(leading + k) % count for k in range(count)]
            gathered.append(own_block(share, axes, order))
    return jnp.concatenate(gathered, axis=split_at - 1)


def sent_and_summed(value, axis, dim):
    length = lax.axis_size(axis)
    tiles = lax.all_to_all(in_blocks(value, dim, length), axis, 0, 0, tiled=True)
    return jnp.sum(tiles, axis=0)


def per_device(tokens, cotangent, lengths, w_in, w_down):
    rows = tokens.shape[1]
    width = tokens.shape[2]
    seqs = lengths.shape[1]
    slots = rows // seqs
    hidden_units = w_down.shape[0]
    position = jnp.arange(rows)
    owner_seq = (position // slots)[:, None] == jnp.arange(seqs)[None, :]
    limit = jnp.sum(jnp.where(owner_seq, lengths[0][None, :], 0), axis=1)
    is_alive = position % slots < limit
    zero_value = jnp.zeros((), jnp.bfloat16)
    live_x = jnp.where(is_alive[:, None], tokens[0], zero_value)
    live_dy = jnp.where(is_alive[:, None], cotangent[0], zero_value)
    w_flat = w_in.reshape(width, 2 * hidden_units)
    gate_up = jnp.dot(live_x, w_flat, preferred_element_type=jnp.float32)
    gate = gate_up[:, :hidden_units]
    upward = gate_up[:, hidden_units:]
    sigmoid_gate = jax.nn.sigmoid(gate)
    activated = gate * sigmoid_gate
    hidden = (activated * upward).astype(jnp.bfloat16)
    d_hidden = lax.dot_general(
        live_dy, w_down, (((1,), (1,)), ((), ())), preferred_element_type=jnp.float32
    )
    d_gate = d_hidden * upward * sigmoid_gate * (1.0 + gate * (1.0 - sigmoid_gate))
    d_up = d_hidden * activated
    d_in = jnp.concatenate([d_gate, d_up], axis=1).astype(jnp.bfloat16)
    partial_rows = lax.dot_general(
        d_in, w_flat, (((1,), (1,)), ((), ())), preferred_element_type=jnp.float32
    )
    shard = sum_at_once(partial_rows, DP, 0)
    grad_in = lax.dot_general(
        live_x, d_in, (((0,), (0,)), ((), ())), preferred_element_type=jnp.float32
    )
    grad_down = lax.dot_general(
        live_dy, hidden, (((0,), (0,)), ((), ())), preferred_element_type=jnp.float32
    )
    combined = (
        jnp.concatenate([grad_in.reshape(width, 2, hidden_units), grad_down[:, None, :]], axis=1)
        * GRAD_SCALE
    )
    shared = sent_and_summed(combined, "rep", 0)
    return (shard[None], shared)


def solution(mesh):
    split = Mesh(mesh.devices.reshape(4, 4, 8, mesh.shape["rep"]), ("dp_0", "dp_1", "dp_2", "rep"))
    in_specs = (
        P("rep", None, None),
        P("rep", None, None),
        P("rep", None),
        P(None, None, DP),
        P(DP, None),
    )
    out_specs = (P("rep", DP, None), P("rep", None, DP))
    return jax.shard_map(
        per_device, mesh=split, in_specs=in_specs, out_specs=out_specs, check_vma=False
    )
```

profile of v0, /device:TPU:8, one launch (start us, length us, event | category | flops | bytes accessed | tf_op | source)
XLA Modules:
  0.0 498.1 jit_solution(6122138001584359536)
XLA Ops:
  8.0 0.0 reduce-scatter.3.cloned.1.call-start
  8.1 0.9 fusion.13
  8.9 0.6 copy-done
  9.5 6.3 %fusion = f32[1024,224]{0,1:T(8,128)S(1)} fusion(bf16[4096,224]{0,1:T(8,128)(2,1)S(1)} %bitcast.63, bf16[1,1024,4096]{2,1,0:T(8,128)(2,1)} %param.5, pred[1024]{0:T(1024)(128)(4,1)S(1)} %fusion.14), kind=kOutput, calls=%fused_computation | convolution fusion | flops 1883242496 | bytes 11142144 | tf_op jit(solution)/shard_map/dot_general | solution.py:69
  15.8 3.5 multiply_convert_fusion.2
  19.3 0.2 copy.30
  19.5 0.2 copy.32
  19.7 0.2 copy.31
  19.9 0.2 copy.33
  20.1 2.4 fusion.5
  22.5 5.7 %copy-done.2 = f32[128,8,4096]{2,0,1:T(8,128)} copy-done((f32[128,8,4096]{2,0,1:T(8,128)}, f32[128,8,4096]{2,0,1:T(8,128)S(1)}, u32[]{:S(2)}) %copy-start.2) | copy-done | bytes 16777240
  28.3 3.8 fusion.24
  32.1 0.0 all-reduce.14.cloned.1.call-start
  32.1 7.4 %copy.35 = f32[4,8,4,2,4096]{4,3,2,1,0:T(2,128)} copy(f32[4,8,4,2,4096]{4,1,0,2,3:T(8,128)} %bitcast.67) | data formatting | bytes 8388608 | tf_op jit(solution)/shard_map/transpose | solution.py:29
  39.5 0.0 reduce-scatter.5.cloned.1.call-start
  39.6 43.7 %reduce-scatter.3.cloned.1.call-done = f32[32,2,4096]{2,0,1:T(8,128)} async-done(((f32[128,2,4096]{2,0,1:T(8,128)}), f32[32,2,4096]{2,0,1:T(8,128)}) %reduce-scatter.3.cloned.1.call-update) | async-done | bytes 1048592 | tf_op jit(solution)/shard_map/reduce_scatter | solution.py:32
  83.3 0.2 all-reduce.18.cloned.1.call-start
  83.5 7.7 %split.14 = f32[128,4,4096]{2,0,1:T(8,128)} slice(f32[128,8,4096]{2,0,1:T(8,128)} %copy-done.2), slice={[0:128], [4:8], [0:4096]} | slice | bytes 16777216 | tf_op jit(solution)/shard_map/split | solution.py:41
  91.2 12.1 %copy.36 = f32[8,4,4,4,4096]{4,3,2,1,0:T(4,128)} copy(f32[8,4,4,4,4096]{4,0,2,1,3:T(8,128)} %bitcast.65) | data formatting | bytes 16777216 | tf_op jit(solution)/shard_map/transpose | solution.py:29
  103.3 0.7 dynamic-slice.2
  104.6 35.6 %all-reduce.14.cloned.1.call-done = f32[128,2,4096]{2,1,0:T(2,128)} async-done(((f32[128,2,4096]{2,1,0:T(2,128)}), f32[128,2,4096]{2,1,0:T(2,128)}) %all-reduce.14.cloned.1.call-update) | async-done | bytes 4194320
  140.2 2.3 constant_dynamic-slice_fusion.3
  142.5 26.3 %reduce-scatter.5.cloned.1.call-done = f32[8,2,4096]{2,0,1:T(8,128)} async-done(((f32[32,2,4096]{2,0,1:T(8,128)}), f32[8,2,4096]{2,0,1:T(8,128)}) %reduce-scatter.5.cloned.1.call-update) | async-done | bytes 262160 | tf_op jit(solution)/shard_map/reduce_scatter | solution.py:32
  168.8 1.8 copy.34
  170.6 0.3 all-reduce.20.cloned.1.call-start
  170.9 0.6 dynamic-slice
  172.6 7.2 %fusion.2 = bf16[4096,1024]{0,1:T(8,128)(2,1)} fusion(bf16[1,1024,4096]{2,1,0:T(8,128)(2,1)} %param.5, pred[1024]{0:T(1024)(128)(4,1)S(1)} %fusion.14), kind=kLoop, calls=%fused_computation.5 | loop fusion | flops 4194304 | bytes 16778240 | tf_op jit(solution)/shard_map/dot_general | solution.py:85
  179.8 11.2 %copy.40 = bf16[4096,1024]{1,0:T(8,128)(2,1)} copy(bf16[4096,1024]{0,1:T(8,128)(2,1)} %fusion.2) | data formatting | bytes 16777216 | tf_op jit(solution)/shard_map/dot_general | solution.py:85
  191.0 7.2 %fusion.3 = bf16[4096,1024]{0,1:T(8,128)(2,1)} fusion(bf16[1,1024,4096]{2,1,0:T(8,128)(2,1)} %param.6, pred[1024]{0:T(1024)(128)(4,1)S(1)} %fusion.14), kind=kLoop, calls=%fused_computation.6 | loop fusion | flops 4194304 | bytes 16778240 | tf_op jit(solution)/shard_map/dot_general | solution.py:88
  198.2 12.0 %copy.41 = bf16[4096,1024]{1,0:T(8,128)(2,1)} copy(bf16[4096,1024]{0,1:T(8,128)(2,1)} %fusion.3) | data formatting | bytes 16777216 | tf_op jit(solution)/shard_map/dot_general | solution.py:88
  210.3 8.0 %fusion.25 = f32[2,2048,2,112]{1,3,2,0:T(8,128)} fusion(bf16[2,2048,1024,1]{2,1,3,0:T(8,128)(2,1)} %bitcast.69, bf16[2,112,1024,1]{2,1,0,3:T(8,128)(2,1)S(1)} %bitcast.72), kind=kOutput, calls=%fused_computation.46 | convolution fusion | flops 1879048192 | bytes 12517376 | tf_op jit(solution)/shard_map/dot_general | solution.py:85
  218.3 165.9 %all-reduce.18.cloned.1.call-done = (f32[128,4,4096]{2,1,0:T(4,128)}, f32[32,2,4096]{2,1,0:T(2,128)}, f32[8,2,4096]{2,1,0:T(2,128)}) async-done(((f32[128,4,4096]{2,1,0:T(4,128)}, f32[32,2,4096]{2,1,0:T(2,128)}, f32[8,2,4096]{2,1,0:T(2,128)}), (f32[128,4,4096]{2,1,0:T(4,128)}, f32[32,2,4096]{2,1,0:T(2,128)}, f32[8,2,4096]{2,1,0:T(2,128)})) %all-reduce.18.cloned.1.call-update) | async-done | bytes 9699344
  384.2 2.3 constant_dynamic-slice_fusion.1
  386.5 1.6 constant_dynamic-slice_fusion.2
  388.1 6.3 %convolution_bitcast_fusion = f32[2,2048,1,112]{1,3,2,0:T(8,128)S(1)} fusion(bf16[2,2048,1024]{2,1,0:T(8,128)(2,1)} %bitcast.68, f32[1024,224]{0,1:T(8,128)S(1)} %copy-done.10), kind=kOutput, calls=%fused_computation.8 | convolution fusion | flops 940212224 | bytes 11141120 | tf_op jit(solution)/shard_map/dot_general | solution.py:88
  394.5 3.2 maximum_multiply_fusion
  397.7 6.0 %all-to-all-start = ((f32[2,2048,3,112]{1,3,2,0:T(8,128)}), f32[2,2048,3,112]{1,3,2,0:T(8,128)}, u32[]{:S(2)}, u32[]{:S(2)}) async-start(f32[2,2048,3,112]{1,3,2,0:T(8,128)} %maximum_multiply_fusion), calls=%async_computation.2 | async-start | bytes 11010048 | tf_op jit(solution)/shard_map/all_to_all | solution.py:51
  403.8 0.0 all-reduce.16.cloned.1.call-start
  403.8 0.6 dynamic-slice.6
  405.1 4.1 all-to-all-done
  409.2 4.9 reduce_sum.19
  414.1 1.3 dynamic-slice_bitcast_fusion.2
  415.4 23.1 %all-reduce.20.cloned.1.call-done = (f32[16,4,4096]{2,1,0:T(4,128)}, f32[4,2,4096]{2,1,0:T(2,128)}) async-done(((f32[16,4,4096]{2,1,0:T(4,128)}, f32[4,2,4096]{2,1,0:T(2,128)}), (f32[16,4,4096]{2,1,0:T(4,128)}, f32[4,2,4096]{2,1,0:T(2,128)})) %all-reduce.20.cloned.1.call-update) | async-done | bytes 1179664
  438.5 1.7 constant_dynamic-slice_fusion
  440.2 1.4 dynamic-slice_bitcast_fusion.1
  441.6 46.7 %all-reduce.16.cloned.1.call-done = f32[4,4,4096]{2,1,0:T(4,128)} async-done(((f32[4,4,4096]{2,1,0:T(4,128)}), f32[4,4,4096]{2,1,0:T(4,128)}) %all-reduce.16.cloned.1.call-update) | async-done | bytes 262160
  488.3 1.5 dynamic-slice_bitcast_fusion
  489.7 0.7 maximum_bitcast_fusion
  (29 shorter events, 0.2 us)
Async XLA Ops:
  8.0 1.5 copy-start
  8.0 75.2 %reduce-scatter.3.cloned.1.call-start = ((), (), s32[]{:S(2)}) async-start(), calls=%async_computation.3 | async-start | bytes 5242880 | tf_op jit(solution)/shard_map/reduce_scatter | solution.py:32
  9.5 6.3 %copy-start.3 = (bf16[1,1024,4096]{2,1,0:T(8,128)(2,1)S(1)}, bf16[1,1024,4096]{2,1,0:T(8,128)(2,1)}, u32[]{:S(2)}) copy-start(bf16[1,1024,4096]{2,1,0:T(8,128)(2,1)} %param.6) | copy-start | bytes 25165828
  9.5 6.3 %copy-start.5 = (bf16[112,4096]{1,0:T(8,128)(2,1)S(1)}, bf16[112,4096]{1,0:T(8,128)(2,1)}, u32[]{:S(2)}) copy-start(bf16[112,4096]{1,0:T(8,128)(2,1)} %param.9) | copy-start | bytes 2752516
  15.8 3.5 copy-start.9
  22.5 5.7 %copy-start.2 = (f32[128,8,4096]{2,0,1:T(8,128)}, f32[128,8,4096]{2,0,1:T(8,128)S(1)}, u32[]{:S(2)}) copy-start(f32[128,8,4096]{2,0,1:T(8,128)S(1)} %fusion.5) | copy-start | bytes 50331652
  32.1 108.1 %all-reduce.14.cloned.1.call-start = ((), (), s32[]{:S(2)}) async-start(), calls=%async_computation.5 | async-start | bytes 8388608
  39.5 129.2 %reduce-scatter.5.cloned.1.call-start = ((), (), s32[]{:S(2)}) async-start(), calls=%async_computation.4 | async-start | bytes 1310720 | tf_op jit(solution)/shard_map/reduce_scatter | solution.py:32
  83.3 300.9 %all-reduce.18.cloned.1.call-start = ((), (), s32[]{:S(2)}) async-start(), calls=%async_computation.7 | async-start | bytes 19398656
  91.2 12.1 %copy-start.8 = (u32[256]{0:T(256)S(1)}, u32[256]{0:T(256)}, u32[]{:S(2)}) copy-start(u32[256]{0:T(256)} %constant.51) | copy-start | bytes 3076
  103.3 67.6 %copy-start.7 = (u32[256]{0:T(256)S(1)}, u32[256]{0:T(256)}, u32[]{:S(2)}) copy-start(u32[256]{0:T(256)} %constant.47) | copy-start | bytes 3076
  170.6 267.9 %all-reduce.20.cloned.1.call-start = ((), (), s32[]{:S(2)}) async-start(), calls=%async_computation.8 | async-start | bytes 2359296
  210.3 177.8 %copy-start.10 = (f32[1024,224]{0,1:T(8,128)S(1)}, f32[1024,224]{0,1:T(8,128)}, u32[]{:S(2)}) copy-start(f32[1024,224]{0,1:T(8,128)} %copy-done.9) | copy-start | bytes 2752516
  388.1 6.3 %copy-start.4 = (f32[2,2048,2,112]{1,3,2,0:T(8,128)S(1)}, f32[2,2048,2,112]{1,3,2,0:T(8,128)}, u32[]{:S(2)}) copy-start(f32[2,2048,2,112]{1,3,2,0:T(8,128)} %fusion.25) | copy-start | bytes 11010052
  394.5 9.3 %copy-start.6 = (u32[256]{0:T(256)S(1)}, u32[256]{0:T(256)}, u32[]{:S(2)}) copy-start(u32[256]{0:T(256)} %constant.59) | copy-start | bytes 3076
  394.5 96.0 %copy-start.1 = (bf16[4096,2,112]{0,2,1:T(8,128)(2,1)S(1)}, bf16[4096,2,112]{0,2,1:T(8,128)(2,1)}, u32[]{:S(2)}) copy-start(bf16[4096,2,112]{0,2,1:T(8,128)(2,1)} %param.8) | copy-start | bytes 5505028
  397.7 11.5 %all-to-all-start = ((f32[2,2048,3,112]{1,3,2,0:T(8,128)}), f32[2,2048,3,112]{1,3,2,0:T(8,128)}, u32[]{:S(2)}, u32[]{:S(2)}) async-start(f32[2,2048,3,112]{1,3,2,0:T(8,128)} %maximum_multiply_fusion), calls=%async_computation.2 | async-start | bytes 11010048 | tf_op jit(solution)/shard_map/all_to_all | solution.py:51
  403.8 84.5 %all-reduce.16.cloned.1.call-start = ((), (), s32[]{:S(2)}) async-start(), calls=%async_computation.6 | async-start | bytes 524288
Sparse Core Ops, SparseCore 0:
  32.2 51.0 reduce-scatter.2
  388.2 50.1 all-reduce.19
Sparse Core Ops, SparseCore 1:
  39.6 100.5 all-reduce.13
  142.6 26.1 reduce-scatter.4
  171.8 212.4 all-reduce.17
  440.3 47.9 all-reduce.15
where the time goes:
time: 499 us; the launch traced here: 498 us
  waiting for transfers between devices  345 us (69%)
  local copies, waits for them, and re-layouts  77 us (15%)
  matrix products  26.5 us (5%)
  other arithmetic  24.2 us (5%)
  between operations  18.3 us (4%)
  starting transfers between devices  6.68 us (1%)
    unnamed x10, waiting for transfers between devices  271 us
    reduce_scatter x2, waiting for transfers between devices, own_block(): tiles = lax.psum_scatter(tiles, axes[k], scatter_dimension=0, tiled=True)  69.9 us
    transpose x2, local copies, waits for them, and re-layouts, own_block(): tiles = tiles.transpose(*order, *range(len(axes), tiles.ndim))  19.5 us
    unnamed x29, local copies, waits for them, and re-layouts  16 us
    dot_general x1, local copies, waits for them, and re-layouts, per_device(): lax.dot_general(live_dy, hidden, (((0,), (0,)), ((), ())), preferred_elem...  12 us
    split x2, local copies, waits for them, and re-layouts, sum_at_once(): jnp.split(tiles, cut_rows(tiles.shape[split_at], count), axis=split_at)  11.5 us
    dot_general x1, local copies, waits for them, and re-layouts, per_device(): lax.dot_general(live_x, d_in, (((0,), (0,)), ((), ())), preferred_element...  11.2 us
  transfers between devices with their start and end apart: 7, of which 7 were waited for; matrix products, arithmetic and copies ran while one was open for 19% of the time, Pallas kernels for 0%

commit v1 on v0

v1 whole, which is shorter than its diff:
```python
import jax
import jax.numpy as jnp
import numpy as np
from jax import lax
from jax.sharding import Mesh
from jax.sharding import PartitionSpec as P


DP = ("dp_0", "dp_1", "dp_2")
ALL = DP + ("rep",)
SWAP = [(0, 1), (1, 0)]
GRAD_SCALE = 0.03125
FIRST, SECOND = (1, 0), (0, 1)


def lines(dims, axis_of_core):
    index = np.arange(int(np.prod(dims))).reshape(dims)
    groups = []
    for core, axis in enumerate(axis_of_core):
        moved = np.moveaxis(index[..., core], axis, -1)
        groups += moved.reshape(-1, dims[axis]).tolist()
    return groups


def hop(value, dims, axis_of_core, step):
    pairs = []
    for line in lines(dims, axis_of_core):
        pairs += [(line[k], line[(k + step) % len(line)]) for k in range(len(line))]
    return lax.ppermute(value, ALL, sorted(pairs))


def exchange(value, dims, axis_of_core):
    groups = lines(dims, axis_of_core)
    return lax.all_to_all(value, ALL, 0, 0, tiled=True, axis_index_groups=groups)


def dot(a, b, over_a, over_b):
    return lax.dot_general(
        a, b, (((over_a,), (over_b,)), ((), ())), preferred_element_type=jnp.float32
    )


def per_device(tokens, cotangent, lengths, w_in, w_down, dims):
    ny, nx, nz, nr = dims
    x, dy = tokens[0], cotangent[0]
    rows, width = x.shape
    slots = rows // lengths.shape[1]
    units = w_down.shape[0]
    half = width // nr
    own_rows = rows // (ny * nx * nz)
    rep = lax.axis_index("rep")
    north = rep == 0
    me = jnp.where(north, lax.axis_index("dp_1"), lax.axis_index("dp_0"))
    one = jnp.minimum(lengths[0, 0], 1).astype(jnp.float32)

    w_t = w_in.transpose(1, 2, 0).reshape(2 * units, width)
    w_mine = lax.dynamic_slice_in_dim(w_t, rep * half, half, 1)
    w_gate, w_up = w_mine[:units].astype(jnp.float32), w_mine[units:].astype(jnp.float32)
    next_gate = hop(w_gate, dims, FIRST, -1)
    last_up = hop(w_up, dims, FIRST, 1)
    next_up = hop(w_up, dims, FIRST, -1)
    last_gate = hop(w_gate, dims, FIRST, 1)
    far_gate = hop(next_gate, dims, FIRST, -1)
    far_up = hop(last_up, dims, FIRST, 1)

    position = jnp.arange(rows)
    limit = jnp.where(position < slots, lengths[0, 0], slots + lengths[0, 1])
    is_alive = (position < limit)[None, :]
    gate_up = dot(w_t, x, 1, 1)
    gate, upward = gate_up[:units], gate_up[units:]
    sig = jax.nn.sigmoid(gate)
    activated = gate * sig
    hidden = jnp.where(is_alive, activated * upward, 0.0).astype(jnp.bfloat16)
    d_hidden = jnp.where(is_alive, dot(w_down, dy, 1, 1), 0.0)
    d_gate = d_hidden * upward * sig * (1.0 + gate * (1.0 - sig))
    d_up = d_hidden * activated
    d_in = jnp.concatenate([d_gate, d_up], axis=0).astype(jnp.bfloat16)

    each = rows // (ny * nx)
    order = (position // each % ny) * (nx * each) + (position // (ny * each)) * each + position % each
    turn = (position[:, None] == order[None, :]).astype(jnp.bfloat16)
    turned = dot(d_in, turn, 1, 0)
    plain = d_in.astype(jnp.float32)
    theirs = lax.ppermute(jnp.where(north, plain, turned), "rep", SWAP)
    ours = jnp.where(north, turned, plain)

    def spread(d):
        blocks = d.reshape(2 * units, 4, rows // 4).transpose(1, 0, 2)
        got = exchange(blocks, dims, FIRST)
        twice = jnp.concatenate([got, got])
        return (lax.dynamic_slice_in_dim(twice, me, 4, 0) * one).astype(jnp.bfloat16)

    d_theirs, d_ours = spread(theirs), spread(ours)

    g = jnp.concatenate([dot(d_in, x, 1, 0), dot(hidden, dy, 1, 0)])
    low, high = g[:, :half], g[:, half:]
    away, kept = jnp.where(north, high, low), jnp.where(north, low, high)
    back = lax.ppermute(away, "rep", SWAP)

    arrived = lambda *parts: [(p * one).astype(jnp.bfloat16) for p in parts]
    near = jnp.concatenate([w_mine] + arrived(next_gate, next_up, last_gate, last_up))
    far = jnp.concatenate(arrived(far_gate, far_up))

    def row_sums(d):
        close = jnp.concatenate([d[0], d[1], d[3]])
        partial = dot(close, near, 0, 0) + dot(d[2], far, 0, 0)
        got = exchange(partial.reshape(4, rows // 16, half), dims, SECOND)
        part = jnp.sum(got, axis=0).reshape(nz, own_rows, half)
        return jnp.sum(lax.all_to_all(part, "dp_2", 0, 0, tiled=True), axis=0)

    sum_theirs = row_sums(d_theirs)
    sum_ours = row_sums(d_ours)
    other_half = lax.ppermute(sum_theirs, "rep", SWAP)
    shard = jnp.concatenate(
        [jnp.where(north, sum_ours, other_half), jnp.where(north, other_half, sum_ours)], axis=1
    )
    shared = (kept + back) * GRAD_SCALE
    return shard[None], shared.reshape(3, units, half).transpose(2, 0, 1)


def solution(mesh):
    dims = (4, 4, 8, mesh.shape["rep"])
    split = Mesh(mesh.devices.reshape(dims), ALL)
    in_specs = (
        P("rep", None, None),
        P("rep", None, None),
        P("rep", None),
        P(None, None, DP),
        P(DP, None),
    )
    out_specs = (P("rep", DP, None), P("rep", None, DP))

    def body(*args):
        return per_device(*args, dims)

    return jax.shard_map(
        body, mesh=split, in_specs=in_specs, out_specs=out_specs, check_vma=False
    )
```

time: 499 us -> 158 us (0.32)
  waiting for transfers between devices: 345 us -> 48.9 us
  local copies, waits for them, and re-layouts: 77 us -> 5.69 us
  starting transfers between devices: 6.68 us -> 38 us
  between operations: 18.3 us -> 2.2 us
  matrix products: 26.5 us -> 33.2 us
    unnamed x10 -> x0, waiting for transfers between devices: 271 us -> none
    reduce_scatter x2 -> x0, waiting for transfers between devices: 69.9 us -> none  [own_block(): tiles = lax.psum_scatter(tiles, axes[k], scatter_dimension=0, tiled=True)]
    all_to_all x1 -> x6, waiting for transfers between devices: 4.1 us -> 43.4 us  [the longest x2 24.4 us: row_sums(): return jnp.sum(lax.all_to_all(part, 'dp_2', 0, 0, tiled=True), axis=0)]
    all_to_all x1 -> x6, starting transfers between devices: 6.03 us -> 29.4 us  [the longest x4 18.1 us: exchange(): lax.all_to_all(value, ALL, 0, 0, tiled=True, axis_index_groups=groups)]
    dot_general x2 -> x0, local copies, waits for them, and re-layouts: 23.2 us -> none  [the longest x1 12 us: per_device(): lax.dot_general(live_dy, hidden, (((0,), (0,)), ((), ())), preferred_elem...]
    transpose x2 -> x0, local copies, waits for them, and re-layouts: 19.5 us -> none  [own_block(): tiles = tiles.transpose(*order, *range(len(axes), tiles.ndim))]
    unnamed x29 -> x15, local copies, waits for them, and re-layouts: 16 us -> 1.03 us
    dot_general x2 -> x0, other arithmetic: 14.5 us -> none  [the longest x1 7.24 us: per_device(): lax.dot_general(live_x, d_in, (((0,), (0,)), ((), ())), preferred_element...]
  transfers between devices with their start and end apart: 7 -> 15, of which waited for: 7 -> 7; matrix products, arithmetic and copies ran while one was open for 19% -> 32% of each run, Pallas kernels for 0% -> 0%
where the time goes in v1:
time: 158 us; the launch traced here: 156 us
  waiting for transfers between devices  48.9 us (31%)
  starting transfers between devices  38 us (24%)
  matrix products  33.2 us (21%)
  other arithmetic  28.5 us (18%)
  local copies, waits for them, and re-layouts  5.69 us (4%)
  between operations  2.2 us (1%)
    dot_general x9, matrix products, dot(): lax.dot_general(a, b, (((over_a,), (over_b,)), ((), ())), preferred_eleme...  33.2 us
    all_to_all x2, waiting for transfers between devices, row_sums(): return jnp.sum(lax.all_to_all(part, 'dp_2', 0, 0, tiled=True), axis=0)  24.4 us
    all_to_all x4, waiting for transfers between devices, exchange(): lax.all_to_all(value, ALL, 0, 0, tiled=True, axis_index_groups=groups)  19 us
    all_to_all x4, starting transfers between devices, exchange(): lax.all_to_all(value, ALL, 0, 0, tiled=True, axis_index_groups=groups)  18.1 us
    all_to_all x2, starting transfers between devices, row_sums(): return jnp.sum(lax.all_to_all(part, 'dp_2', 0, 0, tiled=True), axis=0)  11.3 us
    ppermute x6, starting transfers between devices, hop(): return lax.ppermute(value, ALL, sorted(pairs))  8.5 us
    unnamed x3, other arithmetic  6.08 us
    ppermute x6, waiting for transfers between devices, hop(): return lax.ppermute(value, ALL, sorted(pairs))  5.52 us
  transfers between devices with their start and end apart: 15, of which 7 were waited for; matrix products, arithmetic and copies ran while one was open for 32% of the time, Pallas kernels for 0%

profile of v1, /device:TPU:8, one launch (start us, length us, event | category | flops | bytes accessed | tf_op | source)
XLA Modules:
  0.0 156.5 jit_solution(13068674393966125800)
XLA Ops:
  0.6 0.0 copy-start
  0.7 1.3 fusion.60
  2.6 0.7 select_compare_fusion
  3.3 6.7 %fusion.2 = f32[224,1024]{1,0:T(8,128)S(1)} fusion(bf16[224,4096]{1,0:T(8,128)(2,1)} %bitcast.67, bf16[1,1024,4096]{2,1,0:T(8,128)(2,1)} %param.5), kind=kOutput, calls=%fused_computation.2 | convolution fusion | flops 1879048192 | bytes 11141120 | tf_op jit(solution)/shard_map/dot_general | solution.py:38
  10.1 2.9 %multiply_convert_fusion.7 = (bf16[112,1024]{1,0:T(8,128)(2,1)S(1)}, bf16[112,1024]{1,0:T(8,128)(2,1)S(1)}) fusion(f32[224,1024]{1,0:T(8,128)S(1)} %fusion.2, bf16[112,4096]{1,0:T(8,128)(2,1)S(1)} %copy-done, bf16[1,1024,4096]{2,1,0:T(8,128)(2,1)S(1)} %copy-done.2, pred[1024]{0:T(1024)(128)(4,1)S(1)} %select_compare_fusion), kind=kOutput, calls=%fused_computation.51 | convolution fusion | flops 941129728 | bytes 10683392 | tf_op jit(solution)/shard_map/dot_general | solution.py:38
  13.1 2.0 %convert_select_fusion.1 = (f32[224,1024]{1,0:T(8,128)S(1)}, f32[224,1024]{1,0:T(8,128)}) fusion(pred[]{:T(512)S(6)} %eq.19, bf16[112,1024]{1,0:T(8,128)(2,1)S(1)} %get-tuple-element.7, bf16[112,1024]{1,0:T(8,128)(2,1)S(1)} %get-tuple-element.6, s32[1024]{0:T(1024)S(1)} %fusion.49), kind=kOutput, calls=%fused_computation.25 | convolution fusion | flops 473104384 | bytes 2297857 | tf_op jit(solution)/shard_map/dot_general | solution.py:38
  15.1 1.5 dynamic-slice_convert_fusion
  16.6 1.5 collective-permute-start.3
  18.1 1.8 %collective-permute-start = (f32[112,2048]{1,0:T(8,128)}, f32[112,2048]{1,0:T(8,128)}, u32[]{:S(2)}, u32[]{:S(2)}) collective-permute-start(f32[112,2048]{1,0:T(8,128)} %get-tuple-element.3), channel_id=1, source_target_pairs={{0,48},{1,193},{2,50},{3,195},{4,52},{5,197},{6,54},{7,199},{8,56}... | collective-permute-start | bytes 2752520 | tf_op jit(solution)/shard_map/ppermute | solution.py:29
  19.8 1.5 collective-permute-start.1
  21.4 0.5 collective-permute-start.2
  21.8 1.0 copy.20
  22.9 4.0 %all-to-all-start = ((f32[4,224,256]{2,1,0:T(8,128)}), f32[4,224,256]{2,1,0:T(8,128)S(1)}, u32[]{:S(2)}, u32[]{:S(2)}) async-start(f32[4,224,256]{2,1,0:T(8,128)} %bitcast.63), calls=%async_computation | async-start | bytes 1835008 | tf_op jit(solution)/shard_map/all_to_all | solution.py:34
  27.6 1.0 dynamic-slice_dynamic-update-slice_fusion
  28.5 2.3 %copy.19 = f32[28,4,8,256]{3,2,0,1:T(8,128)} copy(f32[28,4,8,256]{3,2,1,0:T(8,128)} %bitcast.27) | data formatting | bytes 1835008 | tf_op jit(solution)/shard_map/reshape | solution.py:88
  30.8 0.7 collective-permute-done.3
  31.5 1.3 collective-permute-start.5
  32.8 1.9 %collective-permute-start.4 = (f32[112,2048]{1,0:T(8,128)}, f32[112,2048]{1,0:T(8,128)}, u32[]{:S(2)}, u32[]{:S(2)}) collective-permute-start(f32[112,2048]{1,0:T(8,128)} %collective-permute-done), channel_id=1, source_target_pairs={{0,48},{1,193},{2,50},{3,195},{4,52},{5,197},{6,54},{7,199},{8,56}... | collective-permute-start | bytes 2752520 | tf_op jit(solution)/shard_map/ppermute | solution.py:29
  34.7 2.0 %fusion.20 = bf16[672,2048]{1,0:T(8,128)(2,1)} fusion(bf16[672,2048]{1,0:T(8,128)(2,1)} %dynamic-slice_dynamic-update-slice_fusion, f32[112,2048]{1,0:T(8,128)} %collective-permute-done, f32[]{:T(128)S(6)} %convert_element_type.42), kind=kLoop, calls=%fused_computation.42 | loop fusion | flops 458752 | bytes 1376260
  36.8 4.8 %collective-permute-done.1 = f32[112,2048]{1,0:T(8,128)} collective-permute-done((f32[112,2048]{1,0:T(8,128)}, f32[112,2048]{1,0:T(8,128)}, u32[]{:S(2)}, u32[]{:S(2)}) %collective-permute-start.1) | collective-permute-done | bytes 917536 | tf_op jit(solution)/shard_map/ppermute | solution.py:29
  41.6 2.0 %fusion.21 = bf16[672,2048]{1,0:T(8,128)(2,1)} fusion(bf16[672,2048]{1,0:T(8,128)(2,1)} %fusion.20, f32[112,2048]{1,0:T(8,128)} %collective-permute-done.1, f32[]{:T(128)S(6)} %convert_element_type.42), kind=kLoop, calls=%fused_computation.43 | loop fusion | flops 458752 | bytes 1376260
  43.6 3.6 %all-to-all-done = f32[4,224,256]{2,1,0:T(8,128)S(1)} async-done(((f32[4,224,256]{2,1,0:T(8,128)}), f32[4,224,256]{2,1,0:T(8,128)S(1)}, u32[]{:S(2)}, u32[]{:S(2)}) %all-to-all-start) | async-done | bytes 917536 | tf_op jit(solution)/shard_map/all_to_all | solution.py:34
  47.2 3.7 %all-to-all-start.3 = ((f32[4,224,256]{2,1,0:T(8,128)}), f32[4,224,256]{2,1,0:T(8,128)S(1)}, u32[]{:S(2)}, u32[]{:S(2)}) async-start(f32[4,224,256]{2,1,0:T(8,128)} %bitcast.61), calls=%async_computation.3 | async-start | bytes 1835008 | tf_op jit(solution)/shard_map/all_to_all | solution.py:34
  50.9 2.0 %fusion.22 = bf16[672,2048]{1,0:T(8,128)(2,1)} fusion(bf16[672,2048]{1,0:T(8,128)(2,1)} %fusion.21, f32[112,2048]{1,0:T(8,128)} %collective-permute-done.2, f32[]{:T(128)S(6)} %convert_element_type.42), kind=kLoop, calls=%fused_computation.44 | loop fusion | flops 458752 | bytes 1376260
  53.0 2.0 %fusion.23 = bf16[672,2048]{1,0:T(8,128)(2,1)} fusion(bf16[672,2048]{1,0:T(8,128)(2,1)} %fusion.22, f32[112,2048]{1,0:T(8,128)} %collective-permute-done.3, f32[]{:T(128)S(6)} %convert_element_type.42), kind=kLoop, calls=%fused_computation.45 | loop fusion | flops 458752 | bytes 1376260 | tf_op jit(solution)/shard_map/concatenate | solution.py:101
  55.0 7.0 %all-to-all-done.3 = f32[4,224,256]{2,1,0:T(8,128)S(1)} async-done(((f32[4,224,256]{2,1,0:T(8,128)}), f32[4,224,256]{2,1,0:T(8,128)S(1)}, u32[]{:S(2)}, u32[]{:S(2)}) %all-to-all-start.3) | async-done | bytes 917536 | tf_op jit(solution)/shard_map/all_to_all | solution.py:34
  61.9 0.3 fusion.16
  62.3 2.8 %fusion.31 = f32[256,2048]{1,0:T(8,128)S(1)} fusion(bf16[672,2048]{1,0:T(8,128)(2,1)} %fusion.23, bf16[224,256]{1,0:T(8,128)(2,1)S(1)} %get-tuple-element.12, bf16[224,256]{1,0:T(8,128)(2,1)S(1)} %get-tuple-element.13, bf16[224,256]{1,0:T(8,128)(2,1)S(1)} %get-tuple-element.11), kind=kOutput, calls=%fused_computation.60 | convolution fusion | flops 705675264 | bytes 5193728 | tf_op jit(solution)/shard_map/dot_general | solution.py:38
  65.1 1.2 multiply_convert_fusion
  66.3 1.2 multiply_convert_fusion.1
  67.6 1.8 %convolution_add_fusion = f32[256,2048]{1,0:T(8,128)} fusion(f32[256,2048]{1,0:T(8,128)S(1)} %fusion.31, bf16[112,2048]{1,0:T(8,128)(2,1)S(1)} %multiply_convert_fusion, bf16[112,2048]{1,0:T(8,128)(2,1)S(1)} %multiply_convert_fusion.1, bf16[4,224,256]{2,1,0:T(8,128)(2,1)S(1)} %get-tuple-element.18), kind=kOutput, calls=%fused_computation.15 | convolution fusion | flops 237240320 | bytes 5226496 | tf_op jit(solution)/shard_map/dot_general | solution.py:38
  69.4 5.5 %all-to-all-start.4 = ((f32[4,64,2048]{2,1,0:T(8,128)}), f32[4,64,2048]{2,1,0:T(8,128)}, u32[]{:S(2)}, u32[]{:S(2)}) async-start(f32[4,64,2048]{2,1,0:T(8,128)} %bitcast.19), calls=%async_computation.4 | async-start | bytes 4194304 | tf_op jit(solution)/shard_map/all_to_all | solution.py:34
  75.0 5.0 %fusion.4 = f32[112,4096]{1,0:T(8,128)S(1)} fusion(bf16[1,1024,4096]{2,1,0:T(8,128)(2,1)} %param.6, f32[224,1024]{1,0:T(8,128)} %copy-done.4, pred[1024]{0:T(1024)(128)(4,1)S(1)} %select_compare_fusion), kind=kOutput, calls=%fused_computation.4 | convolution fusion | flops 940326912 | bytes 11142144 | tf_op jit(solution)/shard_map/dot_general | solution.py:38
  80.0 7.2 %fusion = f32[224,4096]{1,0:T(8,128)} fusion(bf16[1,1024,4096]{2,1,0:T(8,128)(2,1)} %param.5, bf16[112,1024]{1,0:T(8,128)(2,1)S(1)} %copy-done.6, bf16[112,1024]{1,0:T(8,128)(2,1)S(1)} %get-tuple-element.6), kind=kOutput, calls=%fused_computation | convolution fusion | flops 1879965696 | bytes 12517376 | tf_op jit(solution)/shard_map/dot_general | solution.py:38
  87.3 2.8 %fusion.25 = f32[256,2048]{1,0:T(8,128)S(1)} fusion(bf16[672,2048]{1,0:T(8,128)(2,1)} %fusion.23, bf16[224,256]{1,0:T(8,128)(2,1)S(1)} %get-tuple-element.9, bf16[224,256]{1,0:T(8,128)(2,1)S(1)} %get-tuple-element.10, bf16[224,256]{1,0:T(8,128)(2,1)S(1)} %get-tuple-element.8), kind=kOutput, calls=%fused_computation.54 | convolution fusion | flops 705675264 | bytes 5193728 | tf_op jit(solution)/shard_map/dot_general | solution.py:38
  90.0 1.8 %convolution_add_fusion.1 = f32[256,2048]{1,0:T(8,128)} fusion(f32[256,2048]{1,0:T(8,128)S(1)} %fusion.25, bf16[112,2048]{1,0:T(8,128)(2,1)S(1)} %multiply_convert_fusion, bf16[112,2048]{1,0:T(8,128)(2,1)S(1)} %multiply_convert_fusion.1, bf16[4,224,256]{2,1,0:T(8,128)(2,1)S(1)} %get-tuple-element.19), kind=kOutput, calls=%fused_computation.16 | convolution fusion | flops 237240320 | bytes 5226496 | tf_op jit(solution)/shard_map/dot_general | solution.py:38
  91.9 4.8 %all-to-all-start.1 = ((f32[4,64,2048]{2,1,0:T(8,128)}), f32[4,64,2048]{2,1,0:T(8,128)}, u32[]{:S(2)}, u32[]{:S(2)}) async-start(f32[4,64,2048]{2,1,0:T(8,128)} %bitcast.64), calls=%async_computation.1 | async-start | bytes 4194304 | tf_op jit(solution)/shard_map/all_to_all | solution.py:34
  96.7 4.1 %broadcast_select_fusion = f32[336,2048]{1,0:T(8,128)} fusion(pred[]{:T(512)S(6)} %eq.19, f32[112,4096]{1,0:T(8,128)S(1)} %fusion.4, f32[224,4096]{1,0:T(8,128)} %fusion), kind=kLoop, calls=%fused_computation.22 | loop fusion | flops 2064384 | bytes 8257537 | tf_op jit(solution)/shard_map/jit(_where)/select_n | solution.py:97
  100.8 2.6 %reduce_sum.38 = f32[64,2048]{1,0:T(8,128)} reduce(f32[4,64,2048]{2,1,0:T(8,128)} %all-to-all-done.4, f32[]{:T(128)} %constant.72.clone.1), dimensions={0}, to_apply=%region_2.3 | reduce | flops 393216 | bytes 2621444 | tf_op jit(solution)/shard_map/reduce_sum | solution.py:108
  103.4 8.4 %all-to-all-done.1 = f32[4,64,2048]{2,1,0:T(8,128)} async-done(((f32[4,64,2048]{2,1,0:T(8,128)}), f32[4,64,2048]{2,1,0:T(8,128)}, u32[]{:S(2)}, u32[]{:S(2)}) %all-to-all-start.1) | async-done | bytes 2097184 | tf_op jit(solution)/shard_map/all_to_all | solution.py:34
  111.9 7.8 %all-to-all-start.5 = ((f32[8,8,2048]{2,1,0:T(8,128)}), f32[8,8,2048]{2,1,0:T(8,128)S(1)}, u32[]{:S(2)}, u32[]{:S(2)}) async-start(f32[8,8,2048]{2,1,0:T(8,128)} %bitcast.20), calls=%async_computation.5 | async-start | bytes 1048576 | tf_op jit(solution)/shard_map/all_to_all | solution.py:109
  119.7 2.6 %reduce_sum.36 = f32[64,2048]{1,0:T(8,128)} reduce(f32[4,64,2048]{2,1,0:T(8,128)} %all-to-all-done.1, f32[]{:T(128)} %constant.72.clone.1), dimensions={0}, to_apply=%region_0.1 | reduce | flops 393216 | bytes 2621444 | tf_op jit(solution)/shard_map/reduce_sum | solution.py:108
  122.3 14.1 %all-to-all-done.5 = f32[8,8,2048]{2,1,0:T(8,128)S(1)} async-done(((f32[8,8,2048]{2,1,0:T(8,128)}), f32[8,8,2048]{2,1,0:T(8,128)S(1)}, u32[]{:S(2)}, u32[]{:S(2)}) %all-to-all-start.5) | async-done | bytes 524320 | tf_op jit(solution)/shard_map/all_to_all | solution.py:109
  136.4 3.5 %all-to-all-start.2 = ((f32[8,8,2048]{2,1,0:T(8,128)}), f32[8,8,2048]{2,1,0:T(8,128)S(1)}, u32[]{:S(2)}, u32[]{:S(2)}) async-start(f32[8,8,2048]{2,1,0:T(8,128)} %bitcast.66), calls=%async_computation.2 | async-start | bytes 1048576 | tf_op jit(solution)/shard_map/all_to_all | solution.py:109
  139.9 0.1 collective-permute-start.7
  140.0 5.4 %add_multiply_fusion = f32[336,2048]{1,0:T(8,128)} fusion(f32[336,2048]{1,0:T(8,128)} %collective-permute-done.8, pred[]{:T(512)S(6)} %eq.19, f32[112,4096]{1,0:T(8,128)S(1)} %fusion.4, f32[224,4096]{1,0:T(8,128)} %fusion), kind=kLoop, calls=%fused_computation.14 | loop fusion | flops 3440640 | bytes 11010049 | tf_op jit(solution)/shard_map/mul | solution.py:117
  145.5 10.3 %all-to-all-done.2 = f32[8,8,2048]{2,1,0:T(8,128)S(1)} async-done(((f32[8,8,2048]{2,1,0:T(8,128)}), f32[8,8,2048]{2,1,0:T(8,128)S(1)}, u32[]{:S(2)}, u32[]{:S(2)}) %all-to-all-start.2) | async-done | bytes 524320 | tf_op jit(solution)/shard_map/all_to_all | solution.py:109
  155.8 0.7 maximum_bitcast_fusion
  (29 shorter events, 0.2 us)
Async XLA Ops:
  0.6 9.4 %copy-start = (bf16[112,4096]{1,0:T(8,128)(2,1)S(1)}, bf16[112,4096]{1,0:T(8,128)(2,1)}, u32[]{:S(2)}) copy-start(bf16[112,4096]{1,0:T(8,128)(2,1)} %param.9) | copy-start | bytes 2752516
  3.3 6.8 %copy-start.2 = (bf16[1,1024,4096]{2,1,0:T(8,128)(2,1)S(1)}, bf16[1,1024,4096]{2,1,0:T(8,128)(2,1)}, u32[]{:S(2)}) copy-start(bf16[1,1024,4096]{2,1,0:T(8,128)(2,1)} %param.6) | copy-start | bytes 25165828
  10.1 2.9 %copy-start.4 = (f32[224,1024]{1,0:T(8,128)}, f32[224,1024]{1,0:T(8,128)S(1)}, u32[]{:S(2)}) copy-start(f32[224,1024]{1,0:T(8,128)S(1)} %fusion.2) | copy-start | bytes 2752516
  13.0 3.5 %copy-start.5 = (bf16[112,1024]{1,0:T(8,128)(2,1)}, bf16[112,1024]{1,0:T(8,128)(2,1)S(1)}, u32[]{:S(2)}) copy-start(bf16[112,1024]{1,0:T(8,128)(2,1)S(1)} %get-tuple-element.7) | copy-start | bytes 688132
  13.1 2.1 %copy-start.3 = (bf16[4096,2,112]{0,2,1:T(8,128)(2,1)S(1)}, bf16[4096,2,112]{0,2,1:T(8,128)(2,1)}, u32[]{:S(2)}) copy-start(bf16[4096,2,112]{0,2,1:T(8,128)(2,1)} %param.8) | copy-start | bytes 5505028
  15.1 13.4 %collective-permute-start.6 = (f32[224,1024]{1,0:T(8,128)}, f32[224,1024]{1,0:T(8,128)}, u32[]{:S(2)}, u32[]{:S(2)}) collective-permute-start(f32[224,1024]{1,0:T(8,128)} %get-tuple-element.5), channel_id=1, source_target_pairs={{0,1},{1,0},{2,3},{3,2},{4,5},{5,4},{6,7},{7,6},{8,9},{9,8},{10,11... | collective-permute-start | bytes 2752520 | tf_op jit(solution)/shard_map/ppermute | solution.py:84
  16.6 14.9 %collective-permute-start.3 = (f32[112,2048]{1,0:T(8,128)}, f32[112,2048]{1,0:T(8,128)}, u32[]{:S(2)}, u32[]{:S(2)}) collective-permute-start(f32[112,2048]{1,0:T(8,128)} %get-tuple-element.2), channel_id=1, source_target_pairs={{0,16},{1,65},{2,18},{3,67},{4,20},{5,69},{6,22},{7,71},{8,24},{9,... | collective-permute-start | bytes 2752520 | tf_op jit(solution)/shard_map/ppermute | solution.py:29
  18.1 14.8 %collective-permute-start = (f32[112,2048]{1,0:T(8,128)}, f32[112,2048]{1,0:T(8,128)}, u32[]{:S(2)}, u32[]{:S(2)}) collective-permute-start(f32[112,2048]{1,0:T(8,128)} %get-tuple-element.3), channel_id=1, source_target_pairs={{0,48},{1,193},{2,50},{3,195},{4,52},{5,197},{6,54},{7,199},{8,56}... | collective-permute-start | bytes 2752520 | tf_op jit(solution)/shard_map/ppermute | solution.py:29
  19.8 21.8 %collective-permute-start.1 = (f32[112,2048]{1,0:T(8,128)}, f32[112,2048]{1,0:T(8,128)}, u32[]{:S(2)}, u32[]{:S(2)}) collective-permute-start(f32[112,2048]{1,0:T(8,128)} %get-tuple-element.2), channel_id=1, source_target_pairs={{0,48},{1,193},{2,50},{3,195},{4,52},{5,197},{6,54},{7,199},{8,56}... | collective-permute-start | bytes 2752520 | tf_op jit(solution)/shard_map/ppermute | solution.py:29
  21.4 29.6 %collective-permute-start.2 = (f32[112,2048]{1,0:T(8,128)}, f32[112,2048]{1,0:T(8,128)}, u32[]{:S(2)}, u32[]{:S(2)}) collective-permute-start(f32[112,2048]{1,0:T(8,128)} %get-tuple-element.3), channel_id=1, source_target_pairs={{0,16},{1,65},{2,18},{3,67},{4,20},{5,69},{6,22},{7,71},{8,24},{9,... | collective-permute-start | bytes 2752520 | tf_op jit(solution)/shard_map/ppermute | solution.py:29
  22.9 24.4 %all-to-all-start = ((f32[4,224,256]{2,1,0:T(8,128)}), f32[4,224,256]{2,1,0:T(8,128)S(1)}, u32[]{:S(2)}, u32[]{:S(2)}) async-start(f32[4,224,256]{2,1,0:T(8,128)} %bitcast.63), calls=%async_computation | async-start | bytes 1835008 | tf_op jit(solution)/shard_map/all_to_all | solution.py:34
  31.5 33.6 %collective-permute-start.5 = (f32[112,2048]{1,0:T(8,128)}, f32[112,2048]{1,0:T(8,128)}, u32[]{:S(2)}, u32[]{:S(2)}) collective-permute-start(f32[112,2048]{1,0:T(8,128)} %collective-permute-done.3), channel_id=1, source_target_pairs={{0,16},{1,65},{2,18},{3,67},{4,20},{5,69},{6,22},{7,71},{8,24},{9,... | collective-permute-start | bytes 2752520 | tf_op jit(solution)/shard_map/ppermute | solution.py:29
  32.8 33.5 %collective-permute-start.4 = (f32[112,2048]{1,0:T(8,128)}, f32[112,2048]{1,0:T(8,128)}, u32[]{:S(2)}, u32[]{:S(2)}) collective-permute-start(f32[112,2048]{1,0:T(8,128)} %collective-permute-done), channel_id=1, source_target_pairs={{0,48},{1,193},{2,50},{3,195},{4,52},{5,197},{6,54},{7,199},{8,56}... | collective-permute-start | bytes 2752520 | tf_op jit(solution)/shard_map/ppermute | solution.py:29
  47.2 14.7 %all-to-all-start.3 = ((f32[4,224,256]{2,1,0:T(8,128)}), f32[4,224,256]{2,1,0:T(8,128)S(1)}, u32[]{:S(2)}, u32[]{:S(2)}) async-start(f32[4,224,256]{2,1,0:T(8,128)} %bitcast.61), calls=%async_computation.3 | async-start | bytes 1835008 | tf_op jit(solution)/shard_map/all_to_all | solution.py:34
  69.4 22.4 %all-to-all-start.4 = ((f32[4,64,2048]{2,1,0:T(8,128)}), f32[4,64,2048]{2,1,0:T(8,128)}, u32[]{:S(2)}, u32[]{:S(2)}) async-start(f32[4,64,2048]{2,1,0:T(8,128)} %bitcast.19), calls=%async_computation.4 | async-start | bytes 4194304 | tf_op jit(solution)/shard_map/all_to_all | solution.py:34
  75.0 5.0 %copy-start.6 = (bf16[112,1024]{1,0:T(8,128)(2,1)S(1)}, bf16[112,1024]{1,0:T(8,128)(2,1)}, u32[]{:S(2)}) copy-start(bf16[112,1024]{1,0:T(8,128)(2,1)} %copy-done.5) | copy-start | bytes 688132
  91.9 20.0 %all-to-all-start.1 = ((f32[4,64,2048]{2,1,0:T(8,128)}), f32[4,64,2048]{2,1,0:T(8,128)}, u32[]{:S(2)}, u32[]{:S(2)}) async-start(f32[4,64,2048]{2,1,0:T(8,128)} %bitcast.64), calls=%async_computation.1 | async-start | bytes 4194304 | tf_op jit(solution)/shard_map/all_to_all | solution.py:34
  100.8 39.2 %collective-permute-start.8 = (f32[336,2048]{1,0:T(8,128)}, f32[336,2048]{1,0:T(8,128)}, u32[]{:S(2)}, u32[]{:S(2)}) collective-permute-start(f32[336,2048]{1,0:T(8,128)} %broadcast_select_fusion), channel_id=1, source_target_pairs={{0,1},{1,0},{2,3},{3,2},{4,5},{5,4},{6,7},{7,6},{8,9},{9,8},{10,11... | collective-permute-start | bytes 8257544 | tf_op jit(solution)/shard_map/ppermute | solution.py:98
  111.9 24.5 %all-to-all-start.5 = ((f32[8,8,2048]{2,1,0:T(8,128)}), f32[8,8,2048]{2,1,0:T(8,128)S(1)}, u32[]{:S(2)}, u32[]{:S(2)}) async-start(f32[8,8,2048]{2,1,0:T(8,128)} %bitcast.20), calls=%async_computation.5 | async-start | bytes 1048576 | tf_op jit(solution)/shard_map/all_to_all | solution.py:109
  136.4 19.4 %all-to-all-start.2 = ((f32[8,8,2048]{2,1,0:T(8,128)}), f32[8,8,2048]{2,1,0:T(8,128)S(1)}, u32[]{:S(2)}, u32[]{:S(2)}) async-start(f32[8,8,2048]{2,1,0:T(8,128)} %bitcast.66), calls=%async_computation.2 | async-start | bytes 1048576 | tf_op jit(solution)/shard_map/all_to_all | solution.py:109
  139.9 15.9 %collective-permute-start.7 = (f32[8,2048]{1,0:T(8,128)S(1)}, f32[8,2048]{1,0:T(8,128)S(1)}, u32[]{:S(2)}, u32[]{:S(2)}) collective-permute-start(f32[8,2048]{1,0:T(8,128)S(1)} %reduce_sum.39), channel_id=1, source_target_pairs={{0,1},{1,0},{2,3},{3,2},{4,5},{5,4},{6,7},{7,6},{8,9},{9,8},{10,11... | collective-permute-start | bytes 196616 | tf_op jit(solution)/shard_map/ppermute | solution.py:113
  140.0 16.5 %copy-start.1 = (bf16[112,4096]{1,0:T(8,128)(2,1)S(1)}, bf16[112,4096]{1,0:T(8,128)(2,1)}, u32[]{:S(2)}) copy-start(bf16[112,4096]{1,0:T(8,128)(2,1)} %param.9) | copy-start | bytes 2752516

commit v2 on v1

--- a/solution.py
+++ b/solution.py
@@ -51,17 +51,16 @@
     rep = lax.axis_index("rep")
     north = rep == 0
     me = jnp.where(north, lax.axis_index("dp_1"), lax.axis_index("dp_0"))
+    across = jnp.where(north, lax.axis_index("dp_0"), lax.axis_index("dp_1"))
     one = jnp.minimum(lengths[0, 0], 1).astype(jnp.float32)
 
     w_t = w_in.transpose(1, 2, 0).reshape(2 * units, width)
     w_mine = lax.dynamic_slice_in_dim(w_t, rep * half, half, 1)
-    w_gate, w_up = w_mine[:units].astype(jnp.float32), w_mine[units:].astype(jnp.float32)
-    next_gate = hop(w_gate, dims, FIRST, -1)
-    last_up = hop(w_up, dims, FIRST, 1)
-    next_up = hop(w_up, dims, FIRST, -1)
-    last_gate = hop(w_gate, dims, FIRST, 1)
-    far_gate = hop(next_gate, dims, FIRST, -1)
-    far_up = hop(last_up, dims, FIRST, 1)
+    w_send = w_mine.astype(jnp.float32)
+    w_next = hop(w_send, dims, FIRST, -1)
+    w_last = hop(w_send, dims, FIRST, 1)
+    far_gate = hop(w_next[:units], dims, FIRST, -1)
+    far_up = hop(w_last[units:], dims, FIRST, 1)
 
     position = jnp.arange(rows)
     limit = jnp.where(position < slots, lengths[0, 0], slots + lengths[0, 1])
@@ -92,21 +91,33 @@
 
     d_theirs, d_ours = spread(theirs), spread(ours)
 
-    g = jnp.concatenate([dot(d_in, x, 1, 0), dot(hidden, dy, 1, 0)])
+    g_in = dot(d_in, x, 1, 0)
+    g_down = dot(hidden, dy, 1, 0)
+    g = jnp.concatenate([g_in, g_down])
     low, high = g[:, :half], g[:, half:]
     away, kept = jnp.where(north, high, low), jnp.where(north, low, high)
     back = lax.ppermute(away, "rep", SWAP)
 
-    arrived = lambda *parts: [(p * one).astype(jnp.bfloat16) for p in parts]
-    near = jnp.concatenate([w_mine] + arrived(next_gate, next_up, last_gate, last_up))
-    far = jnp.concatenate(arrived(far_gate, far_up))
+    arrived = lambda p: (p * one).astype(jnp.bfloat16)
+    w_1, w_3 = arrived(w_next), arrived(w_last)
+    w_2 = jnp.concatenate([arrived(far_gate), arrived(far_up)])
+    cut = half // 2
 
     def row_sums(d):
-        close = jnp.concatenate([d[0], d[1], d[3]])
-        partial = dot(close, near, 0, 0) + dot(d[2], far, 0, 0)
-        got = exchange(partial.reshape(4, rows // 16, half), dims, SECOND)
-        part = jnp.sum(got, axis=0).reshape(nz, own_rows, half)
-        return jnp.sum(lax.all_to_all(part, "dp_2", 0, 0, tiled=True), axis=0)
+        partial = dot(d[0], w_mine, 0, 0) + dot(d[1], w_1, 0, 0)
+        partial = partial + dot(d[3], w_3, 0, 0) + dot(d[2], w_2, 0, 0)
+        blocks = partial.reshape(4, rows // 16, half)
+        blocks = jnp.concatenate([blocks, blocks])
+        mine, b1, b2, b3 = (lax.dynamic_index_in_dim(blocks, across + k, 0, False) for k in range(4))
+        r1 = hop(jnp.concatenate([b2[:, :cut], b1[:, cut:]], axis=1), dims, SECOND, 1)
+        r2 = hop(jnp.concatenate([b3[:, :cut], b2[:, cut:]], axis=1), dims, SECOND, -1)
+        t1 = hop(b1[:, :cut] + r1[:, :cut], dims, SECOND, 1)
+        t2 = hop(b3[:, cut:] + r2[:, cut:], dims, SECOND, -1)
+        left = mine[:, :cut] + r2[:, :cut] + t1
+        right = mine[:, cut:] + r1[:, cut:] + t2
+        part = jnp.concatenate([left, right], axis=1).reshape(nz, own_rows, half)
+        got = lax.all_to_all(part, "dp_2", 0, 0, tiled=True)
+        return jnp.sum(got, axis=0)
 
     sum_theirs = row_sums(d_theirs)
     sum_ours = row_sums(d_ours)

time: 158 us -> 143 us (0.905)
  the two profiles are of different devices: /device:TPU:8 before, /device:TPU:6 now
where the time goes in v2:
time: 143 us; the launch traced here: 142 us
  starting transfers between devices  41.8 us (29%)
  waiting for transfers between devices  37 us (26%)
  matrix products  33.5 us (23%)
  other arithmetic  18.9 us (13%)
  local copies, waits for them, and re-layouts  8.49 us (6%)
  between operations  2.25 us (2%)
    dot_general x13, matrix products, dot(): lax.dot_general(a, b, (((over_a,), (over_b,)), ((), ())), preferred_eleme...  33.5 us
    ppermute x12, waiting for transfers between devices, hop(): return lax.ppermute(value, ALL, sorted(pairs))  21.2 us
    ppermute x12, starting transfers between devices, hop(): return lax.ppermute(value, ALL, sorted(pairs))  18.4 us
    all_to_all x2, starting transfers between devices, row_sums(): got = lax.all_to_all(part, 'dp_2', 0, 0, tiled=True)  13.1 us
    all_to_all x2, starting transfers between devices, exchange(): lax.all_to_all(value, ALL, 0, 0, tiled=True, axis_index_groups=groups)  10.2 us
    all_to_all x2, waiting for transfers between devices, row_sums(): got = lax.all_to_all(part, 'dp_2', 0, 0, tiled=True)  10.1 us
    all_to_all x2, waiting for transfers between devices, exchange(): lax.all_to_all(value, ALL, 0, 0, tiled=True, axis_index_groups=groups)  5.62 us
    mul x1, other arithmetic, per_device(): shared = (kept + back) * GRAD_SCALE  5.54 us
  transfers between devices with their start and end apart: 19, of which 9 were waited for; matrix products, arithmetic and copies ran while one was open for 32% of the time, Pallas kernels for 0%

profile of v2, /device:TPU:6, one launch (start us, length us, event | category | flops | bytes accessed | tf_op | source)
XLA Modules:
  0.0 141.9 jit_solution(16463977815317083993)
XLA Ops:
  0.7 1.3 fusion.74
  2.0 6.7 %fusion.2 = f32[224,1024]{1,0:T(8,128)S(1)} fusion(bf16[224,4096]{1,0:T(8,128)(2,1)} %bitcast.88, bf16[1,1024,4096]{2,1,0:T(8,128)(2,1)} %param.5), kind=kOutput, calls=%fused_computation.2 | convolution fusion | flops 1879048192 | bytes 11141120 | tf_op jit(solution)/shard_map/dot_general | solution.py:38
  9.4 0.6 select_compare_fusion
  10.0 2.9 %multiply_convert_fusion.5 = (bf16[112,1024]{1,0:T(8,128)(2,1)S(1)}, bf16[112,1024]{1,0:T(8,128)(2,1)S(1)}) fusion(f32[224,1024]{1,0:T(8,128)S(1)} %fusion.2, bf16[112,4096]{1,0:T(8,128)(2,1)S(1)} %copy-done, bf16[1,1024,4096]{2,1,0:T(8,128)(2,1)S(1)} %copy-done.3, pred[1024]{0:T(1024)(128)(4,1)S(1)} %select_compare_fusion), kind=kOutput, calls=%fused_computation.91 | convolution fusion | flops 941129728 | bytes 10683392 | tf_op jit(solution)/shard_map/dot_general | solution.py:38
  12.9 2.0 %convert_select_fusion.1 = (f32[224,1024]{1,0:T(8,128)S(1)}, f32[224,1024]{1,0:T(8,128)}) fusion(pred[]{:T(512)S(6)} %eq.19, bf16[112,1024]{1,0:T(8,128)(2,1)S(1)} %get-tuple-element.13, bf16[112,1024]{1,0:T(8,128)(2,1)S(1)} %get-tuple-element.12, s32[1024]{0:T(1024)S(1)} %fusion.63), kind=kOutput, calls=%fused_computation.47 | convolution fusion | flops 473104384 | bytes 2297857 | tf_op jit(solution)/shard_map/dot_general | solution.py:38
  14.9 1.0 copy.14
  15.9 5.7 %all-to-all-start = ((f32[4,224,256]{2,1,0:T(8,128)}), f32[4,224,256]{2,1,0:T(8,128)S(1)}, u32[]{:S(2)}, u32[]{:S(2)}) async-start(f32[4,224,256]{2,1,0:T(8,128)} %bitcast.85), calls=%async_computation | async-start | bytes 1835008 | tf_op jit(solution)/shard_map/all_to_all | solution.py:34
  21.6 1.5 %dynamic-slice_convert_fusion = f32[224,2048]{1,0:T(8,128)} fusion(bf16[224,4096]{1,0:T(8,128)(2,1)S(1)} %bitcast.89, s32[]{:T(128)S(6)} %select_n.127), kind=kLoop, calls=%fused_computation.61 | loop fusion | flops 458752 | bytes 2752516 | tf_op jit(solution)/shard_map/convert_element_type | solution.py:59
  23.1 0.9 collective-permute-start
  24.0 2.4 %collective-permute-start.1 = (f32[224,2048]{1,0:T(8,128)}, f32[224,2048]{1,0:T(8,128)}, u32[]{:S(2)}, u32[]{:S(2)}) collective-permute-start(f32[224,2048]{1,0:T(8,128)} %dynamic-slice_convert_fusion), channel_id=1, source_target_pairs={{0,16},{1,65},{2,18},{3,67},{4,20},{5,69},{6,22},{7,71},{8,24},{9,... | collective-permute-start | bytes 5505032 | tf_op jit(solution)/shard_map/ppermute | solution.py:29
  26.3 7.2 %fusion = f32[224,4096]{1,0:T(8,128)} fusion(bf16[1,1024,4096]{2,1,0:T(8,128)(2,1)} %param.5, bf16[112,1024]{1,0:T(8,128)(2,1)S(1)} %get-tuple-element.13, bf16[112,1024]{1,0:T(8,128)(2,1)S(1)} %get-tuple-element.12), kind=kOutput, calls=%fused_computation | convolution fusion | flops 1879965696 | bytes 12517376 | tf_op jit(solution)/shard_map/dot_general | solution.py:38
  33.6 2.3 %copy.13 = f32[28,4,8,256]{3,2,0,1:T(8,128)} copy(f32[28,4,8,256]{3,2,1,0:T(8,128)} %bitcast.35) | data formatting | bytes 1835008 | tf_op jit(solution)/shard_map/reshape | solution.py:87
  35.9 0.9 copy-done.6
  36.9 4.5 %all-to-all-start.2 = ((f32[4,224,256]{2,1,0:T(8,128)}), f32[4,224,256]{2,1,0:T(8,128)}, u32[]{:S(2)}, u32[]{:S(2)}) async-start(f32[4,224,256]{2,1,0:T(8,128)} %bitcast.83), calls=%async_computation.2 | async-start | bytes 1835008 | tf_op jit(solution)/shard_map/all_to_all | solution.py:34
  41.4 4.8 %fusion.4 = f32[112,4096]{1,0:T(8,128)S(1)} fusion(bf16[1,1024,4096]{2,1,0:T(8,128)(2,1)} %param.6, f32[224,1024]{1,0:T(8,128)S(1)} %copy-done.10, pred[1024]{0:T(1024)(128)(4,1)S(1)} %select_compare_fusion), kind=kOutput, calls=%fused_computation.4 | convolution fusion | flops 940326912 | bytes 11142144 | tf_op jit(solution)/shard_map/dot_general | solution.py:38
  46.2 2.0 %broadcast_select_fusion = f32[336,2048]{1,0:T(8,128)} fusion(pred[]{:T(512)S(6)} %eq.19, f32[112,4096]{1,0:T(8,128)S(1)} %fusion.4, f32[224,4096]{1,0:T(8,128)S(1)} %copy-done.2), kind=kLoop, calls=%fused_computation.44 | loop fusion | flops 2064384 | bytes 8257537 | tf_op jit(solution)/shard_map/jit(_where)/select_n | solution.py:98
  48.8 5.6 %all-to-all-done.2 = f32[4,224,256]{2,1,0:T(8,128)} async-done(((f32[4,224,256]{2,1,0:T(8,128)}), f32[4,224,256]{2,1,0:T(8,128)}, u32[]{:S(2)}, u32[]{:S(2)}) %all-to-all-start.2) | async-done | bytes 917536 | tf_op jit(solution)/shard_map/all_to_all | solution.py:34
  54.4 1.6 %fusion.18 = (bf16[4,224,256]{2,1,0:T(8,128)(2,1)S(1)}, bf16[4,224,256]{2,1,0:T(8,128)(2,1)S(1)}) fusion(s32[]{:T(128)S(6)} %select_n.126, f32[4,224,256]{2,1,0:T(8,128)} %all-to-all-done.2, f32[]{:T(128)S(6)} %convert_element_type.33, f32[4,224,256]{2,1,0:T(8,128)S(1)} %copy-done.7), kind=kLoop, calls=%fused_computation.50 | loop fusion | flops 1376256 | bytes 2752520 | tf_op jit(solution)/shard_map/convert_element_type | solution.py:90
  56.7 1.2 slice.168
  57.9 2.1 %collective-permute-start.3 = (f32[112,2048]{1,0:T(8,128)S(1)}, f32[112,2048]{1,0:T(8,128)S(1)}, u32[]{:S(2)}, u32[]{:S(2)}) collective-permute-start(f32[112,2048]{1,0:T(8,128)S(1)} %slice.168), channel_id=1, source_target_pairs={{0,16},{1,65},{2,18},{3,67},{4,20},{5,69},{6,22},{7,71},{8,24},{9,... | collective-permute-start | bytes 2752520 | tf_op jit(solution)/shard_map/ppermute | solution.py:29
  60.5 1.2 slice.167
  61.8 2.0 %convolution_add_fusion.1 = f32[256,2048]{1,0:T(8,128)S(1)} fusion(f32[256,2048]{1,0:T(8,128)S(1)} %fusion.22, f32[224,2048]{1,0:T(8,128)} %collective-permute-done, f32[]{:T(128)S(6)} %convert_element_type.33, bf16[4,224,256]{2,1,0:T(8,128)(2,1)S(1)} %get-tuple-element.26), kind=kOutput, calls=%fused_computation.33 | convolution fusion | flops 236322816 | bytes 6144004 | tf_op jit(solution)/shard_map/dot_general | solution.py:38
  63.8 2.0 %convolution_add_fusion.3 = f32[256,2048]{1,0:T(8,128)S(1)} fusion(f32[256,2048]{1,0:T(8,128)S(1)} %fusion.24, f32[224,2048]{1,0:T(8,128)} %collective-permute-done, f32[]{:T(128)S(6)} %convert_element_type.33, bf16[4,224,256]{2,1,0:T(8,128)(2,1)S(1)} %get-tuple-element.27), kind=kOutput, calls=%fused_computation.36 | convolution fusion | flops 236322816 | bytes 6144004 | tf_op jit(solution)/shard_map/dot_general | solution.py:38
  65.8 5.6 %collective-permute-done.3 = f32[112,2048]{1,0:T(8,128)S(1)} collective-permute-done((f32[112,2048]{1,0:T(8,128)S(1)}, f32[112,2048]{1,0:T(8,128)S(1)}, u32[]{:S(2)}, u32[]{:S(2)}) %collective-permute-start.3) | collective-permute-done | bytes 917536 | tf_op jit(solution)/shard_map/ppermute | solution.py:29
  71.5 5.0 %collective-permute-done.2 = f32[112,2048]{1,0:T(8,128)S(1)} collective-permute-done((f32[112,2048]{1,0:T(8,128)S(1)}, f32[112,2048]{1,0:T(8,128)S(1)}, u32[]{:S(2)}, u32[]{:S(2)}) %collective-permute-start.2) | collective-permute-done | bytes 917536 | tf_op jit(solution)/shard_map/ppermute | solution.py:29
  77.0 0.5 fusion.27
  77.4 2.1 %fusion.10 = f32[256,2048]{1,0:T(8,128)S(1)} fusion(f32[256,2048]{1,0:T(8,128)S(1)} %fusion.26, f32[256,2048]{1,0:T(8,128)S(1)} %convolution_add_fusion.1, f32[224,2048]{1,0:T(8,128)} %collective-permute-done.1, f32[]{:T(128)S(6)} %convert_element_type.33, bf16[4,224,256]{2,1,0:T(8,128)(2,1)S(1)} %get-tuple-element.26), kind=kOutput, calls=%fused_computation.32 | convolution fusion | flops 236847104 | bytes 8241156 | tf_op jit(solution)/shard_map/dot_general | solution.py:38
  79.5 0.5 fusion.31
  80.1 2.2 %collective-permute-start.9 = (f32[64,2048]{1,0:T(8,128)S(1)}, f32[64,2048]{1,0:T(8,128)S(1)}, u32[]{:S(2)}, u32[]{:S(2)}) collective-permute-start(f32[64,2048]{1,0:T(8,128)S(1)} %pad_maximum_fusion.6), channel_id=1, source_target_pairs={{0,192},{1,49},{2,194},{3,51},{4,196},{5,53},{6,198},{7,55},{8,200... | collective-permute-start | bytes 1572872 | tf_op jit(solution)/shard_map/ppermute | solution.py:29
  82.4 2.0 %fusion.11 = f32[256,2048]{1,0:T(8,128)S(1)} fusion(f32[256,2048]{1,0:T(8,128)S(1)} %fusion.27, f32[256,2048]{1,0:T(8,128)S(1)} %convolution_add_fusion.3, f32[224,2048]{1,0:T(8,128)} %collective-permute-done.1, f32[]{:T(128)S(6)} %convert_element_type.33, bf16[4,224,256]{2,1,0:T(8,128)(2,1)S(1)} %get-tuple-element.27), kind=kOutput, calls=%fused_computation.35 | convolution fusion | flops 236847104 | bytes 8241156 | tf_op jit(solution)/shard_map/dot_general | solution.py:38
  84.5 1.2 fusion.39
  85.8 3.3 %collective-permute-start.4 = (f32[64,2048]{1,0:T(8,128)S(1)}, f32[64,2048]{1,0:T(8,128)S(1)}, u32[]{:S(2)}, u32[]{:S(2)}) collective-permute-start(f32[64,2048]{1,0:T(8,128)S(1)} %pad_maximum_fusion.4), channel_id=1, source_target_pairs={{0,192},{1,49},{2,194},{3,51},{4,196},{5,53},{6,198},{7,55},{8,200... | collective-permute-start | bytes 1572872 | tf_op jit(solution)/shard_map/ppermute | solution.py:29
  89.4 3.4 %collective-permute-start.12 = (f32[64,1024]{1,0:T(8,128)S(1)}, f32[64,1024]{1,0:T(8,128)S(1)}, u32[]{:S(2)}, u32[]{:S(2)}) collective-permute-start(f32[64,1024]{1,0:T(8,128)S(1)} %slice_add_fusion), channel_id=1, source_target_pairs={{0,192},{1,49},{2,194},{3,51},{4,196},{5,53},{6,198},{7,55},{8,200... | collective-permute-start | bytes 786440 | tf_op jit(solution)/shard_map/ppermute | solution.py:29
  93.0 0.9 pad_maximum_fusion.5
  93.8 2.0 %collective-permute-done.4 = f32[64,2048]{1,0:T(8,128)S(1)} collective-permute-done((f32[64,2048]{1,0:T(8,128)S(1)}, f32[64,2048]{1,0:T(8,128)S(1)}, u32[]{:S(2)}, u32[]{:S(2)}) %collective-permute-start.4) | collective-permute-done | bytes 524320 | tf_op jit(solution)/shard_map/ppermute | solution.py:29
  95.9 3.8 %collective-permute-start.7 = (f32[64,1024]{1,0:T(8,128)S(1)}, f32[64,1024]{1,0:T(8,128)S(1)}, u32[]{:S(2)}, u32[]{:S(2)}) collective-permute-start(f32[64,1024]{1,0:T(8,128)S(1)} %slice_add_fusion.4), channel_id=1, source_target_pairs={{0,192},{1,49},{2,194},{3,51},{4,196},{5,53},{6,198},{7,55},{8,200... | collective-permute-start | bytes 786440 | tf_op jit(solution)/shard_map/ppermute | solution.py:29
  99.6 0.9 collective-permute-done.11
  100.6 0.8 maximum_bitcast_fusion.1
  101.5 8.5 %all-to-all-start.3 = ((f32[8,8,2048]{2,1,0:T(8,128)}), f32[8,8,2048]{2,1,0:T(8,128)S(1)}, u32[]{:S(2)}, u32[]{:S(2)}) async-start(f32[8,8,2048]{2,1,0:T(8,128)} %maximum_bitcast_fusion.1), calls=%async_computation.3 | async-start | bytes 1048576 | tf_op jit(solution)/shard_map/all_to_all | solution.py:119
  109.9 1.0 slice_add_fusion.6
  111.0 7.6 %collective-permute-done.6 = f32[64,1024]{1,0:T(8,128)S(1)} collective-permute-done((f32[64,1024]{1,0:T(8,128)S(1)}, f32[64,1024]{1,0:T(8,128)S(1)}, u32[]{:S(2)}, u32[]{:S(2)}) %collective-permute-start.6) | collective-permute-done | bytes 262176 | tf_op jit(solution)/shard_map/ppermute | solution.py:29
  118.6 1.3 fusion.48
  119.9 0.8 maximum_bitcast_fusion
  120.7 2.5 %all-to-all-done.3 = f32[8,8,2048]{2,1,0:T(8,128)S(1)} async-done(((f32[8,8,2048]{2,1,0:T(8,128)}), f32[8,8,2048]{2,1,0:T(8,128)S(1)}, u32[]{:S(2)}, u32[]{:S(2)}) %all-to-all-start.3) | async-done | bytes 524320 | tf_op jit(solution)/shard_map/all_to_all | solution.py:119
  123.2 4.7 %all-to-all-start.1 = ((f32[8,8,2048]{2,1,0:T(8,128)}), f32[8,8,2048]{2,1,0:T(8,128)S(1)}, u32[]{:S(2)}, u32[]{:S(2)}) async-start(f32[8,8,2048]{2,1,0:T(8,128)} %maximum_bitcast_fusion), calls=%async_computation.1 | async-start | bytes 1048576 | tf_op jit(solution)/shard_map/all_to_all | solution.py:119
  128.0 5.5 %add_multiply_fusion = f32[336,2048]{1,0:T(8,128)} fusion(f32[336,2048]{1,0:T(8,128)} %collective-permute-done.14, pred[]{:T(512)S(6)} %eq.19, f32[112,4096]{1,0:T(8,128)S(1)} %fusion.4, f32[224,4096]{1,0:T(8,128)} %fusion), kind=kLoop, calls=%fused_computation.30 | loop fusion | flops 3440640 | bytes 11010049 | tf_op jit(solution)/shard_map/mul | solution.py:128
  133.6 7.6 %all-to-all-done.1 = f32[8,8,2048]{2,1,0:T(8,128)S(1)} async-done(((f32[8,8,2048]{2,1,0:T(8,128)}), f32[8,8,2048]{2,1,0:T(8,128)S(1)}, u32[]{:S(2)}, u32[]{:S(2)}) %all-to-all-start.1) | async-done | bytes 524320 | tf_op jit(solution)/shard_map/all_to_all | solution.py:119
  141.2 0.7 maximum_bitcast_fusion.2
  (62 shorter events, 2.9 us)
Async XLA Ops:
  0.6 9.3 %copy-start = (bf16[112,4096]{1,0:T(8,128)(2,1)S(1)}, bf16[112,4096]{1,0:T(8,128)(2,1)}, u32[]{:S(2)}) copy-start(bf16[112,4096]{1,0:T(8,128)(2,1)} %param.9) | copy-start | bytes 2752516
  2.0 8.0 %copy-start.3 = (bf16[1,1024,4096]{2,1,0:T(8,128)(2,1)S(1)}, bf16[1,1024,4096]{2,1,0:T(8,128)(2,1)}, u32[]{:S(2)}) copy-start(bf16[1,1024,4096]{2,1,0:T(8,128)(2,1)} %param.6) | copy-start | bytes 25165828
  8.7 4.2 %copy-start.9 = (f32[224,1024]{1,0:T(8,128)}, f32[224,1024]{1,0:T(8,128)S(1)}, u32[]{:S(2)}) copy-start(f32[224,1024]{1,0:T(8,128)S(1)} %fusion.2) | copy-start | bytes 2752516
  14.9 6.7 %copy-start.4 = (bf16[4096,2,112]{0,2,1:T(8,128)(2,1)S(1)}, bf16[4096,2,112]{0,2,1:T(8,128)(2,1)}, u32[]{:S(2)}) copy-start(bf16[4096,2,112]{0,2,1:T(8,128)(2,1)} %param.8) | copy-start | bytes 5505028
  14.9 18.7 %collective-permute-start.8 = (f32[224,1024]{1,0:T(8,128)}, f32[224,1024]{1,0:T(8,128)}, u32[]{:S(2)}, u32[]{:S(2)}) collective-permute-start(f32[224,1024]{1,0:T(8,128)} %get-tuple-element.11), channel_id=1, source_target_pairs={{0,1},{1,0},{2,3},{3,2},{4,5},{5,4},{6,7},{7,6},{8,9},{9,8},{10,11... | collective-permute-start | bytes 2752520 | tf_op jit(solution)/shard_map/ppermute | solution.py:83
  15.9 20.0 %all-to-all-start = ((f32[4,224,256]{2,1,0:T(8,128)}), f32[4,224,256]{2,1,0:T(8,128)S(1)}, u32[]{:S(2)}, u32[]{:S(2)}) async-start(f32[4,224,256]{2,1,0:T(8,128)} %bitcast.85), calls=%async_computation | async-start | bytes 1835008 | tf_op jit(solution)/shard_map/all_to_all | solution.py:34
  23.1 37.4 %collective-permute-start = (f32[224,2048]{1,0:T(8,128)}, f32[224,2048]{1,0:T(8,128)}, u32[]{:S(2)}, u32[]{:S(2)}) collective-permute-start(f32[224,2048]{1,0:T(8,128)} %dynamic-slice_convert_fusion), channel_id=1, source_target_pairs={{0,48},{1,193},{2,50},{3,195},{4,52},{5,197},{6,54},{7,199},{8,56}... | collective-permute-start | bytes 5505032 | tf_op jit(solution)/shard_map/ppermute | solution.py:29
  24.0 32.7 %collective-permute-start.1 = (f32[224,2048]{1,0:T(8,128)}, f32[224,2048]{1,0:T(8,128)}, u32[]{:S(2)}, u32[]{:S(2)}) collective-permute-start(f32[224,2048]{1,0:T(8,128)} %dynamic-slice_convert_fusion), channel_id=1, source_target_pairs={{0,16},{1,65},{2,18},{3,67},{4,20},{5,69},{6,22},{7,71},{8,24},{9,... | collective-permute-start | bytes 5505032 | tf_op jit(solution)/shard_map/ppermute | solution.py:29
  33.6 7.8 %copy-start.10 = (f32[224,1024]{1,0:T(8,128)S(1)}, f32[224,1024]{1,0:T(8,128)}, u32[]{:S(2)}) copy-start(f32[224,1024]{1,0:T(8,128)} %copy-done.9) | copy-start | bytes 2752516
  35.9 0.9 copy-start.6
  36.9 17.5 %all-to-all-start.2 = ((f32[4,224,256]{2,1,0:T(8,128)}), f32[4,224,256]{2,1,0:T(8,128)}, u32[]{:S(2)}, u32[]{:S(2)}) async-start(f32[4,224,256]{2,1,0:T(8,128)} %bitcast.83), calls=%async_computation.2 | async-start | bytes 1835008 | tf_op jit(solution)/shard_map/all_to_all | solution.py:34
  41.4 4.8 %copy-start.2 = (f32[224,4096]{1,0:T(8,128)S(1)}, f32[224,4096]{1,0:T(8,128)}, u32[]{:S(2)}) copy-start(f32[224,4096]{1,0:T(8,128)} %fusion) | copy-start | bytes 11010052
  46.2 8.2 %copy-start.7 = (f32[4,224,256]{2,1,0:T(8,128)S(1)}, f32[4,224,256]{2,1,0:T(8,128)}, u32[]{:S(2)}) copy-start(f32[4,224,256]{2,1,0:T(8,128)} %copy-done.6) | copy-start | bytes 2752516
  48.2 79.8 %collective-permute-start.14 = (f32[336,2048]{1,0:T(8,128)}, f32[336,2048]{1,0:T(8,128)}, u32[]{:S(2)}, u32[]{:S(2)}) collective-permute-start(f32[336,2048]{1,0:T(8,128)} %broadcast_select_fusion), channel_id=1, source_target_pairs={{0,1},{1,0},{2,3},{3,2},{4,5},{5,4},{6,7},{7,6},{8,9},{9,8},{10,11... | collective-permute-start | bytes 8257544 | tf_op jit(solution)/shard_map/ppermute | solution.py:99
  54.4 1.8 %copy-start.5 = (bf16[4096,2,112]{0,2,1:T(8,128)(2,1)S(1)}, bf16[4096,2,112]{0,2,1:T(8,128)(2,1)}, u32[]{:S(2)}) copy-start(bf16[4096,2,112]{0,2,1:T(8,128)(2,1)} %param.8) | copy-start | bytes 5505028
  57.9 13.5 %collective-permute-start.3 = (f32[112,2048]{1,0:T(8,128)S(1)}, f32[112,2048]{1,0:T(8,128)S(1)}, u32[]{:S(2)}, u32[]{:S(2)}) collective-permute-start(f32[112,2048]{1,0:T(8,128)S(1)} %slice.168), channel_id=1, source_target_pairs={{0,16},{1,65},{2,18},{3,67},{4,20},{5,69},{6,22},{7,71},{8,24},{9,... | collective-permute-start | bytes 2752520 | tf_op jit(solution)/shard_map/ppermute | solution.py:29
  61.7 14.7 %collective-permute-start.2 = (f32[112,2048]{1,0:T(8,128)S(1)}, f32[112,2048]{1,0:T(8,128)S(1)}, u32[]{:S(2)}, u32[]{:S(2)}) collective-permute-start(f32[112,2048]{1,0:T(8,128)S(1)} %slice.167), channel_id=1, source_target_pairs={{0,48},{1,193},{2,50},{3,195},{4,52},{5,197},{6,54},{7,199},{8,56}... | collective-permute-start | bytes 2752520 | tf_op jit(solution)/shard_map/ppermute | solution.py:29
  80.1 9.3 %collective-permute-start.9 = (f32[64,2048]{1,0:T(8,128)S(1)}, f32[64,2048]{1,0:T(8,128)S(1)}, u32[]{:S(2)}, u32[]{:S(2)}) collective-permute-start(f32[64,2048]{1,0:T(8,128)S(1)} %pad_maximum_fusion.6), channel_id=1, source_target_pairs={{0,192},{1,49},{2,194},{3,51},{4,196},{5,53},{6,198},{7,55},{8,200... | collective-permute-start | bytes 1572872 | tf_op jit(solution)/shard_map/ppermute | solution.py:29
  82.4 10.5 %collective-permute-start.10 = (f32[64,2048]{1,0:T(8,128)S(1)}, f32[64,2048]{1,0:T(8,128)S(1)}, u32[]{:S(2)}, u32[]{:S(2)}) collective-permute-start(f32[64,2048]{1,0:T(8,128)S(1)} %pad_maximum_fusion.7), channel_id=1, source_target_pairs={{0,64},{1,17},{2,66},{3,19},{4,68},{5,21},{6,70},{7,23},{8,72},{9,... | collective-permute-start | bytes 1572872 | tf_op jit(solution)/shard_map/ppermute | solution.py:29
  85.8 10.0 %collective-permute-start.4 = (f32[64,2048]{1,0:T(8,128)S(1)}, f32[64,2048]{1,0:T(8,128)S(1)}, u32[]{:S(2)}, u32[]{:S(2)}) collective-permute-start(f32[64,2048]{1,0:T(8,128)S(1)} %pad_maximum_fusion.4), channel_id=1, source_target_pairs={{0,192},{1,49},{2,194},{3,51},{4,196},{5,53},{6,198},{7,55},{8,200... | collective-permute-start | bytes 1572872 | tf_op jit(solution)/shard_map/ppermute | solution.py:29
  89.4 10.3 %collective-permute-start.12 = (f32[64,1024]{1,0:T(8,128)S(1)}, f32[64,1024]{1,0:T(8,128)S(1)}, u32[]{:S(2)}, u32[]{:S(2)}) collective-permute-start(f32[64,1024]{1,0:T(8,128)S(1)} %slice_add_fusion), channel_id=1, source_target_pairs={{0,192},{1,49},{2,194},{3,51},{4,196},{5,53},{6,198},{7,55},{8,200... | collective-permute-start | bytes 786440 | tf_op jit(solution)/shard_map/ppermute | solution.py:29
  92.9 7.7 %collective-permute-start.11 = (f32[64,1024]{1,0:T(8,128)S(1)}, f32[64,1024]{1,0:T(8,128)S(1)}, u32[]{:S(2)}, u32[]{:S(2)}) collective-permute-start(f32[64,1024]{1,0:T(8,128)S(1)} %slice_add_fusion.2), channel_id=1, source_target_pairs={{0,64},{1,17},{2,66},{3,19},{4,68},{5,21},{6,70},{7,23},{8,72},{9,... | collective-permute-start | bytes 786440 | tf_op jit(solution)/shard_map/ppermute | solution.py:29
  93.8 16.1 %collective-permute-start.5 = (f32[64,2048]{1,0:T(8,128)}, f32[64,2048]{1,0:T(8,128)}, u32[]{:S(2)}, u32[]{:S(2)}) collective-permute-start(f32[64,2048]{1,0:T(8,128)} %pad_maximum_fusion.5), channel_id=1, source_target_pairs={{0,64},{1,17},{2,66},{3,19},{4,68},{5,21},{6,70},{7,23},{8,72},{9,... | collective-permute-start | bytes 1572872 | tf_op jit(solution)/shard_map/ppermute | solution.py:29
  95.8 4.8 %copy-start.8 = (f32[64,2048]{1,0:T(8,128)}, f32[64,2048]{1,0:T(8,128)S(1)}, u32[]{:S(2)}) copy-start(f32[64,2048]{1,0:T(8,128)S(1)} %collective-permute-done.4) | copy-start | bytes 1572868
  95.9 15.2 %collective-permute-start.7 = (f32[64,1024]{1,0:T(8,128)S(1)}, f32[64,1024]{1,0:T(8,128)S(1)}, u32[]{:S(2)}, u32[]{:S(2)}) collective-permute-start(f32[64,1024]{1,0:T(8,128)S(1)} %slice_add_fusion.4), channel_id=1, source_target_pairs={{0,192},{1,49},{2,194},{3,51},{4,196},{5,53},{6,198},{7,55},{8,200... | collective-permute-start | bytes 786440 | tf_op jit(solution)/shard_map/ppermute | solution.py:29
  101.5 21.8 %all-to-all-start.3 = ((f32[8,8,2048]{2,1,0:T(8,128)}), f32[8,8,2048]{2,1,0:T(8,128)S(1)}, u32[]{:S(2)}, u32[]{:S(2)}) async-start(f32[8,8,2048]{2,1,0:T(8,128)} %maximum_bitcast_fusion.1), calls=%async_computation.3 | async-start | bytes 1048576 | tf_op jit(solution)/shard_map/all_to_all | solution.py:119
  110.9 7.7 %collective-permute-start.6 = (f32[64,1024]{1,0:T(8,128)S(1)}, f32[64,1024]{1,0:T(8,128)S(1)}, u32[]{:S(2)}, u32[]{:S(2)}) collective-permute-start(f32[64,1024]{1,0:T(8,128)S(1)} %slice_add_fusion.6), channel_id=1, source_target_pairs={{0,64},{1,17},{2,66},{3,19},{4,68},{5,21},{6,70},{7,23},{8,72},{9,... | collective-permute-start | bytes 786440 | tf_op jit(solution)/shard_map/ppermute | solution.py:29
  123.2 18.0 %all-to-all-start.1 = ((f32[8,8,2048]{2,1,0:T(8,128)}), f32[8,8,2048]{2,1,0:T(8,128)S(1)}, u32[]{:S(2)}, u32[]{:S(2)}) async-start(f32[8,8,2048]{2,1,0:T(8,128)} %maximum_bitcast_fusion), calls=%async_computation.1 | async-start | bytes 1048576 | tf_op jit(solution)/shard_map/all_to_all | solution.py:119
  127.9 13.3 %collective-permute-start.13 = (f32[8,2048]{1,0:T(8,128)S(1)}, f32[8,2048]{1,0:T(8,128)S(1)}, u32[]{:S(2)}, u32[]{:S(2)}) collective-permute-start(f32[8,2048]{1,0:T(8,128)S(1)} %reduce_sum.19), channel_id=1, source_target_pairs={{0,1},{1,0},{2,3},{3,2},{4,5},{5,4},{6,7},{7,6},{8,9},{9,8},{10,11... | collective-permute-start | bytes 196616 | tf_op jit(solution)/shard_map/ppermute | solution.py:124
  128.0 13.9 %copy-start.1 = (bf16[112,4096]{1,0:T(8,128)(2,1)S(1)}, bf16[112,4096]{1,0:T(8,128)(2,1)}, u32[]{:S(2)}) copy-start(bf16[112,4096]{1,0:T(8,128)(2,1)} %param.9) | copy-start | bytes 2752516

commit v3 on v2

--- a/solution.py
+++ b/solution.py
@@ -55,12 +55,14 @@
     one = jnp.minimum(lengths[0, 0], 1).astype(jnp.float32)
 
     w_t = w_in.transpose(1, 2, 0).reshape(2 * units, width)
-    w_mine = lax.dynamic_slice_in_dim(w_t, rep * half, half, 1)
-    w_send = w_mine.astype(jnp.float32)
-    w_next = hop(w_send, dims, FIRST, -1)
-    w_last = hop(w_send, dims, FIRST, 1)
-    far_gate = hop(w_next[:units], dims, FIRST, -1)
-    far_up = hop(w_last[units:], dims, FIRST, 1)
+    w_mine = jnp.where(north, w_t[:, :half], w_t[:, half:])
+    w_gate, w_up = w_mine[:units].astype(jnp.float32), w_mine[units:].astype(jnp.float32)
+    next_gate = hop(w_gate, dims, FIRST, -1)
+    last_up = hop(w_up, dims, FIRST, 1)
+    next_up = hop(w_up, dims, FIRST, -1)
+    last_gate = hop(w_gate, dims, FIRST, 1)
+    far_gate = hop(next_gate, dims, FIRST, -1)
+    far_up = hop(last_up, dims, FIRST, 1)
 
     position = jnp.arange(rows)
     limit = jnp.where(position < slots, lengths[0, 0], slots + lengths[0, 1])
@@ -83,13 +85,11 @@
     theirs = lax.ppermute(jnp.where(north, plain, turned), "rep", SWAP)
     ours = jnp.where(north, turned, plain)
 
-    def spread(d):
-        blocks = d.reshape(2 * units, 4, rows // 4).transpose(1, 0, 2)
-        got = exchange(blocks, dims, FIRST)
-        twice = jnp.concatenate([got, got])
-        return (lax.dynamic_slice_in_dim(twice, me, 4, 0) * one).astype(jnp.bfloat16)
-
-    d_theirs, d_ours = spread(theirs), spread(ours)
+    cols = rows // 4
+    blocks = [jnp.concatenate([d[:, k * cols : (k + 1) * cols] for d in (ours, theirs)]) for k in range(4)]
+    got = exchange(jnp.stack(blocks), dims, FIRST)
+    got = lax.dynamic_slice_in_dim(jnp.concatenate([got, got]), me, 4, 0)
+    d_all = (got * one).astype(jnp.bfloat16)
 
     g_in = dot(d_in, x, 1, 0)
     g_down = dot(hidden, dy, 1, 0)
@@ -99,8 +99,9 @@
     back = lax.ppermute(away, "rep", SWAP)
 
     arrived = lambda p: (p * one).astype(jnp.bfloat16)
-    w_1, w_3 = arrived(w_next), arrived(w_last)
+    w_1 = jnp.concatenate([arrived(next_gate), arrived(next_up)])
     w_2 = jnp.concatenate([arrived(far_gate), arrived(far_up)])
+    w_3 = jnp.concatenate([arrived(last_gate), arrived(last_up)])
     cut = half // 2
 
     def row_sums(d):
@@ -111,16 +112,17 @@
         mine, b1, b2, b3 = (lax.dynamic_index_in_dim(blocks, across + k, 0, False) for k in range(4))
         r1 = hop(jnp.concatenate([b2[:, :cut], b1[:, cut:]], axis=1), dims, SECOND, 1)
         r2 = hop(jnp.concatenate([b3[:, :cut], b2[:, cut:]], axis=1), dims, SECOND, -1)
-        t1 = hop(b1[:, :cut] + r1[:, :cut], dims, SECOND, 1)
-        t2 = hop(b3[:, cut:] + r2[:, cut:], dims, SECOND, -1)
+        up, down = b1[:, :cut] + r1[:, :cut], b3[:, cut:] + r2[:, cut:]
+        t1 = hop(up, dims, SECOND, 1)
+        t2 = hop(down, dims, SECOND, -1)
         left = mine[:, :cut] + r2[:, :cut] + t1
         right = mine[:, cut:] + r1[:, cut:] + t2
         part = jnp.concatenate([left, right], axis=1).reshape(nz, own_rows, half)
         got = lax.all_to_all(part, "dp_2", 0, 0, tiled=True)
         return jnp.sum(got, axis=0)
 
-    sum_theirs = row_sums(d_theirs)
-    sum_ours = row_sums(d_ours)
+    sum_theirs = row_sums(d_all[:, 2 * units :])
+    sum_ours = row_sums(d_all[:, : 2 * units])
     other_half = lax.ppermute(sum_theirs, "rep", SWAP)
     shard = jnp.concatenate(
         [jnp.where(north, sum_ours, other_half), jnp.where(north, other_half, sum_ours)], axis=1

time: 143 us -> 142 us (level)
  the two profiles are of different devices: /device:TPU:6 before, /device:TPU:8 now
where the time goes in v3:
time: 142 us; the launch traced here: 140 us
  starting transfers between devices  38.3 us (27%)
  waiting for transfers between devices  36.9 us (26%)
  other arithmetic  31.2 us (22%)
  matrix products  27.5 us (19%)
  local copies, waits for them, and re-layouts  3.79 us (3%)
  between operations  2.42 us (2%)
    dot_general x13, matrix products, dot(): lax.dot_general(a, b, (((over_a,), (over_b,)), ((), ())), preferred_eleme...  27.5 us
    ppermute x14, waiting for transfers between devices, hop(): return lax.ppermute(value, ALL, sorted(pairs))  24.1 us
    ppermute x14, starting transfers between devices, hop(): return lax.ppermute(value, ALL, sorted(pairs))  21.3 us
    all_to_all x2, waiting for transfers between devices, row_sums(): got = lax.all_to_all(part, 'dp_2', 0, 0, tiled=True)  12.7 us
    all_to_all x2, starting transfers between devices, row_sums(): got = lax.all_to_all(part, 'dp_2', 0, 0, tiled=True)  12 us
    convert_element_type x6, other arithmetic, per_device(): arrived = lambda p: (p * one).astype(jnp.bfloat16)  9.09 us
    mul x1, other arithmetic, per_device(): shared = (kept + back) * GRAD_SCALE  5.54 us
    all_to_all x1, starting transfers between devices, exchange(): lax.all_to_all(value, ALL, 0, 0, tiled=True, axis_index_groups=groups)  4.39 us
  transfers between devices with their start and end apart: 20, of which 10 were waited for; matrix products, arithmetic and copies ran while one was open for 40% of the time, Pallas kernels for 0%

profile of v3, /device:TPU:8, one launch (start us, length us, event | category | flops | bytes accessed | tf_op | source)
XLA Modules:
  0.0 140.1 jit_solution(10346309008832750211)
XLA Ops:
  0.7 1.7 %slice_select_fusion = bf16[224,2048]{1,0:T(8,128)(2,1)S(1)} fusion(bf16[224,4096]{1,0:T(8,128)(2,1)} %bitcast.87, pred[]{:T(512)S(6)} %eq.19), kind=kLoop, calls=%fused_computation.48 | loop fusion | flops 458752 | bytes 2752513 | tf_op jit(solution)/shard_map/jit(_where)/select_n | solution.py:58
  2.4 0.9 copy-done.3
  3.3 1.5 %slice_convert_fusion.1 = (f32[112,2048]{1,0:T(8,128)}, f32[112,2048]{1,0:T(8,128)}) fusion(bf16[224,2048]{1,0:T(8,128)(2,1)S(1)} %slice_select_fusion), kind=kLoop, calls=%fused_computation.81 | loop fusion | flops 458752 | bytes 2752512 | tf_op jit(solution)/shard_map/convert_element_type | solution.py:59
  4.8 1.5 %collective-permute-start.3 = (f32[112,2048]{1,0:T(8,128)}, f32[112,2048]{1,0:T(8,128)}, u32[]{:S(2)}, u32[]{:S(2)}) collective-permute-start(f32[112,2048]{1,0:T(8,128)} %get-tuple-element.14), channel_id=1, source_target_pairs={{0,16},{1,65},{2,18},{3,67},{4,20},{5,69},{6,22},{7,71},{8,24},{9,... | collective-permute-start | bytes 2752520 | tf_op jit(solution)/shard_map/ppermute | solution.py:29
  6.3 1.7 %collective-permute-start.1 = (f32[112,2048]{1,0:T(8,128)}, f32[112,2048]{1,0:T(8,128)}, u32[]{:S(2)}, u32[]{:S(2)}) collective-permute-start(f32[112,2048]{1,0:T(8,128)} %get-tuple-element.14), channel_id=1, source_target_pairs={{0,48},{1,193},{2,50},{3,195},{4,52},{5,197},{6,54},{7,199},{8,56}... | collective-permute-start | bytes 2752520 | tf_op jit(solution)/shard_map/ppermute | solution.py:29
  8.3 3.0 %collective-permute-start.2 = (f32[112,2048]{1,0:T(8,128)}, f32[112,2048]{1,0:T(8,128)}, u32[]{:S(2)}, u32[]{:S(2)}) collective-permute-start(f32[112,2048]{1,0:T(8,128)} %get-tuple-element.15), channel_id=1, source_target_pairs={{0,48},{1,193},{2,50},{3,195},{4,52},{5,197},{6,54},{7,199},{8,56}... | collective-permute-start | bytes 2752520 | tf_op jit(solution)/shard_map/ppermute | solution.py:29
  11.3 0.6 fusion.69
  11.9 6.3 %fusion.2 = f32[224,1024]{1,0:T(8,128)S(1)} fusion(bf16[224,4096]{1,0:T(8,128)(2,1)S(1)} %bitcast.88, bf16[1,1024,4096]{2,1,0:T(8,128)(2,1)} %param.5), kind=kOutput, calls=%fused_computation.2 | convolution fusion | flops 1879048192 | bytes 11141120 | tf_op jit(solution)/shard_map/dot_general | solution.py:38
  18.8 0.7 select_compare_fusion
  19.5 2.9 %multiply_convert_fusion.7 = (bf16[112,1024]{1,0:T(8,128)(2,1)S(1)}, bf16[112,1024]{1,0:T(8,128)(2,1)S(1)}) fusion(f32[224,1024]{1,0:T(8,128)S(1)} %fusion.2, bf16[112,4096]{1,0:T(8,128)(2,1)S(1)} %copy-done, bf16[1,1024,4096]{2,1,0:T(8,128)(2,1)S(1)} %bitcast.83, pred[1024]{0:T(1024)(128)(4,1)S(1)} %select_compare_fusion), kind=kOutput, calls=%fused_computation.89 | convolution fusion | flops 941129728 | bytes 10683392 | tf_op jit(solution)/shard_map/dot_general | solution.py:38
  22.4 2.3 %convert_select_fusion.1 = (f32[224,1024]{1,0:T(8,128)}, f32[224,1024]{1,0:T(8,128)}) fusion(pred[]{:T(512)S(6)} %eq.19, bf16[112,1024]{1,0:T(8,128)(2,1)S(1)} %get-tuple-element.13, bf16[112,1024]{1,0:T(8,128)(2,1)S(1)} %get-tuple-element.12, s32[1024]{0:T(1024)S(1)} %fusion.52), kind=kOutput, calls=%fused_computation.47 | convolution fusion | flops 473104384 | bytes 2297857 | tf_op jit(solution)/shard_map/dot_general | solution.py:38
  25.3 7.2 %fusion = f32[224,4096]{1,0:T(8,128)} fusion(bf16[1,1024,4096]{2,1,0:T(8,128)(2,1)} %param.5, bf16[112,1024]{1,0:T(8,128)(2,1)S(1)} %get-tuple-element.13, bf16[112,1024]{1,0:T(8,128)(2,1)S(1)} %get-tuple-element.12), kind=kOutput, calls=%fused_computation | convolution fusion | flops 1879965696 | bytes 12517376 | tf_op jit(solution)/shard_map/dot_general | solution.py:38
  32.6 5.1 %fusion.4 = f32[112,4096]{1,0:T(8,128)S(1)} fusion(bf16[1,1024,4096]{2,1,0:T(8,128)(2,1)} %param.6, f32[224,1024]{1,0:T(8,128)} %copy-done.13, pred[1024]{0:T(1024)(128)(4,1)S(1)} %select_compare_fusion), kind=kOutput, calls=%fused_computation.4 | convolution fusion | flops 940326912 | bytes 11142144 | tf_op jit(solution)/shard_map/dot_general | solution.py:38
  37.7 2.0 %broadcast_select_fusion = f32[336,2048]{1,0:T(8,128)} fusion(pred[]{:T(512)S(6)} %eq.19, f32[112,4096]{1,0:T(8,128)S(1)} %fusion.4, f32[224,4096]{1,0:T(8,128)S(1)} %copy-done.2), kind=kLoop, calls=%fused_computation.44 | loop fusion | flops 2064384 | bytes 8257537 | tf_op jit(solution)/shard_map/jit(_where)/select_n | solution.py:98
  39.8 0.6 collective-permute-start.16
  40.6 1.4 pad_maximum_fusion.1
  42.0 4.4 %all-to-all-start = ((f32[4,448,256]{2,1,0:T(8,128)}), f32[4,448,256]{2,1,0:T(8,128)}, u32[]{:S(2)}, u32[]{:S(2)}) async-start(f32[4,448,256]{2,1,0:T(8,128)} %pad_maximum_fusion.1), calls=%async_computation | async-start | bytes 3670016 | tf_op jit(solution)/shard_map/all_to_all | solution.py:34
  46.4 3.2 %collective-permute-start.5 = (f32[112,2048]{1,0:T(8,128)}, f32[112,2048]{1,0:T(8,128)S(1)}, u32[]{:S(2)}, u32[]{:S(2)}) collective-permute-start(f32[112,2048]{1,0:T(8,128)} %collective-permute-done.1), channel_id=1, source_target_pairs={{0,48},{1,193},{2,50},{3,195},{4,52},{5,197},{6,54},{7,199},{8,56}... | collective-permute-start | bytes 2752520 | tf_op jit(solution)/shard_map/ppermute | solution.py:29
  49.6 2.0 %multiply_convert_fusion.5 = bf16[112,2048]{1,0:T(8,128)(2,1)} fusion(f32[112,2048]{1,0:T(8,128)} %collective-permute-done.1, f32[]{:T(128)S(6)} %convert_element_type.39), kind=kLoop, calls=%fused_computation.57 | loop fusion | flops 458752 | bytes 1376260 | tf_op jit(solution)/shard_map/convert_element_type | solution.py:101
  51.6 1.2 multiply_convert_fusion.2
  52.9 2.1 %multiply_convert_fusion.3 = bf16[112,2048]{1,0:T(8,128)(2,1)} fusion(f32[112,2048]{1,0:T(8,128)} %collective-permute-done.3, f32[]{:T(128)S(6)} %convert_element_type.39), kind=kLoop, calls=%fused_computation.55 | loop fusion | flops 458752 | bytes 1376260 | tf_op jit(solution)/shard_map/convert_element_type | solution.py:101
  54.9 2.0 %multiply_convert_fusion.4 = bf16[112,2048]{1,0:T(8,128)(2,1)} fusion(f32[112,2048]{1,0:T(8,128)} %collective-permute-done.2, f32[]{:T(128)S(6)} %convert_element_type.39), kind=kLoop, calls=%fused_computation.56 | loop fusion | flops 458752 | bytes 1376260 | tf_op jit(solution)/shard_map/convert_element_type | solution.py:101
  57.0 12.8 %collective-permute-done.5 = f32[112,2048]{1,0:T(8,128)S(1)} collective-permute-done((f32[112,2048]{1,0:T(8,128)}, f32[112,2048]{1,0:T(8,128)S(1)}, u32[]{:S(2)}, u32[]{:S(2)}) %collective-permute-start.5) | collective-permute-done | bytes 917536 | tf_op jit(solution)/shard_map/ppermute | solution.py:29
  69.8 0.9 multiply_convert_fusion.1
  71.0 0.8 multiply_convert_fusion
  71.8 1.8 %fusion.13 = bf16[4,448,256]{2,1,0:T(8,128)(2,1)S(1)} fusion(s32[]{:T(128)S(6)} %select_n.131, f32[4,448,256]{2,1,0:T(8,128)} %all-to-all-done, f32[]{:T(128)S(6)} %convert_element_type.39), kind=kLoop, calls=%fused_computation.42 | loop fusion | flops 1376256 | bytes 2752520 | tf_op jit(solution)/shard_map/convert_element_type | solution.py:92
  74.6 0.5 copy-done.5
  78.5 2.2 %collective-permute-start.11 = (f32[64,2048]{1,0:T(8,128)S(1)}, f32[64,2048]{1,0:T(8,128)S(1)}, u32[]{:S(2)}, u32[]{:S(2)}) collective-permute-start(f32[64,2048]{1,0:T(8,128)S(1)} %pad_maximum_fusion.13), channel_id=1, source_target_pairs={{0,192},{1,49},{2,194},{3,51},{4,196},{5,53},{6,198},{7,55},{8,200... | collective-permute-start | bytes 1572872 | tf_op jit(solution)/shard_map/ppermute | solution.py:29
  82.5 1.2 fusion.28
  83.9 2.1 %collective-permute-start.7 = (f32[64,2048]{1,0:T(8,128)S(1)}, f32[64,2048]{1,0:T(8,128)S(1)}, u32[]{:S(2)}, u32[]{:S(2)}) collective-permute-start(f32[64,2048]{1,0:T(8,128)S(1)} %pad_maximum_fusion.11), channel_id=1, source_target_pairs={{0,192},{1,49},{2,194},{3,51},{4,196},{5,53},{6,198},{7,55},{8,200... | collective-permute-start | bytes 1572872 | tf_op jit(solution)/shard_map/ppermute | solution.py:29
  86.0 1.8 %collective-permute-done.11 = f32[64,2048]{1,0:T(8,128)S(1)} collective-permute-done((f32[64,2048]{1,0:T(8,128)S(1)}, f32[64,2048]{1,0:T(8,128)S(1)}, u32[]{:S(2)}, u32[]{:S(2)}) %collective-permute-start.11) | collective-permute-done | bytes 524320 | tf_op jit(solution)/shard_map/ppermute | solution.py:29
  87.8 2.2 %collective-permute-start.14 = (f32[64,1024]{1,0:T(8,128)S(1)}, f32[64,1024]{1,0:T(8,128)S(1)}, u32[]{:S(2)}, u32[]{:S(2)}) collective-permute-start(f32[64,1024]{1,0:T(8,128)S(1)} %slice_add_fusion), channel_id=1, source_target_pairs={{0,192},{1,49},{2,194},{3,51},{4,196},{5,53},{6,198},{7,55},{8,200... | collective-permute-start | bytes 786440 | tf_op jit(solution)/shard_map/ppermute | solution.py:29
  90.4 0.8 pad_maximum_fusion.12
  91.2 1.7 %collective-permute-start.8 = (f32[64,2048]{1,0:T(8,128)}, f32[64,2048]{1,0:T(8,128)}, u32[]{:S(2)}, u32[]{:S(2)}) collective-permute-start(f32[64,2048]{1,0:T(8,128)} %pad_maximum_fusion.12), channel_id=1, source_target_pairs={{0,64},{1,17},{2,66},{3,19},{4,68},{5,21},{6,70},{7,23},{8,72},{9,... | collective-permute-start | bytes 1572872 | tf_op jit(solution)/shard_map/ppermute | solution.py:29
  93.4 2.2 %collective-permute-start.10 = (f32[64,1024]{1,0:T(8,128)S(1)}, f32[64,1024]{1,0:T(8,128)S(1)}, u32[]{:S(2)}, u32[]{:S(2)}) collective-permute-start(f32[64,1024]{1,0:T(8,128)S(1)} %slice_add_fusion.4), channel_id=1, source_target_pairs={{0,192},{1,49},{2,194},{3,51},{4,196},{5,53},{6,198},{7,55},{8,200... | collective-permute-start | bytes 786440 | tf_op jit(solution)/shard_map/ppermute | solution.py:29
  96.2 1.0 collective-permute-done.13
  97.4 0.8 maximum_bitcast_fusion.1
  98.2 8.5 %all-to-all-start.2 = ((f32[8,8,2048]{2,1,0:T(8,128)}), f32[8,8,2048]{2,1,0:T(8,128)S(1)}, u32[]{:S(2)}, u32[]{:S(2)}) async-start(f32[8,8,2048]{2,1,0:T(8,128)} %maximum_bitcast_fusion.1), calls=%async_computation.2 | async-start | bytes 1048576 | tf_op jit(solution)/shard_map/all_to_all | solution.py:121
  106.7 1.0 slice_add_fusion.6
  107.7 0.7 collective-permute-start.9
  108.4 6.9 %collective-permute-done.9 = f32[64,1024]{1,0:T(8,128)S(1)} collective-permute-done((f32[64,1024]{1,0:T(8,128)S(1)}, f32[64,1024]{1,0:T(8,128)S(1)}, u32[]{:S(2)}, u32[]{:S(2)}) %collective-permute-start.9) | collective-permute-done | bytes 262176 | tf_op jit(solution)/shard_map/ppermute | solution.py:29
  115.3 1.3 fusion.37
  116.6 0.8 maximum_bitcast_fusion
  117.4 4.3 %all-to-all-done.2 = f32[8,8,2048]{2,1,0:T(8,128)S(1)} async-done(((f32[8,8,2048]{2,1,0:T(8,128)}), f32[8,8,2048]{2,1,0:T(8,128)S(1)}, u32[]{:S(2)}, u32[]{:S(2)}) %all-to-all-start.2) | async-done | bytes 524320 | tf_op jit(solution)/shard_map/all_to_all | solution.py:121
  121.7 3.5 %all-to-all-start.1 = ((f32[8,8,2048]{2,1,0:T(8,128)}), f32[8,8,2048]{2,1,0:T(8,128)S(1)}, u32[]{:S(2)}, u32[]{:S(2)}) async-start(f32[8,8,2048]{2,1,0:T(8,128)} %maximum_bitcast_fusion), calls=%async_computation.1 | async-start | bytes 1048576 | tf_op jit(solution)/shard_map/all_to_all | solution.py:121
  125.3 5.5 %add_multiply_fusion = f32[336,2048]{1,0:T(8,128)} fusion(f32[336,2048]{1,0:T(8,128)} %collective-permute-done.16, pred[]{:T(512)S(6)} %eq.19, f32[112,4096]{1,0:T(8,128)S(1)} %fusion.4, f32[224,4096]{1,0:T(8,128)} %fusion), kind=kLoop, calls=%fused_computation.32 | loop fusion | flops 3440640 | bytes 11010049 | tf_op jit(solution)/shard_map/mul | solution.py:130
  130.9 8.5 %all-to-all-done.1 = f32[8,8,2048]{2,1,0:T(8,128)S(1)} async-done(((f32[8,8,2048]{2,1,0:T(8,128)}), f32[8,8,2048]{2,1,0:T(8,128)S(1)}, u32[]{:S(2)}, u32[]{:S(2)}) %all-to-all-start.1) | async-done | bytes 524320 | tf_op jit(solution)/shard_map/all_to_all | solution.py:121
  139.4 0.7 maximum_bitcast_fusion.6
  (83 shorter events, 8.7 us)
Async XLA Ops:
  0.6 18.8 %copy-start = (bf16[112,4096]{1,0:T(8,128)(2,1)S(1)}, bf16[112,4096]{1,0:T(8,128)(2,1)}, u32[]{:S(2)}) copy-start(bf16[112,4096]{1,0:T(8,128)(2,1)} %param.9) | copy-start | bytes 2752516
  0.7 10.6 %copy-start.14 = (s32[1,2]{1,0:T(1,128)S(1)}, s32[1,2]{1,0:T(1,128)}, u32[]{:S(2)}) copy-start(s32[1,2]{1,0:T(1,128)} %param.7) | copy-start | bytes 28
  0.7 11.2 %copy-start.10 = (bf16[4096,2,112]{0,2,1:T(8,128)(2,1)S(1)}, bf16[4096,2,112]{0,2,1:T(8,128)(2,1)}, u32[]{:S(2)}) copy-start(bf16[4096,2,112]{0,2,1:T(8,128)(2,1)} %param.8) | copy-start | bytes 5505028
  2.4 0.9 copy-start.3
  3.3 16.1 %slice-start = ((s8[8388608]{0:T(1024)(128)(4,1)}), s8[4194304]{0:T(1024)(128)(4,1)S(1)}, s32[]{:S(2)}) async-start(s8[8388608]{0:T(1024)(128)(4,1)} %bitcast.82), calls=%async_computation.3 | async-start | bytes 8388608
  4.8 48.1 %collective-permute-start.3 = (f32[112,2048]{1,0:T(8,128)}, f32[112,2048]{1,0:T(8,128)}, u32[]{:S(2)}, u32[]{:S(2)}) collective-permute-start(f32[112,2048]{1,0:T(8,128)} %get-tuple-element.14), channel_id=1, source_target_pairs={{0,16},{1,65},{2,18},{3,67},{4,20},{5,69},{6,22},{7,71},{8,24},{9,... | collective-permute-start | bytes 2752520 | tf_op jit(solution)/shard_map/ppermute | solution.py:29
  6.3 40.1 %collective-permute-start.1 = (f32[112,2048]{1,0:T(8,128)}, f32[112,2048]{1,0:T(8,128)}, u32[]{:S(2)}, u32[]{:S(2)}) collective-permute-start(f32[112,2048]{1,0:T(8,128)} %get-tuple-element.14), channel_id=1, source_target_pairs={{0,48},{1,193},{2,50},{3,195},{4,52},{5,197},{6,54},{7,199},{8,56}... | collective-permute-start | bytes 2752520 | tf_op jit(solution)/shard_map/ppermute | solution.py:29
  8.0 41.6 %collective-permute-start.4 = (f32[112,2048]{1,0:T(8,128)}, f32[112,2048]{1,0:T(8,128)}, u32[]{:S(2)}, u32[]{:S(2)}) collective-permute-start(f32[112,2048]{1,0:T(8,128)} %get-tuple-element.15), channel_id=1, source_target_pairs={{0,16},{1,65},{2,18},{3,67},{4,20},{5,69},{6,22},{7,71},{8,24},{9,... | collective-permute-start | bytes 2752520 | tf_op jit(solution)/shard_map/ppermute | solution.py:29
  8.3 46.7 %collective-permute-start.2 = (f32[112,2048]{1,0:T(8,128)}, f32[112,2048]{1,0:T(8,128)}, u32[]{:S(2)}, u32[]{:S(2)}) collective-permute-start(f32[112,2048]{1,0:T(8,128)} %get-tuple-element.15), channel_id=1, source_target_pairs={{0,48},{1,193},{2,50},{3,195},{4,52},{5,197},{6,54},{7,199},{8,56}... | collective-permute-start | bytes 2752520 | tf_op jit(solution)/shard_map/ppermute | solution.py:29
  11.9 7.6 %slice-start.1 = ((s8[8388608]{0:T(1024)(128)(4,1)}), s8[4194304]{0:T(1024)(128)(4,1)S(1)}, s32[]{:S(2)}) async-start(s8[8388608]{0:T(1024)(128)(4,1)} %bitcast.82), calls=%async_computation.4 | async-start | bytes 8388608
  18.1 4.3 %copy-start.13 = (f32[224,1024]{1,0:T(8,128)}, f32[224,1024]{1,0:T(8,128)S(1)}, u32[]{:S(2)}) copy-start(f32[224,1024]{1,0:T(8,128)S(1)} %fusion.2) | copy-start | bytes 2752516
  24.7 15.1 %collective-permute-start = (f32[224,1024]{1,0:T(8,128)}, f32[224,1024]{1,0:T(8,128)S(1)}, u32[]{:S(2)}, u32[]{:S(2)}) collective-permute-start(f32[224,1024]{1,0:T(8,128)} %get-tuple-element.11), channel_id=1, source_target_pairs={{0,1},{1,0},{2,3},{3,2},{4,5},{5,4},{6,7},{7,6},{8,9},{9,8},{10,11... | collective-permute-start | bytes 2752520 | tf_op jit(solution)/shard_map/ppermute | solution.py:85
  32.6 5.1 %copy-start.2 = (f32[224,4096]{1,0:T(8,128)S(1)}, f32[224,4096]{1,0:T(8,128)}, u32[]{:S(2)}) copy-start(f32[224,4096]{1,0:T(8,128)} %fusion) | copy-start | bytes 11010052
  37.7 2.0 %copy-start.11 = (f32[224,1024]{1,0:T(8,128)S(1)}, f32[224,1024]{1,0:T(8,128)}, u32[]{:S(2)}) copy-start(f32[224,1024]{1,0:T(8,128)} %get-tuple-element.10) | copy-start | bytes 2752516
  39.8 85.6 %collective-permute-start.16 = (f32[336,2048]{1,0:T(8,128)}, f32[336,2048]{1,0:T(8,128)}, u32[]{:S(2)}, u32[]{:S(2)}) collective-permute-start(f32[336,2048]{1,0:T(8,128)} %broadcast_select_fusion), channel_id=1, source_target_pairs={{0,1},{1,0},{2,3},{3,2},{4,5},{5,4},{6,7},{7,6},{8,9},{9,8},{10,11... | collective-permute-start | bytes 8257544 | tf_op jit(solution)/shard_map/ppermute | solution.py:99
  42.0 29.9 %all-to-all-start = ((f32[4,448,256]{2,1,0:T(8,128)}), f32[4,448,256]{2,1,0:T(8,128)}, u32[]{:S(2)}, u32[]{:S(2)}) async-start(f32[4,448,256]{2,1,0:T(8,128)} %pad_maximum_fusion.1), calls=%async_computation | async-start | bytes 3670016 | tf_op jit(solution)/shard_map/all_to_all | solution.py:34
  46.4 23.4 %collective-permute-start.5 = (f32[112,2048]{1,0:T(8,128)}, f32[112,2048]{1,0:T(8,128)S(1)}, u32[]{:S(2)}, u32[]{:S(2)}) collective-permute-start(f32[112,2048]{1,0:T(8,128)} %collective-permute-done.1), channel_id=1, source_target_pairs={{0,48},{1,193},{2,50},{3,195},{4,52},{5,197},{6,54},{7,199},{8,56}... | collective-permute-start | bytes 2752520 | tf_op jit(solution)/shard_map/ppermute | solution.py:29
  49.6 21.4 %collective-permute-start.6 = (f32[112,2048]{1,0:T(8,128)}, f32[112,2048]{1,0:T(8,128)S(1)}, u32[]{:S(2)}, u32[]{:S(2)}) collective-permute-start(f32[112,2048]{1,0:T(8,128)} %collective-permute-done.4), channel_id=1, source_target_pairs={{0,16},{1,65},{2,18},{3,67},{4,20},{5,69},{6,22},{7,71},{8,24},{9,... | collective-permute-start | bytes 2752520 | tf_op jit(solution)/shard_map/ppermute | solution.py:29
  70.7 2.9 %copy-start.4 = (bf16[224,2048]{1,0:T(8,128)(2,1)S(1)}, bf16[224,2048]{1,0:T(8,128)(2,1)}, u32[]{:S(2)}) copy-start(bf16[224,2048]{1,0:T(8,128)(2,1)} %copy-done.3) | copy-start | bytes 2752516
  74.1 1.0 copy-start.5
  74.1 1.2 copy-start.8
  75.2 1.0 copy-start.6
  76.3 1.0 copy-start.7
  76.3 1.2 copy-start.9
  78.5 9.3 %collective-permute-start.11 = (f32[64,2048]{1,0:T(8,128)S(1)}, f32[64,2048]{1,0:T(8,128)S(1)}, u32[]{:S(2)}, u32[]{:S(2)}) collective-permute-start(f32[64,2048]{1,0:T(8,128)S(1)} %pad_maximum_fusion.13), channel_id=1, source_target_pairs={{0,192},{1,49},{2,194},{3,51},{4,196},{5,53},{6,198},{7,55},{8,200... | collective-permute-start | bytes 1572872 | tf_op jit(solution)/shard_map/ppermute | solution.py:29
  80.8 9.5 %collective-permute-start.12 = (f32[64,2048]{1,0:T(8,128)S(1)}, f32[64,2048]{1,0:T(8,128)S(1)}, u32[]{:S(2)}, u32[]{:S(2)}) collective-permute-start(f32[64,2048]{1,0:T(8,128)S(1)} %pad_maximum_fusion.14), channel_id=1, source_target_pairs={{0,64},{1,17},{2,66},{3,19},{4,68},{5,21},{6,70},{7,23},{8,72},{9,... | collective-permute-start | bytes 1572872 | tf_op jit(solution)/shard_map/ppermute | solution.py:29
  83.9 9.5 %collective-permute-start.7 = (f32[64,2048]{1,0:T(8,128)S(1)}, f32[64,2048]{1,0:T(8,128)S(1)}, u32[]{:S(2)}, u32[]{:S(2)}) collective-permute-start(f32[64,2048]{1,0:T(8,128)S(1)} %pad_maximum_fusion.11), channel_id=1, source_target_pairs={{0,192},{1,49},{2,194},{3,51},{4,196},{5,53},{6,198},{7,55},{8,200... | collective-permute-start | bytes 1572872 | tf_op jit(solution)/shard_map/ppermute | solution.py:29
  87.8 8.4 %collective-permute-start.14 = (f32[64,1024]{1,0:T(8,128)S(1)}, f32[64,1024]{1,0:T(8,128)S(1)}, u32[]{:S(2)}, u32[]{:S(2)}) collective-permute-start(f32[64,1024]{1,0:T(8,128)S(1)} %slice_add_fusion), channel_id=1, source_target_pairs={{0,192},{1,49},{2,194},{3,51},{4,196},{5,53},{6,198},{7,55},{8,200... | collective-permute-start | bytes 786440 | tf_op jit(solution)/shard_map/ppermute | solution.py:29
  90.3 6.9 %collective-permute-start.13 = (f32[64,1024]{1,0:T(8,128)S(1)}, f32[64,1024]{1,0:T(8,128)S(1)}, u32[]{:S(2)}, u32[]{:S(2)}) collective-permute-start(f32[64,1024]{1,0:T(8,128)S(1)} %slice_add_fusion.2), channel_id=1, source_target_pairs={{0,64},{1,17},{2,66},{3,19},{4,68},{5,21},{6,70},{7,23},{8,72},{9,... | collective-permute-start | bytes 786440 | tf_op jit(solution)/shard_map/ppermute | solution.py:29
  91.2 15.4 %collective-permute-start.8 = (f32[64,2048]{1,0:T(8,128)}, f32[64,2048]{1,0:T(8,128)}, u32[]{:S(2)}, u32[]{:S(2)}) collective-permute-start(f32[64,2048]{1,0:T(8,128)} %pad_maximum_fusion.12), channel_id=1, source_target_pairs={{0,64},{1,17},{2,66},{3,19},{4,68},{5,21},{6,70},{7,23},{8,72},{9,... | collective-permute-start | bytes 1572872 | tf_op jit(solution)/shard_map/ppermute | solution.py:29
  93.4 4.0 %copy-start.12 = (f32[64,2048]{1,0:T(8,128)}, f32[64,2048]{1,0:T(8,128)S(1)}, u32[]{:S(2)}) copy-start(f32[64,2048]{1,0:T(8,128)S(1)} %collective-permute-done.7) | copy-start | bytes 1572868
  93.4 14.9 %collective-permute-start.10 = (f32[64,1024]{1,0:T(8,128)S(1)}, f32[64,1024]{1,0:T(8,128)S(1)}, u32[]{:S(2)}, u32[]{:S(2)}) collective-permute-start(f32[64,1024]{1,0:T(8,128)S(1)} %slice_add_fusion.4), channel_id=1, source_target_pairs={{0,192},{1,49},{2,194},{3,51},{4,196},{5,53},{6,198},{7,55},{8,200... | collective-permute-start | bytes 786440 | tf_op jit(solution)/shard_map/ppermute | solution.py:29
  98.2 23.5 %all-to-all-start.2 = ((f32[8,8,2048]{2,1,0:T(8,128)}), f32[8,8,2048]{2,1,0:T(8,128)S(1)}, u32[]{:S(2)}, u32[]{:S(2)}) async-start(f32[8,8,2048]{2,1,0:T(8,128)} %maximum_bitcast_fusion.1), calls=%async_computation.2 | async-start | bytes 1048576 | tf_op jit(solution)/shard_map/all_to_all | solution.py:121
  107.7 7.7 %collective-permute-start.9 = (f32[64,1024]{1,0:T(8,128)S(1)}, f32[64,1024]{1,0:T(8,128)S(1)}, u32[]{:S(2)}, u32[]{:S(2)}) collective-permute-start(f32[64,1024]{1,0:T(8,128)S(1)} %slice_add_fusion.6), channel_id=1, source_target_pairs={{0,64},{1,17},{2,66},{3,19},{4,68},{5,21},{6,70},{7,23},{8,72},{9,... | collective-permute-start | bytes 786440 | tf_op jit(solution)/shard_map/ppermute | solution.py:29
  121.7 17.7 %all-to-all-start.1 = ((f32[8,8,2048]{2,1,0:T(8,128)}), f32[8,8,2048]{2,1,0:T(8,128)S(1)}, u32[]{:S(2)}, u32[]{:S(2)}) async-start(f32[8,8,2048]{2,1,0:T(8,128)} %maximum_bitcast_fusion), calls=%async_computation.1 | async-start | bytes 1048576 | tf_op jit(solution)/shard_map/all_to_all | solution.py:121
  125.2 14.2 %collective-permute-start.15 = (f32[8,2048]{1,0:T(8,128)S(1)}, f32[8,2048]{1,0:T(8,128)S(1)}, u32[]{:S(2)}, u32[]{:S(2)}) collective-permute-start(f32[8,2048]{1,0:T(8,128)S(1)} %reduce_sum.19), channel_id=1, source_target_pairs={{0,1},{1,0},{2,3},{3,2},{4,5},{5,4},{6,7},{7,6},{8,9},{9,8},{10,11... | collective-permute-start | bytes 196616 | tf_op jit(solution)/shard_map/ppermute | solution.py:126
  125.3 14.8 %copy-start.1 = (bf16[112,4096]{1,0:T(8,128)(2,1)S(1)}, bf16[112,4096]{1,0:T(8,128)(2,1)}, u32[]{:S(2)}) copy-start(bf16[112,4096]{1,0:T(8,128)(2,1)} %param.9) | copy-start | bytes 2752516

commit v4 on v3

--- a/solution.py
+++ b/solution.py
@@ -55,8 +55,9 @@
     one = jnp.minimum(lengths[0, 0], 1).astype(jnp.float32)
 
     w_t = w_in.transpose(1, 2, 0).reshape(2 * units, width)
-    w_mine = jnp.where(north, w_t[:, :half], w_t[:, half:])
-    w_gate, w_up = w_mine[:units].astype(jnp.float32), w_mine[units:].astype(jnp.float32)
+    w_mine = lax.dynamic_slice_in_dim(w_t, rep * half, half, 1)
+    mine_of = lambda part: jnp.where(north, part[:, :half], part[:, half:]).astype(jnp.float32)
+    w_gate, w_up = mine_of(w_t[:units]), mine_of(w_t[units:])
     next_gate = hop(w_gate, dims, FIRST, -1)
     last_up = hop(w_up, dims, FIRST, 1)
     next_up = hop(w_up, dims, FIRST, -1)
@@ -72,7 +73,8 @@
     sig = jax.nn.sigmoid(gate)
     activated = gate * sig
     hidden = jnp.where(is_alive, activated * upward, 0.0).astype(jnp.bfloat16)
-    d_hidden = jnp.where(is_alive, dot(w_down, dy, 1, 1), 0.0)
+    d_hidden = dot(w_down, dy, 1, 1)
+    d_hidden = jnp.where(is_alive, d_hidden, 0.0)
     d_gate = d_hidden * upward * sig * (1.0 + gate * (1.0 - sig))
     d_up = d_hidden * activated
     d_in = jnp.concatenate([d_gate, d_up], axis=0).astype(jnp.bfloat16)
@@ -82,14 +84,14 @@
     turn = (position[:, None] == order[None, :]).astype(jnp.bfloat16)
     turned = dot(d_in, turn, 1, 0)
     plain = d_in.astype(jnp.float32)
-    theirs = lax.ppermute(jnp.where(north, plain, turned), "rep", SWAP)
-    ours = jnp.where(north, turned, plain)
+    away, ours = jnp.where(north, plain, turned), jnp.where(north, turned, plain)
+    theirs = lax.ppermute(away, "rep", SWAP)
 
     cols = rows // 4
     blocks = [jnp.concatenate([d[:, k * cols : (k + 1) * cols] for d in (ours, theirs)]) for k in range(4)]
     got = exchange(jnp.stack(blocks), dims, FIRST)
-    got = lax.dynamic_slice_in_dim(jnp.concatenate([got, got]), me, 4, 0)
-    d_all = (got * one).astype(jnp.bfloat16)
+    picked = [lax.dynamic_index_in_dim(got, (me + k) & 3, 0, False) for k in range(4)]
+    d_all = [(d * one).astype(jnp.bfloat16) for d in picked]
 
     g_in = dot(d_in, x, 1, 0)
     g_down = dot(hidden, dy, 1, 0)
@@ -104,29 +106,30 @@
     w_3 = jnp.concatenate([arrived(last_gate), arrived(last_up)])
     cut = half // 2
 
-    def row_sums(d):
+    def product(r):
+        at = ((r + rep) & 1) * 2 * units
+        d = [lax.dynamic_slice_in_dim(value, at, 2 * units, 0) for value in d_all]
         partial = dot(d[0], w_mine, 0, 0) + dot(d[1], w_1, 0, 0)
         partial = partial + dot(d[3], w_3, 0, 0) + dot(d[2], w_2, 0, 0)
-        blocks = partial.reshape(4, rows // 16, half)
-        blocks = jnp.concatenate([blocks, blocks])
-        mine, b1, b2, b3 = (lax.dynamic_index_in_dim(blocks, across + k, 0, False) for k in range(4))
-        r1 = hop(jnp.concatenate([b2[:, :cut], b1[:, cut:]], axis=1), dims, SECOND, 1)
-        r2 = hop(jnp.concatenate([b3[:, :cut], b2[:, cut:]], axis=1), dims, SECOND, -1)
-        up, down = b1[:, :cut] + r1[:, :cut], b3[:, cut:] + r2[:, cut:]
-        t1 = hop(up, dims, SECOND, 1)
-        t2 = hop(down, dims, SECOND, -1)
-        left = mine[:, :cut] + r2[:, :cut] + t1
-        right = mine[:, cut:] + r1[:, cut:] + t2
-        part = jnp.concatenate([left, right], axis=1).reshape(nz, own_rows, half)
-        got = lax.all_to_all(part, "dp_2", 0, 0, tiled=True)
-        return jnp.sum(got, axis=0)
+        return partial.reshape(4, rows // 16, half)
 
-    sum_theirs = row_sums(d_all[:, 2 * units :])
-    sum_ours = row_sums(d_all[:, : 2 * units])
-    other_half = lax.ppermute(sum_theirs, "rep", SWAP)
-    shard = jnp.concatenate(
-        [jnp.where(north, sum_ours, other_half), jnp.where(north, other_half, sum_ours)], axis=1
+    products = [product(r) for r in range(nr)]
+    mine, b1, b2, b3 = (
+        jnp.concatenate([lax.dynamic_index_in_dim(p, (across + k) & 3, 0, False) for p in products])
+        for k in range(4)
     )
+    r1 = hop(jnp.concatenate([b2[:, :cut], b1[:, cut:]], axis=1), dims, SECOND, 1)
+    r2 = hop(jnp.concatenate([b3[:, :cut], b2[:, cut:]], axis=1), dims, SECOND, -1)
+    up_2, down_2 = lax.optimization_barrier((b1[:, :cut] + r1[:, :cut], b3[:, cut:] + r2[:, cut:]))
+    t1 = hop(up_2, dims, SECOND, 1)
+    t2 = hop(down_2, dims, SECOND, -1)
+    left = mine[:, :cut] + r2[:, :cut] + t1
+    right = mine[:, cut:] + r1[:, cut:] + t2
+    part = jnp.concatenate([left, right], axis=1).reshape(nr, nz, own_rows, half)
+    part = part.transpose(1, 0, 2, 3).reshape(nz * nr, own_rows, half)
+    got = lax.all_to_all(part, ("dp_2", "rep"), 0, 0, tiled=True)
+    shard = jnp.sum(got.reshape(nz, nr, own_rows, half), axis=0)
+    shard = shard.transpose(1, 0, 2).reshape(own_rows, width)
     shared = (kept + back) * GRAD_SCALE
     return shard[None], shared.reshape(3, units, half).transpose(2, 0, 1)
 

time: 142 us -> 148 us (1.042)
  the two profiles are of different devices: /device:TPU:8 before, /device:TPU:1 now
where the time goes in v4:
time: 148 us
  waiting for transfers between devices  49.5 us (33%)
  starting transfers between devices  35.1 us (24%)
  other arithmetic  26.4 us (18%)
  matrix products  23.8 us (16%)
  local copies, waits for them, and re-layouts  10.5 us (7%)
  between operations  2.36 us (2%)
    ppermute x10, waiting for transfers between devices, hop(): return lax.ppermute(value, ALL, sorted(pairs))  26.9 us
    dot_general x13, matrix products, dot(): lax.dot_general(a, b, (((over_a,), (over_b,)), ((), ())), preferred_eleme...  23.8 us
    all_to_all x1, waiting for transfers between devices, per_device(): got = lax.all_to_all(part, ('dp_2', 'rep'), 0, 0, tiled=True)  22.5 us
    ppermute x10, starting transfers between devices, hop(): return lax.ppermute(value, ALL, sorted(pairs))  13.5 us
    all_to_all x1, starting transfers between devices, per_device(): got = lax.all_to_all(part, ('dp_2', 'rep'), 0, 0, tiled=True)  12.9 us
    convert_element_type x6, other arithmetic, per_device(): arrived = lambda p: (p * one).astype(jnp.bfloat16)  9.07 us
    mul x1, other arithmetic, per_device(): shared = (kept + back) * GRAD_SCALE  5.54 us
    all_to_all x1, starting transfers between devices, exchange(): lax.all_to_all(value, ALL, 0, 0, tiled=True, axis_index_groups=groups)  4.4 us
  transfers between devices with their start and end apart: 14, of which 5 were waited for; matrix products, arithmetic and copies ran while one was open for 29% of the time, Pallas kernels for 0%

profile of v4, /device:TPU:1, one launch (start us, length us, event | category | flops | bytes accessed | tf_op | source)
XLA Modules:
  0.0 147.7 jit_solution(17849406124521874350)
XLA Ops:
  0.7 3.0 %slice_bitcast_fusion.1 = (bf16[112,4096]{1,0:T(8,128)(2,1)}, bf16[112,4096]{1,0:T(8,128)(2,1)}) fusion(bf16[2,112,4096]{2,1,0:T(8,128)(2,1)} %bitcast.92), kind=kLoop, calls=%fused_computation.47 | loop fusion | bytes 3670016 | tf_op jit(solution)/shard_map/slice | solution.py:60
  3.7 2.4 %fusion.29 = f32[112,2048]{1,0:T(8,128)} fusion(bf16[112,4096]{1,0:T(8,128)(2,1)} %get-tuple-element.19, pred[]{:T(512)S(6)} %eq.19), kind=kLoop, calls=%fused_computation.82 | loop fusion | flops 458752 | bytes 1835009 | tf_op jit(solution)/shard_map/convert_element_type | solution.py:59
  6.1 2.1 %collective-permute-start.4 = (f32[112,2048]{1,0:T(8,128)}, f32[112,2048]{1,0:T(8,128)}, u32[]{:S(2)}, u32[]{:S(2)}) collective-permute-start(f32[112,2048]{1,0:T(8,128)} %fusion.29), channel_id=1, source_target_pairs={{0,16},{1,65},{2,18},{3,67},{4,20},{5,69},{6,22},{7,71},{8,24},{9,... | collective-permute-start | bytes 2752520 | tf_op jit(solution)/shard_map/ppermute | solution.py:29
  8.2 1.4 collective-permute-start.2
  9.6 0.6 fusion.83
  10.9 0.7 select_compare_fusion
  11.6 6.2 %fusion.2 = f32[224,1024]{1,0:T(8,128)S(1)} fusion(bf16[224,4096]{1,0:T(8,128)(2,1)S(1)} %bitcast.93, bf16[1,1024,4096]{2,1,0:T(8,128)(2,1)} %param.5), kind=kOutput, calls=%fused_computation.2 | convolution fusion | flops 1879048192 | bytes 11141120 | tf_op jit(solution)/shard_map/dot_general | solution.py:38
  17.8 2.9 %multiply_convert_fusion.11 = (bf16[112,1024]{1,0:T(8,128)(2,1)S(1)}, bf16[112,1024]{1,0:T(8,128)(2,1)S(1)}) fusion(f32[224,1024]{1,0:T(8,128)S(1)} %fusion.2, bf16[112,4096]{1,0:T(8,128)(2,1)S(1)} %copy-done, bf16[1,1024,4096]{2,1,0:T(8,128)(2,1)S(1)} %bitcast.87, pred[1024]{0:T(1024)(128)(4,1)S(1)} %select_compare_fusion), kind=kOutput, calls=%fused_computation.96 | convolution fusion | flops 941129728 | bytes 10683392 | tf_op jit(solution)/shard_map/dot_general | solution.py:38
  20.7 2.3 %convert_select_fusion.1 = (f32[224,1024]{1,0:T(8,128)}, f32[224,1024]{1,0:T(8,128)}) fusion(pred[]{:T(512)S(6)} %eq.19, bf16[112,1024]{1,0:T(8,128)(2,1)S(1)} %get-tuple-element.23, bf16[112,1024]{1,0:T(8,128)(2,1)S(1)} %get-tuple-element.22, s32[1024]{0:T(1024)S(1)} %fusion.68), kind=kOutput, calls=%fused_computation.34 | convolution fusion | flops 473104384 | bytes 2297857 | tf_op jit(solution)/shard_map/dot_general | solution.py:38
  23.0 2.9 %collective-permute-start = (f32[224,1024]{1,0:T(8,128)}, f32[224,1024]{1,0:T(8,128)}, u32[]{:S(2)}, u32[]{:S(2)}) collective-permute-start(f32[224,1024]{1,0:T(8,128)} %get-tuple-element.21), channel_id=1, source_target_pairs={{0,1},{1,0},{2,3},{3,2},{4,5},{5,4},{6,7},{7,6},{8,9},{9,8},{10,11... | collective-permute-start | bytes 2752520 | tf_op jit(solution)/shard_map/ppermute | solution.py:88
  25.9 1.0 fusion.30
  26.9 2.7 %collective-permute-start.1 = (f32[112,2048]{1,0:T(8,128)}, f32[112,2048]{1,0:T(8,128)}, u32[]{:S(2)}, u32[]{:S(2)}) collective-permute-start(f32[112,2048]{1,0:T(8,128)} %fusion.30), channel_id=1, source_target_pairs={{0,48},{1,193},{2,50},{3,195},{4,52},{5,197},{6,54},{7,199},{8,56}... | collective-permute-start | bytes 2752520 | tf_op jit(solution)/shard_map/ppermute | solution.py:29
  30.2 7.3 %fusion = f32[224,4096]{1,0:T(8,128)} fusion(bf16[1,1024,4096]{2,1,0:T(8,128)(2,1)} %param.5, bf16[112,1024]{1,0:T(8,128)(2,1)S(1)} %get-tuple-element.23, bf16[112,1024]{1,0:T(8,128)(2,1)S(1)} %get-tuple-element.22), kind=kOutput, calls=%fused_computation | convolution fusion | flops 1879965696 | bytes 12517376 | tf_op jit(solution)/shard_map/dot_general | solution.py:38
  37.7 1.3 fusion.82
  39.1 1.3 pad_maximum_fusion.1
  40.5 4.4 %all-to-all-start = ((f32[4,448,256]{2,1,0:T(8,128)}), f32[4,448,256]{2,1,0:T(8,128)}, u32[]{:S(2)}, u32[]{:S(2)}) async-start(f32[4,448,256]{2,1,0:T(8,128)} %pad_maximum_fusion.1), calls=%async_computation | async-start | bytes 3670016 | tf_op jit(solution)/shard_map/all_to_all | solution.py:34
  44.9 1.4 collective-permute-start.6
  46.3 1.5 %collective-permute-start.5 = (f32[112,2048]{1,0:T(8,128)}, f32[112,2048]{1,0:T(8,128)S(1)}, u32[]{:S(2)}, u32[]{:S(2)}) collective-permute-start(f32[112,2048]{1,0:T(8,128)} %collective-permute-done.1), channel_id=1, source_target_pairs={{0,48},{1,193},{2,50},{3,195},{4,52},{5,197},{6,54},{7,199},{8,56}... | collective-permute-start | bytes 2752520 | tf_op jit(solution)/shard_map/ppermute | solution.py:29
  47.9 1.2 multiply_convert_fusion.2
  49.1 2.0 %multiply_convert_fusion.5 = bf16[112,2048]{1,0:T(8,128)(2,1)} fusion(f32[112,2048]{1,0:T(8,128)} %collective-permute-done.1, f32[]{:T(128)S(6)} %convert_element_type.52), kind=kLoop, calls=%fused_computation.56 | loop fusion | flops 458752 | bytes 1376260 | tf_op jit(solution)/shard_map/convert_element_type | solution.py:103
  51.1 2.1 %multiply_convert_fusion.4 = bf16[112,2048]{1,0:T(8,128)(2,1)} fusion(f32[112,2048]{1,0:T(8,128)} %collective-permute-done.2, f32[]{:T(128)S(6)} %convert_element_type.52), kind=kLoop, calls=%fused_computation.55 | loop fusion | flops 458752 | bytes 1376260 | tf_op jit(solution)/shard_map/convert_element_type | solution.py:103
  53.2 2.0 %multiply_convert_fusion.3 = bf16[112,2048]{1,0:T(8,128)(2,1)} fusion(f32[112,2048]{1,0:T(8,128)} %collective-permute-done.3, f32[]{:T(128)S(6)} %convert_element_type.52), kind=kLoop, calls=%fused_computation.54 | loop fusion | flops 458752 | bytes 1376260 | tf_op jit(solution)/shard_map/convert_element_type | solution.py:103
  55.2 13.4 %collective-permute-done.6 = f32[112,2048]{1,0:T(8,128)S(1)} collective-permute-done((f32[112,2048]{1,0:T(8,128)}, f32[112,2048]{1,0:T(8,128)S(1)}, u32[]{:S(2)}, u32[]{:S(2)}) %collective-permute-start.6) | collective-permute-done | bytes 917536 | tf_op jit(solution)/shard_map/ppermute | solution.py:29
  68.6 0.9 multiply_convert_fusion
  69.5 0.8 multiply_convert_fusion.1
  70.3 1.6 %multiply_convert_fusion.6 = (bf16[1,448,256]{2,1,0:T(8,128)(2,1)S(1)}, bf16[1,448,256]{2,1,0:T(8,128)(2,1)S(1)}, bf16[1,448,256]{2,1,0:T(8,128)(2,1)S(1)}, bf16[1,448,256]{2,1,0:T(8,128)(2,1)S(1)}) fusion(f32[4,448,256]{2,1,0:T(8,128)} %all-to-all-done, s32[]{:T(128)S(6)} %select_n.155, f32[]{:T(128)S(6)} %convert_element_type.52, s32[]{:T(128)S(6)} %select_n.154, ...), kind=kLoop, calls=%fused_computation.91 | loop fusion | flops 917504 | bytes 2752532 | tf_op jit(solution)/shard_map/convert_element_type | solution.py:94
  71.9 0.5 fusion.17
  72.9 0.5 copy-done.4
  74.0 0.5 convolution_add_fusion.5
  74.5 0.5 copy-done.6
  75.6 0.5 convolution_add_fusion.4
  76.0 0.5 copy-done.5
  77.2 0.5 convolution_add_fusion.3
  78.4 1.5 %collective-permute-start.8 = (f32[128,2048]{1,0:T(8,128)S(1)}, f32[128,2048]{1,0:T(8,128)S(1)}, u32[]{:S(2)}, u32[]{:S(2)}) collective-permute-start(f32[128,2048]{1,0:T(8,128)S(1)} %fusion.15), channel_id=1, source_target_pairs={{0,64},{1,17},{2,66},{3,19},{4,68},{5,21},{6,70},{7,23},{8,72},{9,... | collective-permute-start | bytes 3145736 | tf_op jit(solution)/shard_map/ppermute | solution.py:29
  79.9 1.3 slice-done.3
  81.4 1.4 fusion.4
  82.8 0.6 copy-done.2
  83.5 2.0 %broadcast_select_fusion = f32[336,2048]{1,0:T(8,128)} fusion(pred[]{:T(512)S(6)} %eq.19, f32[112,4096]{1,0:T(8,128)S(1)} %fusion.4, f32[224,4096]{1,0:T(8,128)S(1)} %copy-done.2), kind=kLoop, calls=%fused_computation.23 | loop fusion | flops 2064384 | bytes 8257537 | tf_op jit(solution)/shard_map/jit(_where)/select_n | solution.py:100
  85.5 1.4 collective-permute-start.11
  86.9 5.3 %collective-permute-done.7 = f32[128,2048]{1,0:T(8,128)S(1)} collective-permute-done((f32[128,2048]{1,0:T(8,128)S(1)}, f32[128,2048]{1,0:T(8,128)S(1)}, u32[]{:S(2)}, u32[]{:S(2)}) %collective-permute-start.7) | collective-permute-done | bytes 1048608 | tf_op jit(solution)/shard_map/ppermute | solution.py:29
  92.3 1.3 collective-permute-done.8
  94.0 2.4 %collective-permute-start.10 = (f32[128,1024]{1,0:T(8,128)S(1)}, f32[128,1024]{1,0:T(8,128)S(1)}, u32[]{:S(2)}, u32[]{:S(2)}) collective-permute-start(f32[128,1024]{1,0:T(8,128)S(1)} %slice_add_fusion.1), channel_id=1, source_target_pairs={{0,192},{1,49},{2,194},{3,51},{4,196},{5,53},{6,198},{7,55},{8,200... | collective-permute-start | bytes 1572872 | tf_op jit(solution)/shard_map/ppermute | solution.py:29
  96.4 6.9 %collective-permute-done.9 = f32[128,1024]{1,0:T(8,128)S(1)} collective-permute-done((f32[128,1024]{1,0:T(8,128)S(1)}, f32[128,1024]{1,0:T(8,128)S(1)}, u32[]{:S(2)}, u32[]{:S(2)}) %collective-permute-start.9) | collective-permute-done | bytes 524320 | tf_op jit(solution)/shard_map/ppermute | solution.py:29
  103.6 1.1 copy.7
  104.8 12.9 %all-to-all-start.1 = ((f32[16,8,2048]{2,1,0:T(8,128)}), f32[16,8,2048]{2,1,0:T(8,128)}, u32[]{:S(2)}, u32[]{:S(2)}) async-start(f32[16,8,2048]{2,1,0:T(8,128)} %bitcast.96), calls=%async_computation.1 | async-start | bytes 2097152 | tf_op jit(solution)/shard_map/all_to_all | solution.py:130
  117.7 5.5 %add_multiply_fusion = f32[336,2048]{1,0:T(8,128)} fusion(f32[336,2048]{1,0:T(8,128)} %collective-permute-done.11, pred[]{:T(512)S(6)} %eq.19, f32[112,4096]{1,0:T(8,128)S(1)} %fusion.4, f32[224,4096]{1,0:T(8,128)} %fusion), kind=kLoop, calls=%fused_computation.14 | loop fusion | flops 3440640 | bytes 11010049 | tf_op jit(solution)/shard_map/mul | solution.py:133
  123.2 22.5 %all-to-all-done.1 = f32[16,8,2048]{2,1,0:T(8,128)} async-done(((f32[16,8,2048]{2,1,0:T(8,128)}), f32[16,8,2048]{2,1,0:T(8,128)}, u32[]{:S(2)}, u32[]{:S(2)}) %all-to-all-start.1) | async-done | bytes 1048608 | tf_op jit(solution)/shard_map/all_to_all | solution.py:130
  145.7 1.9 %reduce_sum.9 = f32[2,8,2048]{2,1,0:T(8,128)} reduce(f32[8,2,8,2048]{3,2,1,0:T(8,128)} %bitcast.34, f32[]{:T(128)} %constant.113.clone.1), dimensions={0}, to_apply=%region_0.1 | reduce | flops 229376 | bytes 1179652 | tf_op jit(solution)/shard_map/reduce_sum | solution.py:131
  (63 shorter events, 4.1 us)
Async XLA Ops:
  0.6 17.1 %copy-start = (bf16[112,4096]{1,0:T(8,128)(2,1)S(1)}, bf16[112,4096]{1,0:T(8,128)(2,1)}, u32[]{:S(2)}) copy-start(bf16[112,4096]{1,0:T(8,128)(2,1)} %param.9) | copy-start | bytes 2752516
  0.7 9.0 %copy-start.13 = (s32[1,2]{1,0:T(1,128)S(1)}, s32[1,2]{1,0:T(1,128)}, u32[]{:S(2)}) copy-start(s32[1,2]{1,0:T(1,128)} %param.7) | copy-start | bytes 28
  0.7 10.9 %copy-start.3 = (bf16[4096,2,112]{0,2,1:T(8,128)(2,1)S(1)}, bf16[4096,2,112]{0,2,1:T(8,128)(2,1)}, u32[]{:S(2)}) copy-start(bf16[4096,2,112]{0,2,1:T(8,128)(2,1)} %param.8) | copy-start | bytes 5505028
  3.7 14.0 %slice-start = ((s8[8388608]{0:T(1024)(128)(4,1)}), s8[4194304]{0:T(1024)(128)(4,1)S(1)}, s32[]{:S(2)}) async-start(s8[8388608]{0:T(1024)(128)(4,1)} %bitcast.86), calls=%async_computation.2 | async-start | bytes 8388608
  6.1 38.8 %collective-permute-start.4 = (f32[112,2048]{1,0:T(8,128)}, f32[112,2048]{1,0:T(8,128)}, u32[]{:S(2)}, u32[]{:S(2)}) collective-permute-start(f32[112,2048]{1,0:T(8,128)} %fusion.29), channel_id=1, source_target_pairs={{0,16},{1,65},{2,18},{3,67},{4,20},{5,69},{6,22},{7,71},{8,24},{9,... | collective-permute-start | bytes 2752520 | tf_op jit(solution)/shard_map/ppermute | solution.py:29
  8.2 42.9 %collective-permute-start.2 = (f32[112,2048]{1,0:T(8,128)}, f32[112,2048]{1,0:T(8,128)}, u32[]{:S(2)}, u32[]{:S(2)}) collective-permute-start(f32[112,2048]{1,0:T(8,128)} %fusion.29), channel_id=1, source_target_pairs={{0,48},{1,193},{2,50},{3,195},{4,52},{5,197},{6,54},{7,199},{8,56}... | collective-permute-start | bytes 2752520 | tf_op jit(solution)/shard_map/ppermute | solution.py:29
  11.5 6.2 %slice-start.1 = ((s8[8388608]{0:T(1024)(128)(4,1)}), s8[4194304]{0:T(1024)(128)(4,1)S(1)}, s32[]{:S(2)}) async-start(s8[8388608]{0:T(1024)(128)(4,1)} %bitcast.86), calls=%async_computation.3 | async-start | bytes 8388608
  17.8 2.9 %copy-start.11 = (f32[224,1024]{1,0:T(8,128)}, f32[224,1024]{1,0:T(8,128)S(1)}, u32[]{:S(2)}) copy-start(f32[224,1024]{1,0:T(8,128)S(1)} %fusion.2) | copy-start | bytes 2752516
  20.7 5.1 %copy-start.9 = (bf16[112,4096]{1,0:T(8,128)(2,1)S(1)}, bf16[112,4096]{1,0:T(8,128)(2,1)}, u32[]{:S(2)}) copy-start(bf16[112,4096]{1,0:T(8,128)(2,1)} %get-tuple-element.18) | copy-start | bytes 2752516
  23.0 14.7 %collective-permute-start = (f32[224,1024]{1,0:T(8,128)}, f32[224,1024]{1,0:T(8,128)}, u32[]{:S(2)}, u32[]{:S(2)}) collective-permute-start(f32[224,1024]{1,0:T(8,128)} %get-tuple-element.21), channel_id=1, source_target_pairs={{0,1},{1,0},{2,3},{3,2},{4,5},{5,4},{6,7},{7,6},{8,9},{9,8},{10,11... | collective-permute-start | bytes 2752520 | tf_op jit(solution)/shard_map/ppermute | solution.py:88
  26.9 26.3 %collective-permute-start.3 = (f32[112,2048]{1,0:T(8,128)}, f32[112,2048]{1,0:T(8,128)}, u32[]{:S(2)}, u32[]{:S(2)}) collective-permute-start(f32[112,2048]{1,0:T(8,128)} %fusion.30), channel_id=1, source_target_pairs={{0,16},{1,65},{2,18},{3,67},{4,20},{5,69},{6,22},{7,71},{8,24},{9,... | collective-permute-start | bytes 2752520 | tf_op jit(solution)/shard_map/ppermute | solution.py:29
  26.9 19.4 %collective-permute-start.1 = (f32[112,2048]{1,0:T(8,128)}, f32[112,2048]{1,0:T(8,128)}, u32[]{:S(2)}, u32[]{:S(2)}) collective-permute-start(f32[112,2048]{1,0:T(8,128)} %fusion.30), channel_id=1, source_target_pairs={{0,48},{1,193},{2,50},{3,195},{4,52},{5,197},{6,54},{7,199},{8,56}... | collective-permute-start | bytes 2752520 | tf_op jit(solution)/shard_map/ppermute | solution.py:29
  30.2 7.3 %copy-start.10 = (f32[224,1024]{1,0:T(8,128)S(1)}, f32[224,1024]{1,0:T(8,128)}, u32[]{:S(2)}) copy-start(f32[224,1024]{1,0:T(8,128)} %get-tuple-element.20) | copy-start | bytes 2752516
  40.5 29.9 %all-to-all-start = ((f32[4,448,256]{2,1,0:T(8,128)}), f32[4,448,256]{2,1,0:T(8,128)}, u32[]{:S(2)}, u32[]{:S(2)}) async-start(f32[4,448,256]{2,1,0:T(8,128)} %pad_maximum_fusion.1), calls=%async_computation | async-start | bytes 3670016 | tf_op jit(solution)/shard_map/all_to_all | solution.py:34
  44.9 23.7 %collective-permute-start.6 = (f32[112,2048]{1,0:T(8,128)}, f32[112,2048]{1,0:T(8,128)S(1)}, u32[]{:S(2)}, u32[]{:S(2)}) collective-permute-start(f32[112,2048]{1,0:T(8,128)} %collective-permute-done.4), channel_id=1, source_target_pairs={{0,16},{1,65},{2,18},{3,67},{4,20},{5,69},{6,22},{7,71},{8,24},{9,... | collective-permute-start | bytes 2752520 | tf_op jit(solution)/shard_map/ppermute | solution.py:29
  46.3 23.2 %collective-permute-start.5 = (f32[112,2048]{1,0:T(8,128)}, f32[112,2048]{1,0:T(8,128)S(1)}, u32[]{:S(2)}, u32[]{:S(2)}) collective-permute-start(f32[112,2048]{1,0:T(8,128)} %collective-permute-done.1), channel_id=1, source_target_pairs={{0,48},{1,193},{2,50},{3,195},{4,52},{5,197},{6,54},{7,199},{8,56}... | collective-permute-start | bytes 2752520 | tf_op jit(solution)/shard_map/ppermute | solution.py:29
  72.4 1.0 copy-start.4
  72.4 1.2 copy-start.7
  74.0 1.0 copy-start.6
  75.5 1.0 copy-start.5
  75.5 1.1 copy-start.8
  77.7 2.2 %slice-start.2 = ((s8[8388608]{0:T(1024)(128)(4,1)}), s8[4194304]{0:T(1024)(128)(4,1)S(1)}, s32[]{:S(2)}) async-start(s8[8388608]{0:T(1024)(128)(4,1)} %bitcast.88), calls=%async_computation.4 | async-start | bytes 8388608
  78.0 3.2 %slice-start.3 = ((s8[8388608]{0:T(1024)(128)(4,1)}), s8[4194304]{0:T(1024)(128)(4,1)S(1)}, s32[]{:S(2)}) async-start(s8[8388608]{0:T(1024)(128)(4,1)} %bitcast.88), calls=%async_computation.5 | async-start | bytes 8388608
  78.2 3.2 %copy-start.12 = (f32[224,1024]{1,0:T(8,128)S(1)}, f32[224,1024]{1,0:T(8,128)}, u32[]{:S(2)}) copy-start(f32[224,1024]{1,0:T(8,128)} %copy-done.11) | copy-start | bytes 2752516
  78.2 14.0 %collective-permute-start.7 = (f32[128,2048]{1,0:T(8,128)S(1)}, f32[128,2048]{1,0:T(8,128)S(1)}, u32[]{:S(2)}, u32[]{:S(2)}) collective-permute-start(f32[128,2048]{1,0:T(8,128)S(1)} %pad_maximum_fusion.2), channel_id=1, source_target_pairs={{0,192},{1,49},{2,194},{3,51},{4,196},{5,53},{6,198},{7,55},{8,200... | collective-permute-start | bytes 3145736 | tf_op jit(solution)/shard_map/ppermute | solution.py:29
  78.4 15.2 %collective-permute-start.8 = (f32[128,2048]{1,0:T(8,128)S(1)}, f32[128,2048]{1,0:T(8,128)S(1)}, u32[]{:S(2)}, u32[]{:S(2)}) collective-permute-start(f32[128,2048]{1,0:T(8,128)S(1)} %fusion.15), channel_id=1, source_target_pairs={{0,64},{1,17},{2,66},{3,19},{4,68},{5,21},{6,70},{7,23},{8,72},{9,... | collective-permute-start | bytes 3145736 | tf_op jit(solution)/shard_map/ppermute | solution.py:29
  81.4 2.0 %copy-start.2 = (f32[224,4096]{1,0:T(8,128)S(1)}, f32[224,4096]{1,0:T(8,128)}, u32[]{:S(2)}) copy-start(f32[224,4096]{1,0:T(8,128)} %fusion) | copy-start | bytes 11010052
  85.5 32.2 %collective-permute-start.11 = (f32[336,2048]{1,0:T(8,128)}, f32[336,2048]{1,0:T(8,128)}, u32[]{:S(2)}, u32[]{:S(2)}) collective-permute-start(f32[336,2048]{1,0:T(8,128)} %broadcast_select_fusion), channel_id=1, source_target_pairs={{0,1},{1,0},{2,3},{3,2},{4,5},{5,4},{6,7},{7,6},{8,9},{9,8},{10,11... | collective-permute-start | bytes 8257544 | tf_op jit(solution)/shard_map/ppermute | solution.py:101
  93.7 9.6 %collective-permute-start.9 = (f32[128,1024]{1,0:T(8,128)S(1)}, f32[128,1024]{1,0:T(8,128)S(1)}, u32[]{:S(2)}, u32[]{:S(2)}) collective-permute-start(f32[128,1024]{1,0:T(8,128)S(1)} %fusion.26), channel_id=1, source_target_pairs={{0,64},{1,17},{2,66},{3,19},{4,68},{5,21},{6,70},{7,23},{8,72},{9,... | collective-permute-start | bytes 1572872 | tf_op jit(solution)/shard_map/ppermute | solution.py:29
  94.0 9.3 %collective-permute-start.10 = (f32[128,1024]{1,0:T(8,128)S(1)}, f32[128,1024]{1,0:T(8,128)S(1)}, u32[]{:S(2)}, u32[]{:S(2)}) collective-permute-start(f32[128,1024]{1,0:T(8,128)S(1)} %slice_add_fusion.1), channel_id=1, source_target_pairs={{0,192},{1,49},{2,194},{3,51},{4,196},{5,53},{6,198},{7,55},{8,200... | collective-permute-start | bytes 1572872 | tf_op jit(solution)/shard_map/ppermute | solution.py:29
  104.8 41.0 %all-to-all-start.1 = ((f32[16,8,2048]{2,1,0:T(8,128)}), f32[16,8,2048]{2,1,0:T(8,128)}, u32[]{:S(2)}, u32[]{:S(2)}) async-start(f32[16,8,2048]{2,1,0:T(8,128)} %bitcast.96), calls=%async_computation.1 | async-start | bytes 2097152 | tf_op jit(solution)/shard_map/all_to_all | solution.py:130
  117.7 30.0 %copy-start.1 = (bf16[112,4096]{1,0:T(8,128)(2,1)S(1)}, bf16[112,4096]{1,0:T(8,128)(2,1)}, u32[]{:S(2)}) copy-start(bf16[112,4096]{1,0:T(8,128)(2,1)} %param.9) | copy-start | bytes 2752516

commit v5 on v4

--- a/solution.py
+++ b/solution.py
@@ -10,6 +10,7 @@
 ALL = DP + ("rep",)
 SWAP = [(0, 1), (1, 0)]
 GRAD_SCALE = 0.03125
+CHUNKS = 2
 FIRST, SECOND = (1, 0), (0, 1)
 
 
@@ -55,15 +56,17 @@
     one = jnp.minimum(lengths[0, 0], 1).astype(jnp.float32)
 
     w_t = w_in.transpose(1, 2, 0).reshape(2 * units, width)
-    w_mine = lax.dynamic_slice_in_dim(w_t, rep * half, half, 1)
-    mine_of = lambda part: jnp.where(north, part[:, :half], part[:, half:]).astype(jnp.float32)
-    w_gate, w_up = mine_of(w_t[:units]), mine_of(w_t[units:])
-    next_gate = hop(w_gate, dims, FIRST, -1)
-    last_up = hop(w_up, dims, FIRST, 1)
-    next_up = hop(w_up, dims, FIRST, -1)
-    last_gate = hop(w_gate, dims, FIRST, 1)
-    far_gate = hop(next_gate, dims, FIRST, -1)
-    far_up = hop(last_up, dims, FIRST, 1)
+    cut = half // CHUNKS
+    w_mine, near, far = [], [], []
+    for c in range(CHUNKS):
+        w_mine.append(lax.dynamic_slice_in_dim(w_t, rep * half + c * cut, cut, 1))
+        sent = w_mine[c].astype(jnp.float32)
+        w_next = hop(sent, dims, FIRST, -1)
+        w_last = hop(sent, dims, FIRST, 1)
+        far_gate = hop(w_next[:units], dims, FIRST, -1)
+        far_up = hop(w_last[units:], dims, FIRST, 1)
+        near.append((w_next, w_last))
+        far.append((far_gate, far_up))
 
     position = jnp.arange(rows)
     limit = jnp.where(position < slots, lengths[0, 0], slots + lengths[0, 1])
@@ -101,35 +104,36 @@
     back = lax.ppermute(away, "rep", SWAP)
 
     arrived = lambda p: (p * one).astype(jnp.bfloat16)
-    w_1 = jnp.concatenate([arrived(next_gate), arrived(next_up)])
-    w_2 = jnp.concatenate([arrived(far_gate), arrived(far_up)])
-    w_3 = jnp.concatenate([arrived(last_gate), arrived(last_up)])
-    cut = half // 2
+    edge = cut // 2
+    halves = []
+    for c in range(CHUNKS):
+        w_1, w_3 = arrived(near[c][0]), arrived(near[c][1])
+        w_2 = jnp.concatenate([arrived(far[c][0]), arrived(far[c][1])])
 
-    def product(r):
-        at = ((r + rep) & 1) * 2 * units
-        d = [lax.dynamic_slice_in_dim(value, at, 2 * units, 0) for value in d_all]
-        partial = dot(d[0], w_mine, 0, 0) + dot(d[1], w_1, 0, 0)
-        partial = partial + dot(d[3], w_3, 0, 0) + dot(d[2], w_2, 0, 0)
-        return partial.reshape(4, rows // 16, half)
+        def product(r):
+            at = ((r + rep) & 1) * 2 * units
+            d = [lax.dynamic_slice_in_dim(value, at, 2 * units, 0) for value in d_all]
+            partial = dot(d[0], w_mine[c], 0, 0) + dot(d[1], w_1, 0, 0)
+            partial = partial + dot(d[3], w_3, 0, 0) + dot(d[2], w_2, 0, 0)
+            return partial.reshape(4, rows // 16, cut)
 
-    products = [product(r) for r in range(nr)]
-    mine, b1, b2, b3 = (
-        jnp.concatenate([lax.dynamic_index_in_dim(p, (across + k) & 3, 0, False) for p in products])
-        for k in range(4)
-    )
-    r1 = hop(jnp.concatenate([b2[:, :cut], b1[:, cut:]], axis=1), dims, SECOND, 1)
-    r2 = hop(jnp.concatenate([b3[:, :cut], b2[:, cut:]], axis=1), dims, SECOND, -1)
-    up_2, down_2 = lax.optimization_barrier((b1[:, :cut] + r1[:, :cut], b3[:, cut:] + r2[:, cut:]))
-    t1 = hop(up_2, dims, SECOND, 1)
-    t2 = hop(down_2, dims, SECOND, -1)
-    left = mine[:, :cut] + r2[:, :cut] + t1
-    right = mine[:, cut:] + r1[:, cut:] + t2
-    part = jnp.concatenate([left, right], axis=1).reshape(nr, nz, own_rows, half)
-    part = part.transpose(1, 0, 2, 3).reshape(nz * nr, own_rows, half)
-    got = lax.all_to_all(part, ("dp_2", "rep"), 0, 0, tiled=True)
-    shard = jnp.sum(got.reshape(nz, nr, own_rows, half), axis=0)
-    shard = shard.transpose(1, 0, 2).reshape(own_rows, width)
+        products = [product(r) for r in range(nr)]
+        mine, b1, b2, b3 = (
+            jnp.concatenate([lax.dynamic_index_in_dim(p, (across + k) & 3, 0, False) for p in products])
+            for k in range(4)
+        )
+        r1 = hop(jnp.concatenate([b2[:, :edge], b1[:, edge:]], axis=1), dims, SECOND, 1)
+        r2 = hop(jnp.concatenate([b3[:, :edge], b2[:, edge:]], axis=1), dims, SECOND, -1)
+        up, down = lax.optimization_barrier((b1[:, :edge] + r1[:, :edge], b3[:, edge:] + r2[:, edge:]))
+        t1 = hop(up, dims, SECOND, 1)
+        t2 = hop(down, dims, SECOND, -1)
+        left = mine[:, :edge] + r2[:, :edge] + t1
+        right = mine[:, edge:] + r1[:, edge:] + t2
+        part = jnp.concatenate([left, right], axis=1).reshape(nr, nz, own_rows, cut)
+        part = part.transpose(1, 0, 2, 3).reshape(nz * nr, own_rows, cut)
+        got = lax.all_to_all(part, ("dp_2", "rep"), 0, 0, tiled=True)
+        halves.append(jnp.sum(got.reshape(nz, nr, own_rows, cut), axis=0))
+    shard = jnp.concatenate([h[r] for r in range(nr) for h in halves], axis=1)
     shared = (kept + back) * GRAD_SCALE
     return shard[None], shared.reshape(3, units, half).transpose(2, 0, 1)
 

time: 148 us -> 148 us (level)
  waiting for transfers between devices: 49.5 us -> 33.5 us
  matrix products: 23.8 us -> 37.5 us
  starting transfers between devices: 35.1 us -> 43.1 us
  other arithmetic: 26.4 us -> 22.8 us
  local copies, waits for them, and re-layouts: 10.5 us -> 7.84 us
    dot_general x13 -> x21, matrix products: 23.8 us -> 37.5 us  [dot(): lax.dot_general(a, b, (((over_a,), (over_b,)), ((), ())), preferred_eleme...]
    ppermute x10 -> x16, waiting for transfers between devices: 26.9 us -> 17.1 us  [hop(): return lax.ppermute(value, ALL, sorted(pairs))]
    convert_element_type x6 -> x4, other arithmetic: 9.07 us -> 2.85 us  [per_device(): arrived = lambda p: (p * one).astype(jnp.bfloat16)]
    all_to_all x1 -> x2, waiting for transfers between devices: 22.5 us -> 16.4 us  [per_device(): got = lax.all_to_all(part, ('dp_2', 'rep'), 0, 0, tiled=True)]
    ppermute x10 -> x16, starting transfers between devices: 13.5 us -> 18.6 us  [hop(): return lax.ppermute(value, ALL, sorted(pairs))]
    add x3 -> x6, other arithmetic: 0.4 us -> 3.37 us  [the longest x2 1.32 us: per_device(): left = mine[:, :edge] + r2[:, :edge] + t1]
    unnamed x36 -> x20, local copies, waits for them, and re-layouts: 4.09 us -> 1.26 us
    all_to_all x1 -> x2, starting transfers between devices: 12.9 us -> 15.7 us  [per_device(): got = lax.all_to_all(part, ('dp_2', 'rep'), 0, 0, tiled=True)]
  transfers between devices with their start and end apart: 14 -> 21, of which waited for: 5 -> 8; matrix products, arithmetic and copies ran while one was open for 29% -> 33% of each run, Pallas kernels for 0% -> 0%
where the time goes in v5:
time: 148 us; the launch traced here: 147 us
  starting transfers between devices  43.1 us (29%)
  matrix products  37.5 us (25%)
  waiting for transfers between devices  33.5 us (23%)
  other arithmetic  22.8 us (15%)
  local copies, waits for them, and re-layouts  7.84 us (5%)
  between operations  2.48 us (2%)
    dot_general x21, matrix products, dot(): lax.dot_general(a, b, (((over_a,), (over_b,)), ((), ())), preferred_eleme...  37.5 us
    ppermute x16, starting transfers between devices, hop(): return lax.ppermute(value, ALL, sorted(pairs))  18.6 us
    ppermute x16, waiting for transfers between devices, hop(): return lax.ppermute(value, ALL, sorted(pairs))  17.1 us
    all_to_all x2, waiting for transfers between devices, per_device(): got = lax.all_to_all(part, ('dp_2', 'rep'), 0, 0, tiled=True)  16.4 us
    all_to_all x2, starting transfers between devices, per_device(): got = lax.all_to_all(part, ('dp_2', 'rep'), 0, 0, tiled=True)  15.7 us
    mul x1, other arithmetic, per_device(): shared = (kept + back) * GRAD_SCALE  5.54 us
    all_to_all x1, starting transfers between devices, exchange(): lax.all_to_all(value, ALL, 0, 0, tiled=True, axis_index_groups=groups)  4.39 us
    ppermute x1, starting transfers between devices, per_device(): theirs = lax.ppermute(away, 'rep', SWAP)  3.2 us
  transfers between devices with their start and end apart: 21, of which 8 were waited for; matrix products, arithmetic and copies ran while one was open for 33% of the time, Pallas kernels for 0%

profile of v5, /device:TPU:1, one launch (start us, length us, event | category | flops | bytes accessed | tf_op | source)
XLA Modules:
  0.0 147.2 jit_solution(489531891843713092)
XLA Ops:
  0.7 1.3 fusion.126
  2.0 6.6 %fusion.2 = f32[224,1024]{1,0:T(8,128)S(1)} fusion(bf16[224,4096]{1,0:T(8,128)(2,1)} %bitcast.132, bf16[1,1024,4096]{2,1,0:T(8,128)(2,1)} %param.5), kind=kOutput, calls=%fused_computation.2 | convolution fusion | flops 1879048192 | bytes 11141120 | tf_op jit(solution)/shard_map/dot_general | solution.py:39
  9.9 6.3 %multiply_convert_fusion.13 = (bf16[112,1024]{1,0:T(8,128)(2,1)S(1)}, bf16[112,1024]{1,0:T(8,128)(2,1)S(1)}) fusion(f32[224,1024]{1,0:T(8,128)S(1)} %fusion.2, bf16[112,4096]{1,0:T(8,128)(2,1)S(1)} %copy-done, bf16[1,1024,4096]{2,1,0:T(8,128)(2,1)} %param.6, pred[1024]{0:T(1024)(128)(4,1)S(1)} %select_compare_fusion), kind=kOutput, calls=%fused_computation.90 | convolution fusion | flops 941129728 | bytes 10683392 | tf_op jit(solution)/shard_map/dot_general | solution.py:39
  16.2 2.3 %convert_select_fusion.1 = (f32[224,1024]{1,0:T(8,128)}, f32[224,1024]{1,0:T(8,128)}) fusion(pred[]{:T(512)S(6)} %eq.19, bf16[112,1024]{1,0:T(8,128)(2,1)S(1)} %get-tuple-element.19, bf16[112,1024]{1,0:T(8,128)(2,1)S(1)} %get-tuple-element.18, s32[1024]{0:T(1024)S(1)} %fusion.113), kind=kOutput, calls=%fused_computation.32 | convolution fusion | flops 473104384 | bytes 2297857 | tf_op jit(solution)/shard_map/dot_general | solution.py:39
  18.5 3.2 %collective-permute-start = (f32[224,1024]{1,0:T(8,128)}, f32[224,1024]{1,0:T(8,128)S(1)}, u32[]{:S(2)}, u32[]{:S(2)}) collective-permute-start(f32[224,1024]{1,0:T(8,128)} %get-tuple-element.17), channel_id=1, source_target_pairs={{0,1},{1,0},{2,3},{3,2},{4,5},{5,4},{6,7},{7,6},{8,9},{9,8},{10,11... | collective-permute-start | bytes 2752520 | tf_op jit(solution)/shard_map/ppermute | solution.py:91
  21.7 1.5 %dynamic-slice_convert_fusion.1 = (f32[224,1024]{1,0:T(8,128)}, f32[224,1024]{1,0:T(8,128)}) fusion(bf16[224,4096]{1,0:T(8,128)(2,1)S(1)} %bitcast.133, s32[]{:T(128)S(6)} %select_n.156, s32[]{:T(128)S(6)} %select_n.166), kind=kLoop, calls=%fused_computation.100 | loop fusion | flops 458752 | bytes 2752520 | tf_op jit(solution)/shard_map/convert_element_type | solution.py:63
  23.2 1.0 collective-permute-start.1
  24.7 2.2 %collective-permute-start.9 = (f32[224,1024]{1,0:T(8,128)}, f32[224,1024]{1,0:T(8,128)}, u32[]{:S(2)}, u32[]{:S(2)}) collective-permute-start(f32[224,1024]{1,0:T(8,128)} %get-tuple-element.11), channel_id=1, source_target_pairs={{0,48},{1,193},{2,50},{3,195},{4,52},{5,197},{6,54},{7,199},{8,56}... | collective-permute-start | bytes 2752520 | tf_op jit(solution)/shard_map/ppermute | solution.py:30
  26.9 7.2 %fusion = f32[224,4096]{1,0:T(8,128)} fusion(bf16[1,1024,4096]{2,1,0:T(8,128)(2,1)} %param.5, bf16[112,1024]{1,0:T(8,128)(2,1)S(1)} %get-tuple-element.19, bf16[112,1024]{1,0:T(8,128)(2,1)S(1)} %get-tuple-element.18), kind=kOutput, calls=%fused_computation | convolution fusion | flops 1879965696 | bytes 12517376 | tf_op jit(solution)/shard_map/dot_general | solution.py:39
  34.5 1.4 pad_maximum_fusion.1
  35.9 4.4 %all-to-all-start = ((f32[4,448,256]{2,1,0:T(8,128)}), f32[4,448,256]{2,1,0:T(8,128)}, u32[]{:S(2)}, u32[]{:S(2)}) async-start(f32[4,448,256]{2,1,0:T(8,128)} %pad_maximum_fusion.1), calls=%async_computation | async-start | bytes 3670016 | tf_op jit(solution)/shard_map/all_to_all | solution.py:35
  40.3 0.9 copy-done.3
  41.2 1.4 collective-permute-start.4
  42.6 5.1 %fusion.4 = f32[112,4096]{1,0:T(8,128)S(1)} fusion(bf16[1,1024,4096]{2,1,0:T(8,128)(2,1)} %param.6, f32[224,1024]{1,0:T(8,128)} %copy-done.9, pred[1024]{0:T(1024)(128)(4,1)S(1)} %select_compare_fusion), kind=kOutput, calls=%fused_computation.4 | convolution fusion | flops 940326912 | bytes 11142144 | tf_op jit(solution)/shard_map/dot_general | solution.py:39
  47.7 1.8 %slice.195 = f32[112,1024]{1,0:T(8,128)} slice(f32[224,1024]{1,0:T(8,128)} %collective-permute-done.1), slice={[0:112], [0:1024]} | slice | bytes 917504 | tf_op jit(solution)/shard_map/slice | solution.py:66
  49.5 1.3 collective-permute-start.3
  50.9 2.0 %broadcast_select_fusion = f32[336,2048]{1,0:T(8,128)} fusion(pred[]{:T(512)S(6)} %eq.19, f32[112,4096]{1,0:T(8,128)S(1)} %fusion.4, f32[224,4096]{1,0:T(8,128)S(1)} %copy-done.2), kind=kLoop, calls=%fused_computation.17 | loop fusion | flops 2064384 | bytes 8257537 | tf_op jit(solution)/shard_map/jit(_where)/select_n | solution.py:103
  52.8 1.2 collective-permute-start.17
  54.8 1.4 collective-permute-start.12
  56.1 1.0 slice.210
  57.2 1.5 %collective-permute-start.11 = (f32[112,1024]{1,0:T(8,128)S(1)}, f32[112,1024]{1,0:T(8,128)S(1)}, u32[]{:S(2)}, u32[]{:S(2)}) collective-permute-start(f32[112,1024]{1,0:T(8,128)S(1)} %slice.210), channel_id=1, source_target_pairs={{0,48},{1,193},{2,50},{3,195},{4,52},{5,197},{6,54},{7,199},{8,56}... | collective-permute-start | bytes 1376264 | tf_op jit(solution)/shard_map/ppermute | solution.py:30
  58.7 4.2 %collective-permute-done.4 = f32[112,1024]{1,0:T(8,128)} collective-permute-done((f32[112,1024]{1,0:T(8,128)S(1)}, f32[112,1024]{1,0:T(8,128)}, u32[]{:S(2)}, u32[]{:S(2)}) %collective-permute-start.4) | collective-permute-done | bytes 458784 | tf_op jit(solution)/shard_map/ppermute | solution.py:30
  62.9 1.0 multiply_convert_fusion.6
  64.0 1.1 multiply_convert_fusion.7
  65.0 2.7 %collective-permute-done.12 = f32[112,1024]{1,0:T(8,128)S(1)} collective-permute-done((f32[112,1024]{1,0:T(8,128)S(1)}, f32[112,1024]{1,0:T(8,128)S(1)}, u32[]{:S(2)}, u32[]{:S(2)}) %collective-permute-start.12) | collective-permute-done | bytes 458784 | tf_op jit(solution)/shard_map/ppermute | solution.py:30
  68.5 1.7 %multiply_convert_fusion.9 = (bf16[1,448,256]{2,1,0:T(8,128)(2,1)S(1)}, bf16[1,448,256]{2,1,0:T(8,128)(2,1)S(1)}, bf16[1,448,256]{2,1,0:T(8,128)(2,1)S(1)}, bf16[1,448,256]{2,1,0:T(8,128)(2,1)S(1)}) fusion(f32[4,448,256]{2,1,0:T(8,128)} %all-to-all-done, s32[]{:T(128)S(6)} %select_n.158, f32[]{:T(128)S(6)} %convert_element_type.58, s32[]{:T(128)S(6)} %select_n.159, ...), kind=kLoop, calls=%fused_computation.86 | loop fusion | flops 917504 | bytes 2752532 | tf_op jit(solution)/shard_map/convert_element_type | solution.py:97
  73.2 1.5 %convolution_add_fusion.5 = f32[256,1024]{1,0:T(8,128)S(1)} fusion(f32[256,1024]{1,0:T(8,128)S(1)} %fusion.29, f32[224,1024]{1,0:T(8,128)} %collective-permute-done.1, f32[]{:T(128)S(6)} %convert_element_type.58, bf16[1,448,256]{2,1,0:T(8,128)(2,1)S(1)} %get-tuple-element.14, s32[]{:T(128)S(6)} %select_n.162), kind=kOutput, calls=%fused_computation.26 | convolution fusion | flops 118161408 | bytes 3129352 | tf_op jit(solution)/shard_map/dot_general | solution.py:39
  75.2 1.5 %convolution_add_fusion.7 = f32[256,1024]{1,0:T(8,128)S(1)} fusion(f32[256,1024]{1,0:T(8,128)S(1)} %fusion.31, f32[224,1024]{1,0:T(8,128)} %collective-permute-done.1, f32[]{:T(128)S(6)} %convert_element_type.58, bf16[1,448,256]{2,1,0:T(8,128)(2,1)S(1)} %get-tuple-element.14, s32[]{:T(128)S(6)} %select_n.155), kind=kOutput, calls=%fused_computation.29 | convolution fusion | flops 118161408 | bytes 3129352 | tf_op jit(solution)/shard_map/dot_general | solution.py:39
  77.3 2.3 %collective-permute-start.5 = (f32[128,1024]{1,0:T(8,128)S(1)}, f32[128,1024]{1,0:T(8,128)S(1)}, u32[]{:S(2)}, u32[]{:S(2)}) collective-permute-start(f32[128,1024]{1,0:T(8,128)S(1)} %pad_maximum_fusion.2), channel_id=1, source_target_pairs={{0,192},{1,49},{2,194},{3,51},{4,196},{5,53},{6,198},{7,55},{8,200... | collective-permute-start | bytes 1572872 | tf_op jit(solution)/shard_map/ppermute | solution.py:30
  79.7 1.5 %convolution_add_fusion.1 = f32[256,1024]{1,0:T(8,128)S(1)} fusion(f32[256,1024]{1,0:T(8,128)S(1)} %fusion.25, f32[224,1024]{1,0:T(8,128)} %collective-permute-done.9, f32[]{:T(128)S(6)} %convert_element_type.58, bf16[1,448,256]{2,1,0:T(8,128)(2,1)S(1)} %get-tuple-element.14, s32[]{:T(128)S(6)} %select_n.162), kind=kOutput, calls=%fused_computation.20 | convolution fusion | flops 118161408 | bytes 3129352 | tf_op jit(solution)/shard_map/dot_general | solution.py:39
  81.2 1.5 %convolution_add_fusion.3 = f32[256,1024]{1,0:T(8,128)S(1)} fusion(f32[256,1024]{1,0:T(8,128)S(1)} %fusion.27, f32[224,1024]{1,0:T(8,128)} %collective-permute-done.9, f32[]{:T(128)S(6)} %convert_element_type.58, bf16[1,448,256]{2,1,0:T(8,128)(2,1)S(1)} %get-tuple-element.14, s32[]{:T(128)S(6)} %select_n.155), kind=kOutput, calls=%fused_computation.23 | convolution fusion | flops 118161408 | bytes 3129352 | tf_op jit(solution)/shard_map/dot_general | solution.py:39
  83.6 2.0 %collective-permute-done.5 = f32[128,1024]{1,0:T(8,128)S(1)} collective-permute-done((f32[128,1024]{1,0:T(8,128)S(1)}, f32[128,1024]{1,0:T(8,128)S(1)}, u32[]{:S(2)}, u32[]{:S(2)}) %collective-permute-start.5) | collective-permute-done | bytes 524320 | tf_op jit(solution)/shard_map/ppermute | solution.py:30
  85.7 3.5 %collective-permute-done.6 = f32[128,1024]{1,0:T(8,128)S(1)} collective-permute-done((f32[128,1024]{1,0:T(8,128)S(1)}, f32[128,1024]{1,0:T(8,128)S(1)}, u32[]{:S(2)}, u32[]{:S(2)}) %collective-permute-start.6) | collective-permute-done | bytes 524320 | tf_op jit(solution)/shard_map/ppermute | solution.py:30
  89.3 2.7 %collective-permute-start.8 = (f32[128,512]{1,0:T(8,128)S(1)}, f32[128,512]{1,0:T(8,128)S(1)}, u32[]{:S(2)}, u32[]{:S(2)}) collective-permute-start(f32[128,512]{1,0:T(8,128)S(1)} %slice_add_fusion.3), channel_id=1, source_target_pairs={{0,192},{1,49},{2,194},{3,51},{4,196},{5,53},{6,198},{7,55},{8,200... | collective-permute-start | bytes 786440 | tf_op jit(solution)/shard_map/ppermute | solution.py:30
  92.0 0.9 pad_maximum_fusion.4
  93.7 1.5 collective-permute-start.14
  95.9 0.9 copy.7
  96.8 12.2 %all-to-all-start.1 = ((f32[16,8,1024]{2,1,0:T(8,128)}), f32[16,8,1024]{2,1,0:T(8,128)}, u32[]{:S(2)}, u32[]{:S(2)}) async-start(f32[16,8,1024]{2,1,0:T(8,128)} %bitcast.31), calls=%async_computation.1 | async-start | bytes 1048576 | tf_op jit(solution)/shard_map/all_to_all | solution.py:134
  109.0 1.0 slice_add_fusion.1
  110.0 1.0 fusion.46
  111.1 2.7 %collective-permute-start.16 = (f32[128,512]{1,0:T(8,128)S(1)}, f32[128,512]{1,0:T(8,128)S(1)}, u32[]{:S(2)}, u32[]{:S(2)}) collective-permute-start(f32[128,512]{1,0:T(8,128)S(1)} %slice_add_fusion.1), channel_id=1, source_target_pairs={{0,192},{1,49},{2,194},{3,51},{4,196},{5,53},{6,198},{7,55},{8,200... | collective-permute-start | bytes 786440 | tf_op jit(solution)/shard_map/ppermute | solution.py:30
  113.8 4.2 %collective-permute-done.15 = f32[128,512]{1,0:T(8,128)S(1)} collective-permute-done((f32[128,512]{1,0:T(8,128)S(1)}, f32[128,512]{1,0:T(8,128)S(1)}, u32[]{:S(2)}, u32[]{:S(2)}) %collective-permute-start.15) | collective-permute-done | bytes 262176 | tf_op jit(solution)/shard_map/ppermute | solution.py:30
  117.9 1.2 fusion.40
  120.0 6.3 %all-to-all-done.1 = f32[16,8,1024]{2,1,0:T(8,128)} async-done(((f32[16,8,1024]{2,1,0:T(8,128)}), f32[16,8,1024]{2,1,0:T(8,128)}, u32[]{:S(2)}, u32[]{:S(2)}) %all-to-all-start.1) | async-done | bytes 524320 | tf_op jit(solution)/shard_map/all_to_all | solution.py:134
  126.3 3.5 %all-to-all-start.2 = ((f32[16,8,1024]{2,1,0:T(8,128)}), f32[16,8,1024]{2,1,0:T(8,128)S(1)}, u32[]{:S(2)}, u32[]{:S(2)}) async-start(f32[16,8,1024]{2,1,0:T(8,128)} %bitcast.46), calls=%async_computation.2 | async-start | bytes 1048576 | tf_op jit(solution)/shard_map/all_to_all | solution.py:134
  129.8 5.5 %add_multiply_fusion = f32[336,2048]{1,0:T(8,128)} fusion(f32[336,2048]{1,0:T(8,128)} %collective-permute-done.17, pred[]{:T(512)S(6)} %eq.19, f32[112,4096]{1,0:T(8,128)S(1)} %fusion.4, f32[224,4096]{1,0:T(8,128)} %fusion), kind=kLoop, calls=%fused_computation.14 | loop fusion | flops 3440640 | bytes 11010049 | tf_op jit(solution)/shard_map/mul | solution.py:137
  135.4 1.1 reduce_sum.18
  136.5 10.0 %all-to-all-done.2 = f32[16,8,1024]{2,1,0:T(8,128)S(1)} async-done(((f32[16,8,1024]{2,1,0:T(8,128)}), f32[16,8,1024]{2,1,0:T(8,128)S(1)}, u32[]{:S(2)}, u32[]{:S(2)}) %all-to-all-start.2) | async-done | bytes 524320 | tf_op jit(solution)/shard_map/all_to_all | solution.py:134
  (82 shorter events, 10.6 us)
Async XLA Ops:
  0.6 9.3 %copy-start = (bf16[112,4096]{1,0:T(8,128)(2,1)S(1)}, bf16[112,4096]{1,0:T(8,128)(2,1)}, u32[]{:S(2)}) copy-start(bf16[112,4096]{1,0:T(8,128)(2,1)} %param.9) | copy-start | bytes 2752516
  8.6 1.3 copy-start.9
  16.2 5.5 %copy-start.5 = (bf16[4096,2,112]{0,2,1:T(8,128)(2,1)S(1)}, bf16[4096,2,112]{0,2,1:T(8,128)(2,1)}, u32[]{:S(2)}) copy-start(bf16[4096,2,112]{0,2,1:T(8,128)(2,1)} %param.8) | copy-start | bytes 5505028
  18.5 15.7 %collective-permute-start = (f32[224,1024]{1,0:T(8,128)}, f32[224,1024]{1,0:T(8,128)S(1)}, u32[]{:S(2)}, u32[]{:S(2)}) collective-permute-start(f32[224,1024]{1,0:T(8,128)} %get-tuple-element.17), channel_id=1, source_target_pairs={{0,1},{1,0},{2,3},{3,2},{4,5},{5,4},{6,7},{7,6},{8,9},{9,8},{10,11... | collective-permute-start | bytes 2752520 | tf_op jit(solution)/shard_map/ppermute | solution.py:91
  23.2 24.5 %collective-permute-start.1 = (f32[224,1024]{1,0:T(8,128)}, f32[224,1024]{1,0:T(8,128)}, u32[]{:S(2)}, u32[]{:S(2)}) collective-permute-start(f32[224,1024]{1,0:T(8,128)} %get-tuple-element.10), channel_id=1, source_target_pairs={{0,48},{1,193},{2,50},{3,195},{4,52},{5,197},{6,54},{7,199},{8,56}... | collective-permute-start | bytes 2752520 | tf_op jit(solution)/shard_map/ppermute | solution.py:30
  24.3 16.0 %collective-permute-start.2 = (f32[224,1024]{1,0:T(8,128)}, f32[224,1024]{1,0:T(8,128)S(1)}, u32[]{:S(2)}, u32[]{:S(2)}) collective-permute-start(f32[224,1024]{1,0:T(8,128)} %get-tuple-element.10), channel_id=1, source_target_pairs={{0,16},{1,65},{2,18},{3,67},{4,20},{5,69},{6,22},{7,71},{8,24},{9,... | collective-permute-start | bytes 2752520 | tf_op jit(solution)/shard_map/ppermute | solution.py:30
  24.7 9.5 %copy-start.8 = (f32[224,1024]{1,0:T(8,128)S(1)}, f32[224,1024]{1,0:T(8,128)}, u32[]{:S(2)}) copy-start(f32[224,1024]{1,0:T(8,128)} %get-tuple-element.16) | copy-start | bytes 2752516
  24.7 31.5 %collective-permute-start.9 = (f32[224,1024]{1,0:T(8,128)}, f32[224,1024]{1,0:T(8,128)}, u32[]{:S(2)}, u32[]{:S(2)}) collective-permute-start(f32[224,1024]{1,0:T(8,128)} %get-tuple-element.11), channel_id=1, source_target_pairs={{0,48},{1,193},{2,50},{3,195},{4,52},{5,197},{6,54},{7,199},{8,56}... | collective-permute-start | bytes 2752520 | tf_op jit(solution)/shard_map/ppermute | solution.py:30
  26.9 27.8 %collective-permute-start.10 = (f32[224,1024]{1,0:T(8,128)}, f32[224,1024]{1,0:T(8,128)S(1)}, u32[]{:S(2)}, u32[]{:S(2)}) collective-permute-start(f32[224,1024]{1,0:T(8,128)} %get-tuple-element.11), channel_id=1, source_target_pairs={{0,16},{1,65},{2,18},{3,67},{4,20},{5,69},{6,22},{7,71},{8,24},{9,... | collective-permute-start | bytes 2752520 | tf_op jit(solution)/shard_map/ppermute | solution.py:30
  35.9 32.6 %all-to-all-start = ((f32[4,448,256]{2,1,0:T(8,128)}), f32[4,448,256]{2,1,0:T(8,128)}, u32[]{:S(2)}, u32[]{:S(2)}) async-start(f32[4,448,256]{2,1,0:T(8,128)} %pad_maximum_fusion.1), calls=%async_computation | async-start | bytes 3670016 | tf_op jit(solution)/shard_map/all_to_all | solution.py:35
  40.3 0.9 copy-start.3
  41.2 21.7 %collective-permute-start.4 = (f32[112,1024]{1,0:T(8,128)S(1)}, f32[112,1024]{1,0:T(8,128)}, u32[]{:S(2)}, u32[]{:S(2)}) collective-permute-start(f32[112,1024]{1,0:T(8,128)S(1)} %slice.196), channel_id=1, source_target_pairs={{0,16},{1,65},{2,18},{3,67},{4,20},{5,69},{6,22},{7,71},{8,24},{9,... | collective-permute-start | bytes 1376264 | tf_op jit(solution)/shard_map/ppermute | solution.py:30
  42.6 8.2 %copy-start.2 = (f32[224,4096]{1,0:T(8,128)S(1)}, f32[224,4096]{1,0:T(8,128)}, u32[]{:S(2)}) copy-start(f32[224,4096]{1,0:T(8,128)} %fusion) | copy-start | bytes 11010052
  49.5 14.4 %collective-permute-start.3 = (f32[112,1024]{1,0:T(8,128)}, f32[112,1024]{1,0:T(8,128)}, u32[]{:S(2)}, u32[]{:S(2)}) collective-permute-start(f32[112,1024]{1,0:T(8,128)} %slice.195), channel_id=1, source_target_pairs={{0,48},{1,193},{2,50},{3,195},{4,52},{5,197},{6,54},{7,199},{8,56}... | collective-permute-start | bytes 1376264 | tf_op jit(solution)/shard_map/ppermute | solution.py:30
  52.8 77.0 %collective-permute-start.17 = (f32[336,2048]{1,0:T(8,128)}, f32[336,2048]{1,0:T(8,128)}, u32[]{:S(2)}, u32[]{:S(2)}) collective-permute-start(f32[336,2048]{1,0:T(8,128)} %broadcast_select_fusion), channel_id=1, source_target_pairs={{0,1},{1,0},{2,3},{3,2},{4,5},{5,4},{6,7},{7,6},{8,9},{9,8},{10,11... | collective-permute-start | bytes 8257544 | tf_op jit(solution)/shard_map/ppermute | solution.py:104
  54.8 12.9 %collective-permute-start.12 = (f32[112,1024]{1,0:T(8,128)S(1)}, f32[112,1024]{1,0:T(8,128)S(1)}, u32[]{:S(2)}, u32[]{:S(2)}) collective-permute-start(f32[112,1024]{1,0:T(8,128)S(1)} %slice.211), channel_id=1, source_target_pairs={{0,16},{1,65},{2,18},{3,67},{4,20},{5,69},{6,22},{7,71},{8,24},{9,... | collective-permute-start | bytes 1376264 | tf_op jit(solution)/shard_map/ppermute | solution.py:30
  57.2 10.5 %collective-permute-start.11 = (f32[112,1024]{1,0:T(8,128)S(1)}, f32[112,1024]{1,0:T(8,128)S(1)}, u32[]{:S(2)}, u32[]{:S(2)}) collective-permute-start(f32[112,1024]{1,0:T(8,128)S(1)} %slice.210), channel_id=1, source_target_pairs={{0,48},{1,193},{2,50},{3,195},{4,52},{5,197},{6,54},{7,199},{8,56}... | collective-permute-start | bytes 1376264 | tf_op jit(solution)/shard_map/ppermute | solution.py:30
  68.5 2.1 %copy-start.6 = (bf16[4096,2,112]{0,2,1:T(8,128)(2,1)S(1)}, bf16[4096,2,112]{0,2,1:T(8,128)(2,1)}, u32[]{:S(2)}) copy-start(bf16[4096,2,112]{0,2,1:T(8,128)(2,1)} %param.8) | copy-start | bytes 5505028
  71.5 1.0 copy-start.7
  72.9 1.9 %copy-start.4 = (f32[224,1024]{1,0:T(8,128)S(1)}, f32[224,1024]{1,0:T(8,128)}, u32[]{:S(2)}) copy-start(f32[224,1024]{1,0:T(8,128)} %copy-done.3) | copy-start | bytes 2752516
  77.3 8.4 %collective-permute-start.5 = (f32[128,1024]{1,0:T(8,128)S(1)}, f32[128,1024]{1,0:T(8,128)S(1)}, u32[]{:S(2)}, u32[]{:S(2)}) collective-permute-start(f32[128,1024]{1,0:T(8,128)S(1)} %pad_maximum_fusion.2), channel_id=1, source_target_pairs={{0,192},{1,49},{2,194},{3,51},{4,196},{5,53},{6,198},{7,55},{8,200... | collective-permute-start | bytes 1572872 | tf_op jit(solution)/shard_map/ppermute | solution.py:30
  79.6 9.6 %collective-permute-start.6 = (f32[128,1024]{1,0:T(8,128)S(1)}, f32[128,1024]{1,0:T(8,128)S(1)}, u32[]{:S(2)}, u32[]{:S(2)}) collective-permute-start(f32[128,1024]{1,0:T(8,128)S(1)} %fusion.22), channel_id=1, source_target_pairs={{0,64},{1,17},{2,66},{3,19},{4,68},{5,21},{6,70},{7,23},{8,72},{9,... | collective-permute-start | bytes 1572872 | tf_op jit(solution)/shard_map/ppermute | solution.py:30
  89.2 6.5 %collective-permute-start.7 = (f32[128,512]{1,0:T(8,128)S(1)}, f32[128,512]{1,0:T(8,128)S(1)}, u32[]{:S(2)}, u32[]{:S(2)}) collective-permute-start(f32[128,512]{1,0:T(8,128)S(1)} %fusion.49), channel_id=1, source_target_pairs={{0,64},{1,17},{2,66},{3,19},{4,68},{5,21},{6,70},{7,23},{8,72},{9,... | collective-permute-start | bytes 786440 | tf_op jit(solution)/shard_map/ppermute | solution.py:30
  89.3 6.4 %collective-permute-start.8 = (f32[128,512]{1,0:T(8,128)S(1)}, f32[128,512]{1,0:T(8,128)S(1)}, u32[]{:S(2)}, u32[]{:S(2)}) collective-permute-start(f32[128,512]{1,0:T(8,128)S(1)} %slice_add_fusion.3), channel_id=1, source_target_pairs={{0,192},{1,49},{2,194},{3,51},{4,196},{5,53},{6,198},{7,55},{8,200... | collective-permute-start | bytes 786440 | tf_op jit(solution)/shard_map/ppermute | solution.py:30
  92.9 16.2 %collective-permute-start.13 = (f32[128,1024]{1,0:T(8,128)}, f32[128,1024]{1,0:T(8,128)}, u32[]{:S(2)}, u32[]{:S(2)}) collective-permute-start(f32[128,1024]{1,0:T(8,128)} %pad_maximum_fusion.4), channel_id=1, source_target_pairs={{0,192},{1,49},{2,194},{3,51},{4,196},{5,53},{6,198},{7,55},{8,200... | collective-permute-start | bytes 1572872 | tf_op jit(solution)/shard_map/ppermute | solution.py:30
  93.7 16.3 %collective-permute-start.14 = (f32[128,1024]{1,0:T(8,128)}, f32[128,1024]{1,0:T(8,128)}, u32[]{:S(2)}, u32[]{:S(2)}) collective-permute-start(f32[128,1024]{1,0:T(8,128)} %fusion.19), channel_id=1, source_target_pairs={{0,64},{1,17},{2,66},{3,19},{4,68},{5,21},{6,70},{7,23},{8,72},{9,... | collective-permute-start | bytes 1572872 | tf_op jit(solution)/shard_map/ppermute | solution.py:30
  96.8 29.5 %all-to-all-start.1 = ((f32[16,8,1024]{2,1,0:T(8,128)}), f32[16,8,1024]{2,1,0:T(8,128)}, u32[]{:S(2)}, u32[]{:S(2)}) async-start(f32[16,8,1024]{2,1,0:T(8,128)} %bitcast.31), calls=%async_computation.1 | async-start | bytes 1048576 | tf_op jit(solution)/shard_map/all_to_all | solution.py:134
  111.0 6.9 %collective-permute-start.15 = (f32[128,512]{1,0:T(8,128)S(1)}, f32[128,512]{1,0:T(8,128)S(1)}, u32[]{:S(2)}, u32[]{:S(2)}) collective-permute-start(f32[128,512]{1,0:T(8,128)S(1)} %fusion.46), channel_id=1, source_target_pairs={{0,64},{1,17},{2,66},{3,19},{4,68},{5,21},{6,70},{7,23},{8,72},{9,... | collective-permute-start | bytes 786440 | tf_op jit(solution)/shard_map/ppermute | solution.py:30
  111.1 6.8 %collective-permute-start.16 = (f32[128,512]{1,0:T(8,128)S(1)}, f32[128,512]{1,0:T(8,128)S(1)}, u32[]{:S(2)}, u32[]{:S(2)}) collective-permute-start(f32[128,512]{1,0:T(8,128)S(1)} %slice_add_fusion.1), channel_id=1, source_target_pairs={{0,192},{1,49},{2,194},{3,51},{4,196},{5,53},{6,198},{7,55},{8,200... | collective-permute-start | bytes 786440 | tf_op jit(solution)/shard_map/ppermute | solution.py:30
  126.3 20.2 %all-to-all-start.2 = ((f32[16,8,1024]{2,1,0:T(8,128)}), f32[16,8,1024]{2,1,0:T(8,128)S(1)}, u32[]{:S(2)}, u32[]{:S(2)}) async-start(f32[16,8,1024]{2,1,0:T(8,128)} %bitcast.46), calls=%async_computation.2 | async-start | bytes 1048576 | tf_op jit(solution)/shard_map/all_to_all | solution.py:134
  129.8 17.4 %copy-start.1 = (bf16[112,4096]{1,0:T(8,128)(2,1)S(1)}, bf16[112,4096]{1,0:T(8,128)(2,1)}, u32[]{:S(2)}) copy-start(bf16[112,4096]{1,0:T(8,128)(2,1)} %param.9) | copy-start | bytes 2752516

commit v6 on v4

--- a/solution.py
+++ b/solution.py
@@ -56,8 +56,7 @@
 
     w_t = w_in.transpose(1, 2, 0).reshape(2 * units, width)
     w_mine = lax.dynamic_slice_in_dim(w_t, rep * half, half, 1)
-    mine_of = lambda part: jnp.where(north, part[:, :half], part[:, half:]).astype(jnp.float32)
-    w_gate, w_up = mine_of(w_t[:units]), mine_of(w_t[units:])
+    w_gate, w_up = w_mine[:units].astype(jnp.float32), w_mine[units:].astype(jnp.float32)
     next_gate = hop(w_gate, dims, FIRST, -1)
     last_up = hop(w_up, dims, FIRST, 1)
     next_up = hop(w_up, dims, FIRST, -1)
@@ -126,10 +125,28 @@
     left = mine[:, :cut] + r2[:, :cut] + t1
     right = mine[:, cut:] + r1[:, cut:] + t2
     part = jnp.concatenate([left, right], axis=1).reshape(nr, nz, own_rows, half)
-    part = part.transpose(1, 0, 2, 3).reshape(nz * nr, own_rows, half)
-    got = lax.all_to_all(part, ("dp_2", "rep"), 0, 0, tiled=True)
-    shard = jnp.sum(got.reshape(nz, nr, own_rows, half), axis=0)
-    shard = shard.transpose(1, 0, 2).reshape(own_rows, width)
+    iz = lax.axis_index("dp_2")
+    at_z = lambda k: lax.dynamic_index_in_dim(part, (iz + k) & 7, 1, False).reshape(-1, half)
+    b0, b1, b2, b3, b4, b5, b6, b7 = (at_z(k) for k in range(nz))
+    along = (2, 2)
+    ru = hop(jnp.concatenate([b3, b4[:, :cut]], axis=1), dims, along, 2)
+    rd = hop(jnp.concatenate([b5, b4[:, cut:]], axis=1), dims, along, -2)
+    near_up, near_down = b1 + ru[:, :half], b7 + rd[:, :half]
+    far_up_sum = jnp.concatenate([b2[:, :cut] + ru[:, half:], b2[:, cut:]], axis=1)
+    far_down_sum = jnp.concatenate([b6[:, :cut], b6[:, cut:] + rd[:, half:]], axis=1)
+    near_up, near_down, far_up_sum, far_down_sum = lax.optimization_barrier(
+        (near_up, near_down, far_up_sum, far_down_sum)
+    )
+    s2 = hop(far_up_sum, dims, along, 2)
+    s6 = hop(far_down_sum, dims, along, -2)
+    s1 = hop(near_up, dims, along, 1)
+    s7 = hop(near_down, dims, along, -1)
+    total = (b0 + s1 + s7 + s2 + s6).reshape(nr, own_rows, half)
+    kept_half = lax.dynamic_index_in_dim(total, rep, 0, False)
+    other_half = lax.ppermute(lax.dynamic_index_in_dim(total, 1 - rep, 0, False), "rep", SWAP)
+    shard = jnp.concatenate(
+        [jnp.where(north, kept_half, other_half), jnp.where(north, other_half, kept_half)], axis=1
+    )
     shared = (kept + back) * GRAD_SCALE
     return shard[None], shared.reshape(3, units, half).transpose(2, 0, 1)
 

time: 148 us -> 141 us (0.953)
  the two profiles are of different devices: /device:TPU:1 before, /device:TPU:8 now
where the time goes in v6:
time: 141 us; the launch traced here: 138 us
  waiting for transfers between devices  52.9 us (38%)
  starting transfers between devices  32.9 us (23%)
  other arithmetic  24.3 us (17%)
  matrix products  19.3 us (14%)
  local copies, waits for them, and re-layouts  6.53 us (5%)
  between operations  2.48 us (2%)
    ppermute x16, waiting for transfers between devices, hop(): return lax.ppermute(value, ALL, sorted(pairs))  52.9 us
    ppermute x16, starting transfers between devices, hop(): return lax.ppermute(value, ALL, sorted(pairs))  29.2 us
    dot_general x13, matrix products, dot(): lax.dot_general(a, b, (((over_a,), (over_b,)), ((), ())), preferred_eleme...  19.3 us
    convert_element_type x6, other arithmetic, per_device(): arrived = lambda p: (p * one).astype(jnp.bfloat16)  7.48 us
    mul x1, other arithmetic, per_device(): shared = (kept + back) * GRAD_SCALE  5.44 us
    all_to_all x1, starting transfers between devices, exchange(): lax.all_to_all(value, ALL, 0, 0, tiled=True, axis_index_groups=groups)  3.59 us
    unnamed x40, local copies, waits for them, and re-layouts  3.35 us
  transfers between devices with their start and end apart: 20, of which 11 were waited for; matrix products, arithmetic and copies ran while one was open for 19% of the time, Pallas kernels for 0%

profile of v6, /device:TPU:8, one launch (start us, length us, event | category | flops | bytes accessed | tf_op | source)
XLA Modules:
  0.0 138.4 jit_solution(11850911320647291247)
XLA Ops:
  0.7 1.3 fusion.87
  2.6 0.7 select_compare_fusion
  3.3 6.7 %fusion.2 = f32[224,1024]{1,0:T(8,128)S(1)} fusion(bf16[224,4096]{1,0:T(8,128)(2,1)} %bitcast.117, bf16[1,1024,4096]{2,1,0:T(8,128)(2,1)} %param.5), kind=kOutput, calls=%fused_computation.2 | convolution fusion | flops 1879048192 | bytes 11141120 | tf_op jit(solution)/shard_map/dot_general | solution.py:38
  10.1 2.9 %multiply_convert_fusion.11 = (bf16[112,1024]{1,0:T(8,128)(2,1)S(1)}, bf16[112,1024]{1,0:T(8,128)(2,1)S(1)}) fusion(f32[224,1024]{1,0:T(8,128)S(1)} %fusion.2, bf16[112,4096]{1,0:T(8,128)(2,1)S(1)} %copy-done, bf16[1,1024,4096]{2,1,0:T(8,128)(2,1)S(1)} %copy-done.3, pred[1024]{0:T(1024)(128)(4,1)S(1)} %select_compare_fusion), kind=kOutput, calls=%fused_computation.92 | convolution fusion | flops 941129728 | bytes 10683392 | tf_op jit(solution)/shard_map/dot_general | solution.py:38
  13.1 2.3 %convert_select_fusion.1 = (f32[224,1024]{1,0:T(8,128)}, f32[224,1024]{1,0:T(8,128)}) fusion(pred[]{:T(512)S(6)} %eq.19, bf16[112,1024]{1,0:T(8,128)(2,1)S(1)} %get-tuple-element.31, bf16[112,1024]{1,0:T(8,128)(2,1)S(1)} %get-tuple-element.30, s32[1024]{0:T(1024)S(1)} %fusion.70), kind=kOutput, calls=%fused_computation.34 | convolution fusion | flops 473104384 | bytes 2297857 | tf_op jit(solution)/shard_map/dot_general | solution.py:38
  15.3 1.5 %dynamic-slice_convert_fusion.1 = (f32[112,2048]{1,0:T(8,128)}, f32[112,2048]{1,0:T(8,128)}) fusion(bf16[224,4096]{1,0:T(8,128)(2,1)S(1)} %bitcast.118, s32[]{:T(128)S(6)} %select_n.182, s32[]{:T(128)S(6)} %add.304), kind=kLoop, calls=%fused_computation.80 | loop fusion | flops 458752 | bytes 2752520 | tf_op jit(solution)/shard_map/convert_element_type | solution.py:59
  16.8 1.5 %collective-permute-start.3 = (f32[112,2048]{1,0:T(8,128)}, f32[112,2048]{1,0:T(8,128)}, u32[]{:S(2)}, u32[]{:S(2)}) collective-permute-start(f32[112,2048]{1,0:T(8,128)} %get-tuple-element.26), channel_id=1, source_target_pairs={{0,16},{1,65},{2,18},{3,67},{4,20},{5,69},{6,22},{7,71},{8,24},{9,... | collective-permute-start | bytes 2752520 | tf_op jit(solution)/shard_map/ppermute | solution.py:29
  18.3 1.7 %collective-permute-start.1 = (f32[112,2048]{1,0:T(8,128)}, f32[112,2048]{1,0:T(8,128)}, u32[]{:S(2)}, u32[]{:S(2)}) collective-permute-start(f32[112,2048]{1,0:T(8,128)} %get-tuple-element.26), channel_id=1, source_target_pairs={{0,48},{1,193},{2,50},{3,195},{4,52},{5,197},{6,54},{7,199},{8,56}... | collective-permute-start | bytes 2752520 | tf_op jit(solution)/shard_map/ppermute | solution.py:29
  20.3 3.0 %collective-permute-start.2 = (f32[112,2048]{1,0:T(8,128)}, f32[112,2048]{1,0:T(8,128)}, u32[]{:S(2)}, u32[]{:S(2)}) collective-permute-start(f32[112,2048]{1,0:T(8,128)} %get-tuple-element.27), channel_id=1, source_target_pairs={{0,48},{1,193},{2,50},{3,195},{4,52},{5,197},{6,54},{7,199},{8,56}... | collective-permute-start | bytes 2752520 | tf_op jit(solution)/shard_map/ppermute | solution.py:29
  24.0 1.4 fusion.83
  25.5 1.3 pad_maximum_fusion.1
  26.9 3.6 %all-to-all-start = ((f32[4,448,256]{2,1,0:T(8,128)}), f32[4,448,256]{2,1,0:T(8,128)S(1)}, u32[]{:S(2)}, u32[]{:S(2)}) async-start(f32[4,448,256]{2,1,0:T(8,128)} %pad_maximum_fusion.1), calls=%async_computation | async-start | bytes 3670016 | tf_op jit(solution)/shard_map/all_to_all | solution.py:34
  30.5 1.5 %collective-permute-done.1 = f32[112,2048]{1,0:T(8,128)} collective-permute-done((f32[112,2048]{1,0:T(8,128)}, f32[112,2048]{1,0:T(8,128)}, u32[]{:S(2)}, u32[]{:S(2)}) %collective-permute-start.1) | collective-permute-done | bytes 917536 | tf_op jit(solution)/shard_map/ppermute | solution.py:29
  32.0 3.0 %collective-permute-start.5 = (f32[112,2048]{1,0:T(8,128)}, f32[112,2048]{1,0:T(8,128)S(1)}, u32[]{:S(2)}, u32[]{:S(2)}) collective-permute-start(f32[112,2048]{1,0:T(8,128)} %collective-permute-done.1), channel_id=1, source_target_pairs={{0,48},{1,193},{2,50},{3,195},{4,52},{5,197},{6,54},{7,199},{8,56}... | collective-permute-start | bytes 2752520 | tf_op jit(solution)/shard_map/ppermute | solution.py:29
  35.0 6.6 %collective-permute-done.4 = f32[112,2048]{1,0:T(8,128)} collective-permute-done((f32[112,2048]{1,0:T(8,128)}, f32[112,2048]{1,0:T(8,128)}, u32[]{:S(2)}, u32[]{:S(2)}) %collective-permute-start.4) | collective-permute-done | bytes 917536 | tf_op jit(solution)/shard_map/ppermute | solution.py:29
  41.9 1.2 multiply_convert_fusion.5
  43.1 1.2 multiply_convert_fusion.2
  44.4 1.2 multiply_convert_fusion.3
  45.6 2.0 %multiply_convert_fusion.4 = bf16[112,2048]{1,0:T(8,128)(2,1)} fusion(f32[112,2048]{1,0:T(8,128)} %collective-permute-done.2, f32[]{:T(128)S(6)} %convert_element_type.52), kind=kLoop, calls=%fused_computation.53 | loop fusion | flops 458752 | bytes 1376260 | tf_op jit(solution)/shard_map/convert_element_type | solution.py:102
  47.7 13.8 %collective-permute-done.5 = f32[112,2048]{1,0:T(8,128)S(1)} collective-permute-done((f32[112,2048]{1,0:T(8,128)}, f32[112,2048]{1,0:T(8,128)S(1)}, u32[]{:S(2)}, u32[]{:S(2)}) %collective-permute-start.5) | collective-permute-done | bytes 917536 | tf_op jit(solution)/shard_map/ppermute | solution.py:29
  61.5 0.9 multiply_convert_fusion.1
  62.3 0.9 multiply_convert_fusion
  63.3 1.3 copy-done.6
  70.3 1.6 %collective-permute-start.7 = (f32[128,2048]{1,0:T(8,128)S(1)}, f32[128,2048]{1,0:T(8,128)S(1)}, u32[]{:S(2)}, u32[]{:S(2)}) collective-permute-start(f32[128,2048]{1,0:T(8,128)S(1)} %pad_maximum_fusion.2), channel_id=1, source_target_pairs={{0,192},{1,49},{2,194},{3,51},{4,196},{5,53},{6,198},{7,55},{8,200... | collective-permute-start | bytes 3145736 | tf_op jit(solution)/shard_map/ppermute | solution.py:29
  72.6 0.7 slice-done.3
  73.3 2.1 %fusion = f32[224,4096]{1,0:T(8,128)S(1)} fusion(bf16[1,1024,4096]{2,1,0:T(8,128)(2,1)S(1)} %bitcast.111, bf16[112,1024]{1,0:T(8,128)(2,1)S(1)} %copy-done.15, bf16[112,1024]{1,0:T(8,128)(2,1)S(1)} %get-tuple-element.30), kind=kOutput, calls=%fused_computation | convolution fusion | flops 1879965696 | bytes 12517376 | tf_op jit(solution)/shard_map/dot_general | solution.py:38
  75.5 9.7 %collective-permute-done.7 = f32[128,2048]{1,0:T(8,128)S(1)} collective-permute-done((f32[128,2048]{1,0:T(8,128)S(1)}, f32[128,2048]{1,0:T(8,128)S(1)}, u32[]{:S(2)}, u32[]{:S(2)}) %collective-permute-start.7) | collective-permute-done | bytes 1048608 | tf_op jit(solution)/shard_map/ppermute | solution.py:29
  85.2 0.9 slice_add_fusion.1
  86.1 0.7 collective-permute-done.8
  86.8 0.9 fusion.26
  87.8 0.8 collective-permute-start.9
  88.6 2.4 %collective-permute-start.10 = (f32[128,1024]{1,0:T(8,128)}, f32[128,1024]{1,0:T(8,128)}, u32[]{:S(2)}, u32[]{:S(2)}) collective-permute-start(f32[128,1024]{1,0:T(8,128)} %slice_add_fusion.1), channel_id=1, source_target_pairs={{0,192},{1,49},{2,194},{3,51},{4,196},{5,53},{6,198},{7,55},{8,200... | collective-permute-start | bytes 1572872 | tf_op jit(solution)/shard_map/ppermute | solution.py:29
  91.0 1.4 %fusion.4 = f32[112,4096]{1,0:T(8,128)S(1)} fusion(bf16[1,1024,4096]{2,1,0:T(8,128)(2,1)S(1)} %bitcast.109, f32[224,1024]{1,0:T(8,128)S(1)} %copy-done.13, pred[1024]{0:T(1024)(128)(4,1)S(1)} %select_compare_fusion), kind=kOutput, calls=%fused_computation.4 | convolution fusion | flops 940326912 | bytes 11142144 | tf_op jit(solution)/shard_map/dot_general | solution.py:38
  92.4 1.9 %broadcast_select_fusion = f32[336,2048]{1,0:T(8,128)} fusion(pred[]{:T(512)S(6)} %eq.19, f32[112,4096]{1,0:T(8,128)S(1)} %fusion.4, f32[224,4096]{1,0:T(8,128)S(1)} %fusion), kind=kLoop, calls=%fused_computation.23 | loop fusion | flops 2064384 | bytes 8257537 | tf_op jit(solution)/shard_map/jit(_where)/select_n | solution.py:99
  94.4 4.1 %collective-permute-done.9 = f32[128,1024]{1,0:T(8,128)} collective-permute-done((f32[128,1024]{1,0:T(8,128)}, f32[128,1024]{1,0:T(8,128)}, u32[]{:S(2)}, u32[]{:S(2)}) %collective-permute-start.9) | collective-permute-done | bytes 524320 | tf_op jit(solution)/shard_map/ppermute | solution.py:29
  98.6 1.8 %fusion.24 = (f32[128,1024]{1,0:T(8,128)S(1)}, f32[128,1024]{1,0:T(8,128)S(1)}) fusion(f32[128,1024]{1,0:T(8,128)} %collective-permute-done.9, f32[64,2048]{1,0:T(8,128)S(1)} %get-tuple-element.14, f32[64,2048]{1,0:T(8,128)S(1)} %get-tuple-element.18, f32[128,2048]{1,0:T(8,128)} %copy-done.10, f32[128,1024]{1,0:T(8,128)} %collective-permute-done.10, ...), kind=kLoop, calls=%fused_computation.62 | loop fusion | flops 786432 | bytes 4194304 | tf_op jit(solution)/shard_map/add | solution.py:125
  100.6 3.6 %collective-permute-start.11 = (f32[16,3072]{1,0:T(8,128)S(1)}, f32[16,3072]{1,0:T(8,128)S(1)}, u32[]{:S(2)}, u32[]{:S(2)}) collective-permute-start(f32[16,3072]{1,0:T(8,128)S(1)} %pad_maximum_fusion.16), channel_id=1, source_target_pairs={{0,4},{1,5},{2,6},{3,7},{4,8},{5,9},{6,10},{7,11},{8,12},{9,13},{1... | collective-permute-start | bytes 589832 | tf_op jit(solution)/shard_map/ppermute | solution.py:29
  104.2 3.1 %collective-permute-start.12 = (f32[16,3072]{1,0:T(8,128)S(1)}, f32[16,3072]{1,0:T(8,128)S(1)}, u32[]{:S(2)}, u32[]{:S(2)}) collective-permute-start(f32[16,3072]{1,0:T(8,128)S(1)} %pad_maximum_fusion.17), channel_id=1, source_target_pairs={{0,12},{1,13},{2,14},{3,15},{4,0},{5,1},{6,2},{7,3},{8,4},{9,5},{1... | collective-permute-start | bytes 589832 | tf_op jit(solution)/shard_map/ppermute | solution.py:29
  107.3 5.7 %collective-permute-done.11 = f32[16,3072]{1,0:T(8,128)S(1)} collective-permute-done((f32[16,3072]{1,0:T(8,128)S(1)}, f32[16,3072]{1,0:T(8,128)S(1)}, u32[]{:S(2)}, u32[]{:S(2)}) %collective-permute-start.11) | collective-permute-done | bytes 196640 | tf_op jit(solution)/shard_map/ppermute | solution.py:29
  113.1 3.9 %collective-permute-done.12 = f32[16,3072]{1,0:T(8,128)S(1)} collective-permute-done((f32[16,3072]{1,0:T(8,128)S(1)}, f32[16,3072]{1,0:T(8,128)S(1)}, u32[]{:S(2)}, u32[]{:S(2)}) %collective-permute-start.12) | collective-permute-done | bytes 196640 | tf_op jit(solution)/shard_map/ppermute | solution.py:29
  117.1 3.2 %collective-permute-start.14 = (f32[16,2048]{1,0:T(8,128)S(1)}, f32[16,2048]{1,0:T(8,128)S(1)}, u32[]{:S(2)}, u32[]{:S(2)}) collective-permute-start(f32[16,2048]{1,0:T(8,128)S(1)} %get-tuple-element.11), channel_id=1, source_target_pairs={{0,14},{1,15},{2,0},{3,1},{4,2},{5,3},{6,4},{7,5},{8,6},{9,7},{10,... | collective-permute-start | bytes 393224 | tf_op jit(solution)/shard_map/ppermute | solution.py:29
  120.4 2.5 %collective-permute-start.15 = (f32[16,2048]{1,0:T(8,128)S(1)}, f32[16,2048]{1,0:T(8,128)S(1)}, u32[]{:S(2)}, u32[]{:S(2)}) collective-permute-start(f32[16,2048]{1,0:T(8,128)S(1)} %pad_maximum_fusion.18), channel_id=1, source_target_pairs={{0,4},{1,5},{2,6},{3,7},{4,8},{5,9},{6,10},{7,11},{8,12},{9,13},{1... | collective-permute-start | bytes 393224 | tf_op jit(solution)/shard_map/ppermute | solution.py:29
  122.8 1.7 %collective-permute-start.16 = (f32[16,2048]{1,0:T(8,128)S(1)}, f32[16,2048]{1,0:T(8,128)S(1)}, u32[]{:S(2)}, u32[]{:S(2)}) collective-permute-start(f32[16,2048]{1,0:T(8,128)S(1)} %pad_maximum_fusion.19), channel_id=1, source_target_pairs={{0,12},{1,13},{2,14},{3,15},{4,0},{5,1},{6,2},{7,3},{8,4},{9,5},{1... | collective-permute-start | bytes 393224 | tf_op jit(solution)/shard_map/ppermute | solution.py:29
  124.5 3.1 %collective-permute-done.15 = f32[16,2048]{1,0:T(8,128)S(1)} collective-permute-done((f32[16,2048]{1,0:T(8,128)S(1)}, f32[16,2048]{1,0:T(8,128)S(1)}, u32[]{:S(2)}, u32[]{:S(2)}) %collective-permute-start.15) | collective-permute-done | bytes 131104 | tf_op jit(solution)/shard_map/ppermute | solution.py:29
  127.6 3.6 %collective-permute-done.16 = f32[16,2048]{1,0:T(8,128)S(1)} collective-permute-done((f32[16,2048]{1,0:T(8,128)S(1)}, f32[16,2048]{1,0:T(8,128)S(1)}, u32[]{:S(2)}, u32[]{:S(2)}) %collective-permute-start.16) | collective-permute-done | bytes 131104 | tf_op jit(solution)/shard_map/ppermute | solution.py:29
  131.2 0.9 fusion.35
  132.3 5.4 %add_multiply_fusion = f32[336,2048]{1,0:T(8,128)} fusion(f32[336,2048]{1,0:T(8,128)} %collective-permute-done.18, pred[]{:T(512)S(6)} %eq.19, f32[112,4096]{1,0:T(8,128)S(1)} %fusion.4, f32[224,4096]{1,0:T(8,128)} %copy-done.2), kind=kLoop, calls=%fused_computation.14 | loop fusion | flops 3440640 | bytes 11010049 | tf_op jit(solution)/shard_map/mul | solution.py:150
  137.7 0.7 maximum_bitcast_fusion.4
  (88 shorter events, 7.8 us)
Async XLA Ops:
  0.6 9.4 %copy-start = (bf16[112,4096]{1,0:T(8,128)(2,1)S(1)}, bf16[112,4096]{1,0:T(8,128)(2,1)}, u32[]{:S(2)}) copy-start(bf16[112,4096]{1,0:T(8,128)(2,1)} %param.9) | copy-start | bytes 2752516
  3.3 6.8 %copy-start.3 = (bf16[1,1024,4096]{2,1,0:T(8,128)(2,1)S(1)}, bf16[1,1024,4096]{2,1,0:T(8,128)(2,1)}, u32[]{:S(2)}) copy-start(bf16[1,1024,4096]{2,1,0:T(8,128)(2,1)} %param.6) | copy-start | bytes 25165828
  10.1 2.9 %copy-start.12 = (f32[224,1024]{1,0:T(8,128)}, f32[224,1024]{1,0:T(8,128)S(1)}, u32[]{:S(2)}) copy-start(f32[224,1024]{1,0:T(8,128)S(1)} %fusion.2) | copy-start | bytes 2752516
  13.0 2.3 %copy-start.14 = (bf16[112,1024]{1,0:T(8,128)(2,1)}, bf16[112,1024]{1,0:T(8,128)(2,1)S(1)}, u32[]{:S(2)}) copy-start(bf16[112,1024]{1,0:T(8,128)(2,1)S(1)} %get-tuple-element.31) | copy-start | bytes 688132
  13.0 2.3 %copy-start.5 = (bf16[4096,2,112]{0,2,1:T(8,128)(2,1)S(1)}, bf16[4096,2,112]{0,2,1:T(8,128)(2,1)}, u32[]{:S(2)}) copy-start(bf16[4096,2,112]{0,2,1:T(8,128)(2,1)} %param.8) | copy-start | bytes 5505028
  15.3 10.0 %collective-permute-start = (f32[224,1024]{1,0:T(8,128)}, f32[224,1024]{1,0:T(8,128)S(1)}, u32[]{:S(2)}, u32[]{:S(2)}) collective-permute-start(f32[224,1024]{1,0:T(8,128)} %get-tuple-element.29), channel_id=1, source_target_pairs={{0,1},{1,0},{2,3},{3,2},{4,5},{5,4},{6,7},{7,6},{8,9},{9,8},{10,11... | collective-permute-start | bytes 2752520 | tf_op jit(solution)/shard_map/ppermute | solution.py:87
  16.8 27.5 %collective-permute-start.3 = (f32[112,2048]{1,0:T(8,128)}, f32[112,2048]{1,0:T(8,128)}, u32[]{:S(2)}, u32[]{:S(2)}) collective-permute-start(f32[112,2048]{1,0:T(8,128)} %get-tuple-element.26), channel_id=1, source_target_pairs={{0,16},{1,65},{2,18},{3,67},{4,20},{5,69},{6,22},{7,71},{8,24},{9,... | collective-permute-start | bytes 2752520 | tf_op jit(solution)/shard_map/ppermute | solution.py:29
  18.3 13.7 %collective-permute-start.1 = (f32[112,2048]{1,0:T(8,128)}, f32[112,2048]{1,0:T(8,128)}, u32[]{:S(2)}, u32[]{:S(2)}) collective-permute-start(f32[112,2048]{1,0:T(8,128)} %get-tuple-element.26), channel_id=1, source_target_pairs={{0,48},{1,193},{2,50},{3,195},{4,52},{5,197},{6,54},{7,199},{8,56}... | collective-permute-start | bytes 2752520 | tf_op jit(solution)/shard_map/ppermute | solution.py:29
  20.1 21.5 %collective-permute-start.4 = (f32[112,2048]{1,0:T(8,128)}, f32[112,2048]{1,0:T(8,128)}, u32[]{:S(2)}, u32[]{:S(2)}) collective-permute-start(f32[112,2048]{1,0:T(8,128)} %get-tuple-element.27), channel_id=1, source_target_pairs={{0,16},{1,65},{2,18},{3,67},{4,20},{5,69},{6,22},{7,71},{8,24},{9,... | collective-permute-start | bytes 2752520 | tf_op jit(solution)/shard_map/ppermute | solution.py:29
  20.3 25.3 %collective-permute-start.2 = (f32[112,2048]{1,0:T(8,128)}, f32[112,2048]{1,0:T(8,128)}, u32[]{:S(2)}, u32[]{:S(2)}) collective-permute-start(f32[112,2048]{1,0:T(8,128)} %get-tuple-element.27), channel_id=1, source_target_pairs={{0,48},{1,193},{2,50},{3,195},{4,52},{5,197},{6,54},{7,199},{8,56}... | collective-permute-start | bytes 2752520 | tf_op jit(solution)/shard_map/ppermute | solution.py:29
  26.9 36.3 %all-to-all-start = ((f32[4,448,256]{2,1,0:T(8,128)}), f32[4,448,256]{2,1,0:T(8,128)S(1)}, u32[]{:S(2)}, u32[]{:S(2)}) async-start(f32[4,448,256]{2,1,0:T(8,128)} %pad_maximum_fusion.1), calls=%async_computation | async-start | bytes 3670016 | tf_op jit(solution)/shard_map/all_to_all | solution.py:34
  32.0 29.4 %collective-permute-start.5 = (f32[112,2048]{1,0:T(8,128)}, f32[112,2048]{1,0:T(8,128)S(1)}, u32[]{:S(2)}, u32[]{:S(2)}) collective-permute-start(f32[112,2048]{1,0:T(8,128)} %collective-permute-done.1), channel_id=1, source_target_pairs={{0,48},{1,193},{2,50},{3,195},{4,52},{5,197},{6,54},{7,199},{8,56}... | collective-permute-start | bytes 2752520 | tf_op jit(solution)/shard_map/ppermute | solution.py:29
  41.6 20.8 %collective-permute-start.6 = (f32[112,2048]{1,0:T(8,128)}, f32[112,2048]{1,0:T(8,128)S(1)}, u32[]{:S(2)}, u32[]{:S(2)}) collective-permute-start(f32[112,2048]{1,0:T(8,128)} %collective-permute-done.4), channel_id=1, source_target_pairs={{0,16},{1,65},{2,18},{3,67},{4,20},{5,69},{6,22},{7,71},{8,24},{9,... | collective-permute-start | bytes 2752520 | tf_op jit(solution)/shard_map/ppermute | solution.py:29
  63.2 1.5 %copy-start.6 = (bf16[4096,2,112]{0,2,1:T(8,128)(2,1)S(1)}, bf16[4096,2,112]{0,2,1:T(8,128)(2,1)}, u32[]{:S(2)}) copy-start(bf16[4096,2,112]{0,2,1:T(8,128)(2,1)} %param.8) | copy-start | bytes 5505028
  65.2 1.0 copy-start.9
  67.6 1.0 copy-start.7
  67.6 1.1 copy-start.8
  69.7 2.8 %slice-start.2 = ((s8[8388608]{0:T(1024)(128)(4,1)}), s8[4194304]{0:T(1024)(128)(4,1)S(1)}, s32[]{:S(2)}) async-start(s8[8388608]{0:T(1024)(128)(4,1)} %bitcast.110), calls=%async_computation.3 | async-start | bytes 8388608
  70.1 3.2 %slice-start.3 = ((s8[8388608]{0:T(1024)(128)(4,1)}), s8[4194304]{0:T(1024)(128)(4,1)S(1)}, s32[]{:S(2)}) async-start(s8[8388608]{0:T(1024)(128)(4,1)} %bitcast.110), calls=%async_computation.4 | async-start | bytes 8388608
  70.3 3.0 %copy-start.15 = (bf16[112,1024]{1,0:T(8,128)(2,1)S(1)}, bf16[112,1024]{1,0:T(8,128)(2,1)}, u32[]{:S(2)}) copy-start(bf16[112,1024]{1,0:T(8,128)(2,1)} %copy-done.14) | copy-start | bytes 688132
  70.3 14.9 %collective-permute-start.7 = (f32[128,2048]{1,0:T(8,128)S(1)}, f32[128,2048]{1,0:T(8,128)S(1)}, u32[]{:S(2)}, u32[]{:S(2)}) collective-permute-start(f32[128,2048]{1,0:T(8,128)S(1)} %pad_maximum_fusion.2), channel_id=1, source_target_pairs={{0,192},{1,49},{2,194},{3,51},{4,196},{5,53},{6,198},{7,55},{8,200... | collective-permute-start | bytes 3145736 | tf_op jit(solution)/shard_map/ppermute | solution.py:29
  71.9 19.1 %slice-start = ((s8[8388608]{0:T(1024)(128)(4,1)}), s8[4194304]{0:T(1024)(128)(4,1)S(1)}, s32[]{:S(2)}) async-start(s8[8388608]{0:T(1024)(128)(4,1)} %bitcast.108), calls=%async_computation.1 | async-start | bytes 8388608
  72.0 19.0 %slice-start.1 = ((s8[8388608]{0:T(1024)(128)(4,1)}), s8[4194304]{0:T(1024)(128)(4,1)S(1)}, s32[]{:S(2)}) async-start(s8[8388608]{0:T(1024)(128)(4,1)} %bitcast.108), calls=%async_computation.2 | async-start | bytes 8388608
  72.0 14.9 %collective-permute-start.8 = (f32[128,2048]{1,0:T(8,128)S(1)}, f32[128,2048]{1,0:T(8,128)S(1)}, u32[]{:S(2)}, u32[]{:S(2)}) collective-permute-start(f32[128,2048]{1,0:T(8,128)S(1)} %fusion.15), channel_id=1, source_target_pairs={{0,64},{1,17},{2,66},{3,19},{4,68},{5,21},{6,70},{7,23},{8,72},{9,... | collective-permute-start | bytes 3145736 | tf_op jit(solution)/shard_map/ppermute | solution.py:29
  75.4 17.0 %copy-start.2 = (f32[224,4096]{1,0:T(8,128)}, f32[224,4096]{1,0:T(8,128)S(1)}, u32[]{:S(2)}) copy-start(f32[224,4096]{1,0:T(8,128)S(1)} %fusion) | copy-start | bytes 11010052
  75.5 15.5 %copy-start.13 = (f32[224,1024]{1,0:T(8,128)S(1)}, f32[224,1024]{1,0:T(8,128)}, u32[]{:S(2)}) copy-start(f32[224,1024]{1,0:T(8,128)} %copy-done.12) | copy-start | bytes 2752516
  85.2 7.2 %copy-start.10 = (f32[128,2048]{1,0:T(8,128)}, f32[128,2048]{1,0:T(8,128)S(1)}, u32[]{:S(2)}) copy-start(f32[128,2048]{1,0:T(8,128)S(1)} %collective-permute-done.7) | copy-start | bytes 3145732
  86.8 5.6 %copy-start.11 = (f32[128,2048]{1,0:T(8,128)}, f32[128,2048]{1,0:T(8,128)S(1)}, u32[]{:S(2)}) copy-start(f32[128,2048]{1,0:T(8,128)S(1)} %collective-permute-done.8) | copy-start | bytes 3145732
  87.8 10.7 %collective-permute-start.9 = (f32[128,1024]{1,0:T(8,128)}, f32[128,1024]{1,0:T(8,128)}, u32[]{:S(2)}, u32[]{:S(2)}) collective-permute-start(f32[128,1024]{1,0:T(8,128)} %fusion.26), channel_id=1, source_target_pairs={{0,64},{1,17},{2,66},{3,19},{4,68},{5,21},{6,70},{7,23},{8,72},{9,... | collective-permute-start | bytes 1572872 | tf_op jit(solution)/shard_map/ppermute | solution.py:29
  88.6 10.0 %collective-permute-start.10 = (f32[128,1024]{1,0:T(8,128)}, f32[128,1024]{1,0:T(8,128)}, u32[]{:S(2)}, u32[]{:S(2)}) collective-permute-start(f32[128,1024]{1,0:T(8,128)} %slice_add_fusion.1), channel_id=1, source_target_pairs={{0,192},{1,49},{2,194},{3,51},{4,196},{5,53},{6,198},{7,55},{8,200... | collective-permute-start | bytes 1572872 | tf_op jit(solution)/shard_map/ppermute | solution.py:29
  94.4 37.9 %collective-permute-start.18 = (f32[336,2048]{1,0:T(8,128)}, f32[336,2048]{1,0:T(8,128)}, u32[]{:S(2)}, u32[]{:S(2)}) collective-permute-start(f32[336,2048]{1,0:T(8,128)} %broadcast_select_fusion), channel_id=1, source_target_pairs={{0,1},{1,0},{2,3},{3,2},{4,5},{5,4},{6,7},{7,6},{8,9},{9,8},{10,11... | collective-permute-start | bytes 8257544 | tf_op jit(solution)/shard_map/ppermute | solution.py:100
  100.5 16.6 %copy-start.4 = (f32[128,2048]{1,0:T(8,128)}, f32[128,2048]{1,0:T(8,128)S(1)}, u32[]{:S(2)}) copy-start(f32[128,2048]{1,0:T(8,128)S(1)} %pad_maximum_fusion.3) | copy-start | bytes 3145732
  100.6 12.4 %collective-permute-start.11 = (f32[16,3072]{1,0:T(8,128)S(1)}, f32[16,3072]{1,0:T(8,128)S(1)}, u32[]{:S(2)}, u32[]{:S(2)}) collective-permute-start(f32[16,3072]{1,0:T(8,128)S(1)} %pad_maximum_fusion.16), channel_id=1, source_target_pairs={{0,4},{1,5},{2,6},{3,7},{4,8},{5,9},{6,10},{7,11},{8,12},{9,13},{1... | collective-permute-start | bytes 589832 | tf_op jit(solution)/shard_map/ppermute | solution.py:29
  104.2 12.8 %collective-permute-start.12 = (f32[16,3072]{1,0:T(8,128)S(1)}, f32[16,3072]{1,0:T(8,128)S(1)}, u32[]{:S(2)}, u32[]{:S(2)}) collective-permute-start(f32[16,3072]{1,0:T(8,128)S(1)} %pad_maximum_fusion.17), channel_id=1, source_target_pairs={{0,12},{1,13},{2,14},{3,15},{4,0},{5,1},{6,2},{7,3},{8,4},{9,5},{1... | collective-permute-start | bytes 589832 | tf_op jit(solution)/shard_map/ppermute | solution.py:29
  117.0 7.5 %collective-permute-start.13 = (f32[16,2048]{1,0:T(8,128)S(1)}, f32[16,2048]{1,0:T(8,128)S(1)}, u32[]{:S(2)}, u32[]{:S(2)}) collective-permute-start(f32[16,2048]{1,0:T(8,128)S(1)} %get-tuple-element.10), channel_id=1, source_target_pairs={{0,2},{1,3},{2,4},{3,5},{4,6},{5,7},{6,8},{7,9},{8,10},{9,11},{10,... | collective-permute-start | bytes 393224 | tf_op jit(solution)/shard_map/ppermute | solution.py:29
  117.1 7.4 %collective-permute-start.14 = (f32[16,2048]{1,0:T(8,128)S(1)}, f32[16,2048]{1,0:T(8,128)S(1)}, u32[]{:S(2)}, u32[]{:S(2)}) collective-permute-start(f32[16,2048]{1,0:T(8,128)S(1)} %get-tuple-element.11), channel_id=1, source_target_pairs={{0,14},{1,15},{2,0},{3,1},{4,2},{5,3},{6,4},{7,5},{8,6},{9,7},{10,... | collective-permute-start | bytes 393224 | tf_op jit(solution)/shard_map/ppermute | solution.py:29
  120.4 7.3 %collective-permute-start.15 = (f32[16,2048]{1,0:T(8,128)S(1)}, f32[16,2048]{1,0:T(8,128)S(1)}, u32[]{:S(2)}, u32[]{:S(2)}) collective-permute-start(f32[16,2048]{1,0:T(8,128)S(1)} %pad_maximum_fusion.18), channel_id=1, source_target_pairs={{0,4},{1,5},{2,6},{3,7},{4,8},{5,9},{6,10},{7,11},{8,12},{9,13},{1... | collective-permute-start | bytes 393224 | tf_op jit(solution)/shard_map/ppermute | solution.py:29
  122.8 8.4 %collective-permute-start.16 = (f32[16,2048]{1,0:T(8,128)S(1)}, f32[16,2048]{1,0:T(8,128)S(1)}, u32[]{:S(2)}, u32[]{:S(2)}) collective-permute-start(f32[16,2048]{1,0:T(8,128)S(1)} %pad_maximum_fusion.19), channel_id=1, source_target_pairs={{0,12},{1,13},{2,14},{3,15},{4,0},{5,1},{6,2},{7,3},{8,4},{9,5},{1... | collective-permute-start | bytes 393224 | tf_op jit(solution)/shard_map/ppermute | solution.py:29
  132.1 5.6 %collective-permute-start.17 = (f32[8,2048]{1,0:T(8,128)S(1)}, f32[8,2048]{1,0:T(8,128)S(1)}, u32[]{:S(2)}, u32[]{:S(2)}) collective-permute-start(f32[8,2048]{1,0:T(8,128)S(1)} %dynamic-slice_bitcast_fusion.13), channel_id=1, source_target_pairs={{0,1},{1,0},{2,3},{3,2},{4,5},{5,4},{6,7},{7,6},{8,9},{9,8},{10,11... | collective-permute-start | bytes 196616 | tf_op jit(solution)/shard_map/ppermute | solution.py:146
  132.2 6.1 %copy-start.1 = (bf16[112,4096]{1,0:T(8,128)(2,1)S(1)}, bf16[112,4096]{1,0:T(8,128)(2,1)}, u32[]{:S(2)}) copy-start(bf16[112,4096]{1,0:T(8,128)(2,1)} %param.9) | copy-start | bytes 2752516

commit v7 on v6

--- a/solution.py
+++ b/solution.py
@@ -112,21 +112,23 @@
         partial = partial + dot(d[3], w_3, 0, 0) + dot(d[2], w_2, 0, 0)
         return partial.reshape(4, rows // 16, half)
 
-    products = [product(r) for r in range(nr)]
-    mine, b1, b2, b3 = (
-        jnp.concatenate([lax.dynamic_index_in_dim(p, (across + k) & 3, 0, False) for p in products])
-        for k in range(4)
+    parts = []
+    for r in range(nr):
+        p = product(r)
+        mine, b1, b2, b3 = (lax.dynamic_index_in_dim(p, (across + k) & 3, 0, False) for k in range(4))
+        r1 = hop(jnp.concatenate([b2[:, :cut], b1[:, cut:]], axis=1), dims, SECOND, 1)
+        r2 = hop(jnp.concatenate([b3[:, :cut], b2[:, cut:]], axis=1), dims, SECOND, -1)
+        up, down = b1[:, :cut] + r1[:, :cut], b3[:, cut:] + r2[:, cut:]
+        up, down = lax.optimization_barrier((up, down))
+        t1 = hop(up, dims, SECOND, 1)
+        t2 = hop(down, dims, SECOND, -1)
+        left = mine[:, :cut] + r2[:, :cut] + t1
+        right = mine[:, cut:] + r1[:, cut:] + t2
+        parts.append(jnp.concatenate([left, right], axis=1).reshape(nz, own_rows, half))
+    iz = lax.axis_index("dp_2")
+    at_z = lambda k: jnp.concatenate(
+        [lax.dynamic_index_in_dim(part, (iz + k) & 7, 0, False) for part in parts]
     )
-    r1 = hop(jnp.concatenate([b2[:, :cut], b1[:, cut:]], axis=1), dims, SECOND, 1)
-    r2 = hop(jnp.concatenate([b3[:, :cut], b2[:, cut:]], axis=1), dims, SECOND, -1)
-    up_2, down_2 = lax.optimization_barrier((b1[:, :cut] + r1[:, :cut], b3[:, cut:] + r2[:, cut:]))
-    t1 = hop(up_2, dims, SECOND, 1)
-    t2 = hop(down_2, dims, SECOND, -1)
-    left = mine[:, :cut] + r2[:, :cut] + t1
-    right = mine[:, cut:] + r1[:, cut:] + t2
-    part = jnp.concatenate([left, right], axis=1).reshape(nr, nz, own_rows, half)
-    iz = lax.axis_index("dp_2")
-    at_z = lambda k: lax.dynamic_index_in_dim(part, (iz + k) & 7, 1, False).reshape(-1, half)
     b0, b1, b2, b3, b4, b5, b6, b7 = (at_z(k) for k in range(nz))
     along = (2, 2)
     ru = hop(jnp.concatenate([b3, b4[:, :cut]], axis=1), dims, along, 2)
@@ -134,9 +136,8 @@
     near_up, near_down = b1 + ru[:, :half], b7 + rd[:, :half]
     far_up_sum = jnp.concatenate([b2[:, :cut] + ru[:, half:], b2[:, cut:]], axis=1)
     far_down_sum = jnp.concatenate([b6[:, :cut], b6[:, cut:] + rd[:, half:]], axis=1)
-    near_up, near_down, far_up_sum, far_down_sum = lax.optimization_barrier(
-        (near_up, near_down, far_up_sum, far_down_sum)
-    )
+    near_up, far_up_sum = lax.optimization_barrier((near_up, far_up_sum))
+    near_down, far_down_sum = lax.optimization_barrier((near_down, far_down_sum))
     s2 = hop(far_up_sum, dims, along, 2)
     s6 = hop(far_down_sum, dims, along, -2)
     s1 = hop(near_up, dims, along, 1)

time: 141 us -> 136 us (0.965)
  the two profiles are of different devices: /device:TPU:8 before, /device:TPU:1 now
where the time goes in v7:
time: 136 us
  starting transfers between devices  44.8 us (33%)
  waiting for transfers between devices  35.1 us (26%)
  matrix products  27.4 us (20%)
  other arithmetic  22.9 us (17%)
  local copies, waits for them, and re-layouts  2.81 us (2%)
  between operations  2.46 us (2%)
    ppermute x20, waiting for transfers between devices, hop(): return lax.ppermute(value, ALL, sorted(pairs))  35.1 us
    ppermute x20, starting transfers between devices, hop(): return lax.ppermute(value, ALL, sorted(pairs))  33.3 us
    dot_general x13, matrix products, dot(): lax.dot_general(a, b, (((over_a,), (over_b,)), ((), ())), preferred_eleme...  27.4 us
    convert_element_type x6, other arithmetic, per_device(): arrived = lambda p: (p * one).astype(jnp.bfloat16)  7.46 us
    mul x1, other arithmetic, per_device(): shared = (kept + back) * GRAD_SCALE  5.44 us
    all_to_all x1, starting transfers between devices, exchange(): lax.all_to_all(value, ALL, 0, 0, tiled=True, axis_index_groups=groups)  4.38 us
    ppermute x1, starting transfers between devices, per_device(): lax.ppermute(lax.dynamic_index_in_dim(total, 1 - rep, 0, False), 'rep', S...  3.66 us
    ppermute x1, starting transfers between devices, per_device(): theirs = lax.ppermute(away, 'rep', SWAP)  3.43 us
  transfers between devices with their start and end apart: 24, of which 9 were waited for; matrix products, arithmetic and copies ran while one was open for 36% of the time, Pallas kernels for 0%

profile of v7, /device:TPU:1, one launch (start us, length us, event | category | flops | bytes accessed | tf_op | source)
XLA Modules:
  0.0 135.5 jit_solution(7832176714183278695)
XLA Ops:
  0.7 2.8 %dynamic-slice_convert_fusion.1 = (f32[112,2048]{1,0:T(8,128)}, f32[112,2048]{1,0:T(8,128)}) fusion(bf16[224,4096]{1,0:T(8,128)(2,1)} %bitcast.121, s32[]{:T(128)S(6)} %select_n.190, s32[]{:T(128)S(6)} %add.343), kind=kLoop, calls=%fused_computation.55 | loop fusion | flops 458752 | bytes 2752520 | tf_op jit(solution)/shard_map/convert_element_type | solution.py:59
  3.5 2.1 %collective-permute-start.3 = (f32[112,2048]{1,0:T(8,128)}, f32[112,2048]{1,0:T(8,128)}, u32[]{:S(2)}, u32[]{:S(2)}) collective-permute-start(f32[112,2048]{1,0:T(8,128)} %get-tuple-element.30), channel_id=1, source_target_pairs={{0,16},{1,65},{2,18},{3,67},{4,20},{5,69},{6,22},{7,71},{8,24},{9,... | collective-permute-start | bytes 2752520 | tf_op jit(solution)/shard_map/ppermute | solution.py:29
  5.6 1.4 %collective-permute-start.1 = (f32[112,2048]{1,0:T(8,128)}, f32[112,2048]{1,0:T(8,128)}, u32[]{:S(2)}, u32[]{:S(2)}) collective-permute-start(f32[112,2048]{1,0:T(8,128)} %get-tuple-element.30), channel_id=1, source_target_pairs={{0,48},{1,193},{2,50},{3,195},{4,52},{5,197},{6,54},{7,199},{8,56}... | collective-permute-start | bytes 2752520 | tf_op jit(solution)/shard_map/ppermute | solution.py:29
  7.1 2.7 %collective-permute-start.2 = (f32[112,2048]{1,0:T(8,128)}, f32[112,2048]{1,0:T(8,128)}, u32[]{:S(2)}, u32[]{:S(2)}) collective-permute-start(f32[112,2048]{1,0:T(8,128)} %get-tuple-element.31), channel_id=1, source_target_pairs={{0,48},{1,193},{2,50},{3,195},{4,52},{5,197},{6,54},{7,199},{8,56}... | collective-permute-start | bytes 2752520 | tf_op jit(solution)/shard_map/ppermute | solution.py:29
  9.7 0.6 fusion.87
  10.3 6.1 %fusion.2 = f32[224,1024]{1,0:T(8,128)S(1)} fusion(bf16[224,4096]{1,0:T(8,128)(2,1)S(1)} %bitcast.122, bf16[1,1024,4096]{2,1,0:T(8,128)(2,1)} %param.5), kind=kOutput, calls=%fused_computation.2 | convolution fusion | flops 1879048192 | bytes 11141120 | tf_op jit(solution)/shard_map/dot_general | solution.py:38
  17.1 0.7 select_compare_fusion
  17.8 2.9 %multiply_convert_fusion.11 = (bf16[112,1024]{1,0:T(8,128)(2,1)S(1)}, bf16[112,1024]{1,0:T(8,128)(2,1)S(1)}) fusion(f32[224,1024]{1,0:T(8,128)S(1)} %fusion.2, bf16[112,4096]{1,0:T(8,128)(2,1)S(1)} %copy-done, bf16[1,1024,4096]{2,1,0:T(8,128)(2,1)S(1)} %copy-done.3, pred[1024]{0:T(1024)(128)(4,1)S(1)} %select_compare_fusion), kind=kOutput, calls=%fused_computation.67 | convolution fusion | flops 941129728 | bytes 10683392 | tf_op jit(solution)/shard_map/dot_general | solution.py:38
  20.7 2.3 %convert_select_fusion.1 = (f32[224,1024]{1,0:T(8,128)}, f32[224,1024]{1,0:T(8,128)}) fusion(pred[]{:T(512)S(6)} %eq.19, bf16[112,1024]{1,0:T(8,128)(2,1)S(1)} %get-tuple-element.35, bf16[112,1024]{1,0:T(8,128)(2,1)S(1)} %get-tuple-element.34, s32[1024]{0:T(1024)S(1)} %fusion.70), kind=kOutput, calls=%fused_computation.26 | convolution fusion | flops 473104384 | bytes 2297857 | tf_op jit(solution)/shard_map/dot_general | solution.py:38
  23.0 3.4 %collective-permute-start = (f32[224,1024]{1,0:T(8,128)}, f32[224,1024]{1,0:T(8,128)S(1)}, u32[]{:S(2)}, u32[]{:S(2)}) collective-permute-start(f32[224,1024]{1,0:T(8,128)} %get-tuple-element.33), channel_id=1, source_target_pairs={{0,1},{1,0},{2,3},{3,2},{4,5},{5,4},{6,7},{7,6},{8,9},{9,8},{10,11... | collective-permute-start | bytes 2752520 | tf_op jit(solution)/shard_map/ppermute | solution.py:87
  27.1 7.2 %fusion = f32[224,4096]{1,0:T(8,128)} fusion(bf16[1,1024,4096]{2,1,0:T(8,128)(2,1)} %param.5, bf16[112,1024]{1,0:T(8,128)(2,1)S(1)} %get-tuple-element.35, bf16[112,1024]{1,0:T(8,128)(2,1)S(1)} %get-tuple-element.34), kind=kOutput, calls=%fused_computation | convolution fusion | flops 1879965696 | bytes 12517376 | tf_op jit(solution)/shard_map/dot_general | solution.py:38
  34.3 5.1 %fusion.4 = f32[112,4096]{1,0:T(8,128)S(1)} fusion(bf16[1,1024,4096]{2,1,0:T(8,128)(2,1)} %param.6, f32[224,1024]{1,0:T(8,128)} %copy-done.10, pred[1024]{0:T(1024)(128)(4,1)S(1)} %select_compare_fusion), kind=kOutput, calls=%fused_computation.4 | convolution fusion | flops 940326912 | bytes 11142144 | tf_op jit(solution)/shard_map/dot_general | solution.py:38
  39.4 1.9 %broadcast_select_fusion = f32[336,2048]{1,0:T(8,128)} fusion(pred[]{:T(512)S(6)} %eq.19, f32[112,4096]{1,0:T(8,128)S(1)} %fusion.4, f32[224,4096]{1,0:T(8,128)S(1)} %copy-done.2), kind=kLoop, calls=%fused_computation.23 | loop fusion | flops 2064384 | bytes 8257537 | tf_op jit(solution)/shard_map/jit(_where)/select_n | solution.py:99
  41.8 1.4 %pad_maximum_fusion.1 = f32[4,448,256]{2,1,0:T(8,128)} fusion(f32[1,448,256]{2,1,0:T(8,128)S(1)} %get-tuple-element.77, f32[1,448,256]{2,1,0:T(8,128)S(1)} %get-tuple-element.76, f32[1,448,256]{2,1,0:T(8,128)S(1)} %get-tuple-element.75, f32[1,448,256]{2,1,0:T(8,128)S(1)} %get-tuple-element.74), kind=kLoop, calls=%fused_computation.22 | loop fusion | flops 1376256 | bytes 3670016 | tf_op jit(solution)/shard_map/stack | solution.py:91
  43.2 4.4 %all-to-all-start = ((f32[4,448,256]{2,1,0:T(8,128)}), f32[4,448,256]{2,1,0:T(8,128)}, u32[]{:S(2)}, u32[]{:S(2)}) async-start(f32[4,448,256]{2,1,0:T(8,128)} %pad_maximum_fusion.1), calls=%async_computation | async-start | bytes 3670016 | tf_op jit(solution)/shard_map/all_to_all | solution.py:34
  47.6 2.6 %collective-permute-start.5 = (f32[112,2048]{1,0:T(8,128)}, f32[112,2048]{1,0:T(8,128)S(1)}, u32[]{:S(2)}, u32[]{:S(2)}) collective-permute-start(f32[112,2048]{1,0:T(8,128)} %collective-permute-done.1), channel_id=1, source_target_pairs={{0,48},{1,193},{2,50},{3,195},{4,52},{5,197},{6,54},{7,199},{8,56}... | collective-permute-start | bytes 2752520 | tf_op jit(solution)/shard_map/ppermute | solution.py:29
  50.2 1.3 multiply_convert_fusion.5
  51.5 1.2 multiply_convert_fusion.2
  52.7 1.2 multiply_convert_fusion.3
  54.0 2.0 %multiply_convert_fusion.4 = bf16[112,2048]{1,0:T(8,128)(2,1)} fusion(f32[112,2048]{1,0:T(8,128)} %collective-permute-done.2, f32[]{:T(128)S(6)} %convert_element_type.52), kind=kLoop, calls=%fused_computation.34 | loop fusion | flops 458752 | bytes 1376260 | tf_op jit(solution)/shard_map/convert_element_type | solution.py:102
  56.0 14.1 %collective-permute-done.5 = f32[112,2048]{1,0:T(8,128)S(1)} collective-permute-done((f32[112,2048]{1,0:T(8,128)}, f32[112,2048]{1,0:T(8,128)S(1)}, u32[]{:S(2)}, u32[]{:S(2)}) %collective-permute-start.5) | collective-permute-done | bytes 917536 | tf_op jit(solution)/shard_map/ppermute | solution.py:29
  70.1 0.8 multiply_convert_fusion.1
  71.3 0.8 multiply_convert_fusion
  72.1 1.7 %multiply_convert_fusion.6 = (bf16[1,448,256]{2,1,0:T(8,128)(2,1)S(1)}, bf16[1,448,256]{2,1,0:T(8,128)(2,1)S(1)}, bf16[1,448,256]{2,1,0:T(8,128)(2,1)S(1)}, bf16[1,448,256]{2,1,0:T(8,128)(2,1)S(1)}) fusion(f32[4,448,256]{2,1,0:T(8,128)} %all-to-all-done, s32[]{:T(128)S(6)} %select_n.193, f32[]{:T(128)S(6)} %convert_element_type.52, s32[]{:T(128)S(6)} %select_n.192, ...), kind=kLoop, calls=%fused_computation.62 | loop fusion | flops 917504 | bytes 2752532 | tf_op jit(solution)/shard_map/convert_element_type | solution.py:93
  75.0 0.5 convolution_add_fusion.2
  75.5 0.5 convolution_add_fusion.1
  75.9 0.5 copy-done.6
  77.6 2.7 %collective-permute-start.11 = (f32[64,2048]{1,0:T(8,128)S(1)}, f32[64,2048]{1,0:T(8,128)S(1)}, u32[]{:S(2)}, u32[]{:S(2)}) collective-permute-start(f32[64,2048]{1,0:T(8,128)S(1)} %pad_maximum_fusion.13), channel_id=1, source_target_pairs={{0,192},{1,49},{2,194},{3,51},{4,196},{5,53},{6,198},{7,55},{8,200... | collective-permute-start | bytes 1572872 | tf_op jit(solution)/shard_map/ppermute | solution.py:29
  80.8 0.5 convolution_add_fusion.5
  81.3 0.5 convolution_add_fusion.4
  83.0 2.7 %collective-permute-start.7 = (f32[64,2048]{1,0:T(8,128)S(1)}, f32[64,2048]{1,0:T(8,128)S(1)}, u32[]{:S(2)}, u32[]{:S(2)}) collective-permute-start(f32[64,2048]{1,0:T(8,128)S(1)} %pad_maximum_fusion.11), channel_id=1, source_target_pairs={{0,192},{1,49},{2,194},{3,51},{4,196},{5,53},{6,198},{7,55},{8,200... | collective-permute-start | bytes 1572872 | tf_op jit(solution)/shard_map/ppermute | solution.py:29
  85.7 1.4 %collective-permute-done.12 = f32[64,2048]{1,0:T(8,128)S(1)} collective-permute-done((f32[64,2048]{1,0:T(8,128)S(1)}, f32[64,2048]{1,0:T(8,128)S(1)}, u32[]{:S(2)}, u32[]{:S(2)}) %collective-permute-start.12) | collective-permute-done | bytes 524320 | tf_op jit(solution)/shard_map/ppermute | solution.py:29
  87.2 2.8 %collective-permute-start.14 = (f32[64,1024]{1,0:T(8,128)S(1)}, f32[64,1024]{1,0:T(8,128)S(1)}, u32[]{:S(2)}, u32[]{:S(2)}) collective-permute-start(f32[64,1024]{1,0:T(8,128)S(1)} %slice_add_fusion.1), channel_id=1, source_target_pairs={{0,192},{1,49},{2,194},{3,51},{4,196},{5,53},{6,198},{7,55},{8,200... | collective-permute-start | bytes 786440 | tf_op jit(solution)/shard_map/ppermute | solution.py:29
  90.1 2.6 %collective-permute-done.8 = f32[64,2048]{1,0:T(8,128)S(1)} collective-permute-done((f32[64,2048]{1,0:T(8,128)S(1)}, f32[64,2048]{1,0:T(8,128)S(1)}, u32[]{:S(2)}, u32[]{:S(2)}) %collective-permute-start.8) | collective-permute-done | bytes 524320 | tf_op jit(solution)/shard_map/ppermute | solution.py:29
  92.9 2.8 %collective-permute-start.10 = (f32[64,1024]{1,0:T(8,128)S(1)}, f32[64,1024]{1,0:T(8,128)S(1)}, u32[]{:S(2)}, u32[]{:S(2)}) collective-permute-start(f32[64,1024]{1,0:T(8,128)S(1)} %slice_add_fusion.5), channel_id=1, source_target_pairs={{0,192},{1,49},{2,194},{3,51},{4,196},{5,53},{6,198},{7,55},{8,200... | collective-permute-start | bytes 786440 | tf_op jit(solution)/shard_map/ppermute | solution.py:29
  95.8 3.5 %collective-permute-done.9 = f32[64,1024]{1,0:T(8,128)S(1)} collective-permute-done((f32[64,1024]{1,0:T(8,128)S(1)}, f32[64,1024]{1,0:T(8,128)S(1)}, u32[]{:S(2)}, u32[]{:S(2)}) %collective-permute-start.9) | collective-permute-done | bytes 262176 | tf_op jit(solution)/shard_map/ppermute | solution.py:29
  99.7 1.5 %collective-permute-start.15 = (f32[16,3072]{1,0:T(8,128)S(1)}, f32[16,3072]{1,0:T(8,128)S(1)}, u32[]{:S(2)}, u32[]{:S(2)}) collective-permute-start(f32[16,3072]{1,0:T(8,128)S(1)} %pad_maximum_fusion.16), channel_id=1, source_target_pairs={{0,4},{1,5},{2,6},{3,7},{4,8},{5,9},{6,10},{7,11},{8,12},{9,13},{1... | collective-permute-start | bytes 589832 | tf_op jit(solution)/shard_map/ppermute | solution.py:29
  101.2 3.1 %collective-permute-start.17 = (f32[16,3072]{1,0:T(8,128)S(1)}, f32[16,3072]{1,0:T(8,128)S(1)}, u32[]{:S(2)}, u32[]{:S(2)}) collective-permute-start(f32[16,3072]{1,0:T(8,128)S(1)} %fusion.25), channel_id=1, source_target_pairs={{0,12},{1,13},{2,14},{3,15},{4,0},{5,1},{6,2},{7,3},{8,4},{9,5},{1... | collective-permute-start | bytes 589832 | tf_op jit(solution)/shard_map/ppermute | solution.py:29
  104.3 3.5 %collective-permute-done.15 = f32[16,3072]{1,0:T(8,128)S(1)} collective-permute-done((f32[16,3072]{1,0:T(8,128)S(1)}, f32[16,3072]{1,0:T(8,128)S(1)}, u32[]{:S(2)}, u32[]{:S(2)}) %collective-permute-start.15) | collective-permute-done | bytes 196640 | tf_op jit(solution)/shard_map/ppermute | solution.py:29
  107.9 2.7 %collective-permute-start.16 = (f32[16,2048]{1,0:T(8,128)S(1)}, f32[16,2048]{1,0:T(8,128)S(1)}, u32[]{:S(2)}, u32[]{:S(2)}) collective-permute-start(f32[16,2048]{1,0:T(8,128)S(1)} %slice_add_fusion.9), channel_id=1, source_target_pairs={{0,2},{1,3},{2,4},{3,5},{4,6},{5,7},{6,8},{7,9},{8,10},{9,11},{10,... | collective-permute-start | bytes 393224 | tf_op jit(solution)/shard_map/ppermute | solution.py:29
  110.6 2.8 %collective-permute-start.19 = (f32[16,2048]{1,0:T(8,128)S(1)}, f32[16,2048]{1,0:T(8,128)S(1)}, u32[]{:S(2)}, u32[]{:S(2)}) collective-permute-start(f32[16,2048]{1,0:T(8,128)S(1)} %fusion.27), channel_id=1, source_target_pairs={{0,4},{1,5},{2,6},{3,7},{4,8},{5,9},{6,10},{7,11},{8,12},{9,13},{1... | collective-permute-start | bytes 393224 | tf_op jit(solution)/shard_map/ppermute | solution.py:29
  113.4 2.7 %collective-permute-start.18 = (f32[16,2048]{1,0:T(8,128)S(1)}, f32[16,2048]{1,0:T(8,128)S(1)}, u32[]{:S(2)}, u32[]{:S(2)}) collective-permute-start(f32[16,2048]{1,0:T(8,128)S(1)} %slice_add_fusion.8), channel_id=1, source_target_pairs={{0,14},{1,15},{2,0},{3,1},{4,2},{5,3},{6,4},{7,5},{8,6},{9,7},{10,... | collective-permute-start | bytes 393224 | tf_op jit(solution)/shard_map/ppermute | solution.py:29
  116.1 3.3 %collective-permute-done.19 = f32[16,2048]{1,0:T(8,128)S(1)} collective-permute-done((f32[16,2048]{1,0:T(8,128)S(1)}, f32[16,2048]{1,0:T(8,128)S(1)}, u32[]{:S(2)}, u32[]{:S(2)}) %collective-permute-start.19) | collective-permute-done | bytes 131104 | tf_op jit(solution)/shard_map/ppermute | solution.py:29
  119.4 1.3 collective-permute-done.18
  120.7 5.0 %collective-permute-done.20 = f32[16,2048]{1,0:T(8,128)S(1)} collective-permute-done((f32[16,2048]{1,0:T(8,128)S(1)}, f32[16,2048]{1,0:T(8,128)S(1)}, u32[]{:S(2)}, u32[]{:S(2)}) %collective-permute-start.20) | collective-permute-done | bytes 131104 | tf_op jit(solution)/shard_map/ppermute | solution.py:29
  125.7 3.7 %collective-permute-start.21 = (f32[8,2048]{1,0:T(8,128)S(1)}, f32[8,2048]{1,0:T(8,128)S(1)}, u32[]{:S(2)}, u32[]{:S(2)}) collective-permute-start(f32[8,2048]{1,0:T(8,128)S(1)} %dynamic-slice_bitcast_fusion.8), channel_id=1, source_target_pairs={{0,1},{1,0},{2,3},{3,2},{4,5},{5,4},{6,7},{7,6},{8,9},{9,8},{10,11... | collective-permute-start | bytes 196616 | tf_op jit(solution)/shard_map/ppermute | solution.py:147
  129.4 5.4 %add_multiply_fusion = f32[336,2048]{1,0:T(8,128)} fusion(f32[336,2048]{1,0:T(8,128)} %collective-permute-done.22, pred[]{:T(512)S(6)} %eq.19, f32[112,4096]{1,0:T(8,128)S(1)} %fusion.4, f32[224,4096]{1,0:T(8,128)} %fusion), kind=kLoop, calls=%fused_computation.14 | loop fusion | flops 3440640 | bytes 11010049 | tf_op jit(solution)/shard_map/mul | solution.py:151
  134.9 0.7 maximum_bitcast_fusion.6
  (90 shorter events, 5.4 us)
Async XLA Ops:
  0.6 17.1 %copy-start = (bf16[112,4096]{1,0:T(8,128)(2,1)S(1)}, bf16[112,4096]{1,0:T(8,128)(2,1)}, u32[]{:S(2)}) copy-start(bf16[112,4096]{1,0:T(8,128)(2,1)} %param.9) | copy-start | bytes 2752516
  0.6 9.7 %copy-start.4 = (bf16[4096,2,112]{0,2,1:T(8,128)(2,1)S(1)}, bf16[4096,2,112]{0,2,1:T(8,128)(2,1)}, u32[]{:S(2)}) copy-start(bf16[4096,2,112]{0,2,1:T(8,128)(2,1)} %param.8) | copy-start | bytes 5505028
  0.7 9.1 %copy-start.11 = (s32[1,2]{1,0:T(1,128)S(1)}, s32[1,2]{1,0:T(1,128)}, u32[]{:S(2)}) copy-start(s32[1,2]{1,0:T(1,128)} %param.7) | copy-start | bytes 28
  3.5 49.2 %collective-permute-start.3 = (f32[112,2048]{1,0:T(8,128)}, f32[112,2048]{1,0:T(8,128)}, u32[]{:S(2)}, u32[]{:S(2)}) collective-permute-start(f32[112,2048]{1,0:T(8,128)} %get-tuple-element.30), channel_id=1, source_target_pairs={{0,16},{1,65},{2,18},{3,67},{4,20},{5,69},{6,22},{7,71},{8,24},{9,... | collective-permute-start | bytes 2752520 | tf_op jit(solution)/shard_map/ppermute | solution.py:29
  5.6 41.9 %collective-permute-start.1 = (f32[112,2048]{1,0:T(8,128)}, f32[112,2048]{1,0:T(8,128)}, u32[]{:S(2)}, u32[]{:S(2)}) collective-permute-start(f32[112,2048]{1,0:T(8,128)} %get-tuple-element.30), channel_id=1, source_target_pairs={{0,48},{1,193},{2,50},{3,195},{4,52},{5,197},{6,54},{7,199},{8,56}... | collective-permute-start | bytes 2752520 | tf_op jit(solution)/shard_map/ppermute | solution.py:29
  7.0 43.1 %collective-permute-start.4 = (f32[112,2048]{1,0:T(8,128)}, f32[112,2048]{1,0:T(8,128)}, u32[]{:S(2)}, u32[]{:S(2)}) collective-permute-start(f32[112,2048]{1,0:T(8,128)} %get-tuple-element.31), channel_id=1, source_target_pairs={{0,16},{1,65},{2,18},{3,67},{4,20},{5,69},{6,22},{7,71},{8,24},{9,... | collective-permute-start | bytes 2752520 | tf_op jit(solution)/shard_map/ppermute | solution.py:29
  7.1 46.9 %collective-permute-start.2 = (f32[112,2048]{1,0:T(8,128)}, f32[112,2048]{1,0:T(8,128)}, u32[]{:S(2)}, u32[]{:S(2)}) collective-permute-start(f32[112,2048]{1,0:T(8,128)} %get-tuple-element.31), channel_id=1, source_target_pairs={{0,48},{1,193},{2,50},{3,195},{4,52},{5,197},{6,54},{7,199},{8,56}... | collective-permute-start | bytes 2752520 | tf_op jit(solution)/shard_map/ppermute | solution.py:29
  10.3 7.4 %copy-start.3 = (bf16[1,1024,4096]{2,1,0:T(8,128)(2,1)S(1)}, bf16[1,1024,4096]{2,1,0:T(8,128)(2,1)}, u32[]{:S(2)}) copy-start(bf16[1,1024,4096]{2,1,0:T(8,128)(2,1)} %param.6) | copy-start | bytes 25165828
  16.5 4.2 %copy-start.10 = (f32[224,1024]{1,0:T(8,128)}, f32[224,1024]{1,0:T(8,128)S(1)}, u32[]{:S(2)}) copy-start(f32[224,1024]{1,0:T(8,128)S(1)} %fusion.2) | copy-start | bytes 2752516
  23.0 18.4 %collective-permute-start = (f32[224,1024]{1,0:T(8,128)}, f32[224,1024]{1,0:T(8,128)S(1)}, u32[]{:S(2)}, u32[]{:S(2)}) collective-permute-start(f32[224,1024]{1,0:T(8,128)} %get-tuple-element.33), channel_id=1, source_target_pairs={{0,1},{1,0},{2,3},{3,2},{4,5},{5,4},{6,7},{7,6},{8,9},{9,8},{10,11... | collective-permute-start | bytes 2752520 | tf_op jit(solution)/shard_map/ppermute | solution.py:87
  34.3 5.1 %copy-start.2 = (f32[224,4096]{1,0:T(8,128)S(1)}, f32[224,4096]{1,0:T(8,128)}, u32[]{:S(2)}) copy-start(f32[224,4096]{1,0:T(8,128)} %fusion) | copy-start | bytes 11010052
  39.4 1.9 %copy-start.9 = (f32[224,1024]{1,0:T(8,128)S(1)}, f32[224,1024]{1,0:T(8,128)}, u32[]{:S(2)}) copy-start(f32[224,1024]{1,0:T(8,128)} %get-tuple-element.32) | copy-start | bytes 2752516
  41.5 87.9 %collective-permute-start.22 = (f32[336,2048]{1,0:T(8,128)}, f32[336,2048]{1,0:T(8,128)}, u32[]{:S(2)}, u32[]{:S(2)}) collective-permute-start(f32[336,2048]{1,0:T(8,128)} %broadcast_select_fusion), channel_id=1, source_target_pairs={{0,1},{1,0},{2,3},{3,2},{4,5},{5,4},{6,7},{7,6},{8,9},{9,8},{10,11... | collective-permute-start | bytes 8257544 | tf_op jit(solution)/shard_map/ppermute | solution.py:100
  43.2 29.0 %all-to-all-start = ((f32[4,448,256]{2,1,0:T(8,128)}), f32[4,448,256]{2,1,0:T(8,128)}, u32[]{:S(2)}, u32[]{:S(2)}) async-start(f32[4,448,256]{2,1,0:T(8,128)} %pad_maximum_fusion.1), calls=%async_computation | async-start | bytes 3670016 | tf_op jit(solution)/shard_map/all_to_all | solution.py:34
  47.6 22.6 %collective-permute-start.5 = (f32[112,2048]{1,0:T(8,128)}, f32[112,2048]{1,0:T(8,128)S(1)}, u32[]{:S(2)}, u32[]{:S(2)}) collective-permute-start(f32[112,2048]{1,0:T(8,128)} %collective-permute-done.1), channel_id=1, source_target_pairs={{0,48},{1,193},{2,50},{3,195},{4,52},{5,197},{6,54},{7,199},{8,56}... | collective-permute-start | bytes 2752520 | tf_op jit(solution)/shard_map/ppermute | solution.py:29
  50.2 21.1 %collective-permute-start.6 = (f32[112,2048]{1,0:T(8,128)}, f32[112,2048]{1,0:T(8,128)S(1)}, u32[]{:S(2)}, u32[]{:S(2)}) collective-permute-start(f32[112,2048]{1,0:T(8,128)} %collective-permute-done.4), channel_id=1, source_target_pairs={{0,16},{1,65},{2,18},{3,67},{4,20},{5,69},{6,22},{7,71},{8,24},{9,... | collective-permute-start | bytes 2752520 | tf_op jit(solution)/shard_map/ppermute | solution.py:29
  72.1 2.1 %copy-start.5 = (bf16[4096,2,112]{0,2,1:T(8,128)(2,1)S(1)}, bf16[4096,2,112]{0,2,1:T(8,128)(2,1)}, u32[]{:S(2)}) copy-start(bf16[4096,2,112]{0,2,1:T(8,128)(2,1)} %param.8) | copy-start | bytes 5505028
  73.9 1.1 copy-start.7
  75.4 1.0 copy-start.6
  75.4 1.1 copy-start.8
  77.5 9.6 %collective-permute-start.12 = (f32[64,2048]{1,0:T(8,128)S(1)}, f32[64,2048]{1,0:T(8,128)S(1)}, u32[]{:S(2)}, u32[]{:S(2)}) collective-permute-start(f32[64,2048]{1,0:T(8,128)S(1)} %pad_maximum_fusion.14), channel_id=1, source_target_pairs={{0,64},{1,17},{2,66},{3,19},{4,68},{5,21},{6,70},{7,23},{8,72},{9,... | collective-permute-start | bytes 1572872 | tf_op jit(solution)/shard_map/ppermute | solution.py:29
  77.6 9.5 %collective-permute-start.11 = (f32[64,2048]{1,0:T(8,128)S(1)}, f32[64,2048]{1,0:T(8,128)S(1)}, u32[]{:S(2)}, u32[]{:S(2)}) collective-permute-start(f32[64,2048]{1,0:T(8,128)S(1)} %pad_maximum_fusion.13), channel_id=1, source_target_pairs={{0,192},{1,49},{2,194},{3,51},{4,196},{5,53},{6,198},{7,55},{8,200... | collective-permute-start | bytes 1572872 | tf_op jit(solution)/shard_map/ppermute | solution.py:29
  82.6 10.1 %collective-permute-start.8 = (f32[64,2048]{1,0:T(8,128)S(1)}, f32[64,2048]{1,0:T(8,128)S(1)}, u32[]{:S(2)}, u32[]{:S(2)}) collective-permute-start(f32[64,2048]{1,0:T(8,128)S(1)} %pad_maximum_fusion.12), channel_id=1, source_target_pairs={{0,64},{1,17},{2,66},{3,19},{4,68},{5,21},{6,70},{7,23},{8,72},{9,... | collective-permute-start | bytes 1572872 | tf_op jit(solution)/shard_map/ppermute | solution.py:29
  83.0 9.8 %collective-permute-start.7 = (f32[64,2048]{1,0:T(8,128)S(1)}, f32[64,2048]{1,0:T(8,128)S(1)}, u32[]{:S(2)}, u32[]{:S(2)}) collective-permute-start(f32[64,2048]{1,0:T(8,128)S(1)} %pad_maximum_fusion.11), channel_id=1, source_target_pairs={{0,192},{1,49},{2,194},{3,51},{4,196},{5,53},{6,198},{7,55},{8,200... | collective-permute-start | bytes 1572872 | tf_op jit(solution)/shard_map/ppermute | solution.py:29
  87.1 8.5 %collective-permute-start.13 = (f32[64,1024]{1,0:T(8,128)S(1)}, f32[64,1024]{1,0:T(8,128)S(1)}, u32[]{:S(2)}, u32[]{:S(2)}) collective-permute-start(f32[64,1024]{1,0:T(8,128)S(1)} %slice_add_fusion.2), channel_id=1, source_target_pairs={{0,64},{1,17},{2,66},{3,19},{4,68},{5,21},{6,70},{7,23},{8,72},{9,... | collective-permute-start | bytes 786440 | tf_op jit(solution)/shard_map/ppermute | solution.py:29
  87.2 8.4 %collective-permute-start.14 = (f32[64,1024]{1,0:T(8,128)S(1)}, f32[64,1024]{1,0:T(8,128)S(1)}, u32[]{:S(2)}, u32[]{:S(2)}) collective-permute-start(f32[64,1024]{1,0:T(8,128)S(1)} %slice_add_fusion.1), channel_id=1, source_target_pairs={{0,192},{1,49},{2,194},{3,51},{4,196},{5,53},{6,198},{7,55},{8,200... | collective-permute-start | bytes 786440 | tf_op jit(solution)/shard_map/ppermute | solution.py:29
  92.8 6.6 %collective-permute-start.9 = (f32[64,1024]{1,0:T(8,128)S(1)}, f32[64,1024]{1,0:T(8,128)S(1)}, u32[]{:S(2)}, u32[]{:S(2)}) collective-permute-start(f32[64,1024]{1,0:T(8,128)S(1)} %slice_add_fusion.6), channel_id=1, source_target_pairs={{0,64},{1,17},{2,66},{3,19},{4,68},{5,21},{6,70},{7,23},{8,72},{9,... | collective-permute-start | bytes 786440 | tf_op jit(solution)/shard_map/ppermute | solution.py:29
  92.9 6.5 %collective-permute-start.10 = (f32[64,1024]{1,0:T(8,128)S(1)}, f32[64,1024]{1,0:T(8,128)S(1)}, u32[]{:S(2)}, u32[]{:S(2)}) collective-permute-start(f32[64,1024]{1,0:T(8,128)S(1)} %slice_add_fusion.5), channel_id=1, source_target_pairs={{0,192},{1,49},{2,194},{3,51},{4,196},{5,53},{6,198},{7,55},{8,200... | collective-permute-start | bytes 786440 | tf_op jit(solution)/shard_map/ppermute | solution.py:29
  99.7 8.2 %collective-permute-start.15 = (f32[16,3072]{1,0:T(8,128)S(1)}, f32[16,3072]{1,0:T(8,128)S(1)}, u32[]{:S(2)}, u32[]{:S(2)}) collective-permute-start(f32[16,3072]{1,0:T(8,128)S(1)} %pad_maximum_fusion.16), channel_id=1, source_target_pairs={{0,4},{1,5},{2,6},{3,7},{4,8},{5,9},{6,10},{7,11},{8,12},{9,13},{1... | collective-permute-start | bytes 589832 | tf_op jit(solution)/shard_map/ppermute | solution.py:29
  101.2 12.2 %collective-permute-start.17 = (f32[16,3072]{1,0:T(8,128)S(1)}, f32[16,3072]{1,0:T(8,128)S(1)}, u32[]{:S(2)}, u32[]{:S(2)}) collective-permute-start(f32[16,3072]{1,0:T(8,128)S(1)} %fusion.25), channel_id=1, source_target_pairs={{0,12},{1,13},{2,14},{3,15},{4,0},{5,1},{6,2},{7,3},{8,4},{9,5},{1... | collective-permute-start | bytes 589832 | tf_op jit(solution)/shard_map/ppermute | solution.py:29
  107.9 8.2 %collective-permute-start.16 = (f32[16,2048]{1,0:T(8,128)S(1)}, f32[16,2048]{1,0:T(8,128)S(1)}, u32[]{:S(2)}, u32[]{:S(2)}) collective-permute-start(f32[16,2048]{1,0:T(8,128)S(1)} %slice_add_fusion.9), channel_id=1, source_target_pairs={{0,2},{1,3},{2,4},{3,5},{4,6},{5,7},{6,8},{7,9},{8,10},{9,11},{10,... | collective-permute-start | bytes 393224 | tf_op jit(solution)/shard_map/ppermute | solution.py:29
  110.6 8.8 %collective-permute-start.19 = (f32[16,2048]{1,0:T(8,128)S(1)}, f32[16,2048]{1,0:T(8,128)S(1)}, u32[]{:S(2)}, u32[]{:S(2)}) collective-permute-start(f32[16,2048]{1,0:T(8,128)S(1)} %fusion.27), channel_id=1, source_target_pairs={{0,4},{1,5},{2,6},{3,7},{4,8},{5,9},{6,10},{7,11},{8,12},{9,13},{1... | collective-permute-start | bytes 393224 | tf_op jit(solution)/shard_map/ppermute | solution.py:29
  113.4 7.2 %collective-permute-start.18 = (f32[16,2048]{1,0:T(8,128)S(1)}, f32[16,2048]{1,0:T(8,128)S(1)}, u32[]{:S(2)}, u32[]{:S(2)}) collective-permute-start(f32[16,2048]{1,0:T(8,128)S(1)} %slice_add_fusion.8), channel_id=1, source_target_pairs={{0,14},{1,15},{2,0},{3,1},{4,2},{5,3},{6,4},{7,5},{8,6},{9,7},{10,... | collective-permute-start | bytes 393224 | tf_op jit(solution)/shard_map/ppermute | solution.py:29
  116.1 9.6 %collective-permute-start.20 = (f32[16,2048]{1,0:T(8,128)S(1)}, f32[16,2048]{1,0:T(8,128)S(1)}, u32[]{:S(2)}, u32[]{:S(2)}) collective-permute-start(f32[16,2048]{1,0:T(8,128)S(1)} %pad_maximum_fusion.17), channel_id=1, source_target_pairs={{0,12},{1,13},{2,14},{3,15},{4,0},{5,1},{6,2},{7,3},{8,4},{9,5},{1... | collective-permute-start | bytes 393224 | tf_op jit(solution)/shard_map/ppermute | solution.py:29
  125.7 9.1 %collective-permute-start.21 = (f32[8,2048]{1,0:T(8,128)S(1)}, f32[8,2048]{1,0:T(8,128)S(1)}, u32[]{:S(2)}, u32[]{:S(2)}) collective-permute-start(f32[8,2048]{1,0:T(8,128)S(1)} %dynamic-slice_bitcast_fusion.8), channel_id=1, source_target_pairs={{0,1},{1,0},{2,3},{3,2},{4,5},{5,4},{6,7},{7,6},{8,9},{9,8},{10,11... | collective-permute-start | bytes 196616 | tf_op jit(solution)/shard_map/ppermute | solution.py:147
  129.4 6.1 %copy-start.1 = (bf16[112,4096]{1,0:T(8,128)(2,1)S(1)}, bf16[112,4096]{1,0:T(8,128)(2,1)}, u32[]{:S(2)}) copy-start(bf16[112,4096]{1,0:T(8,128)(2,1)} %param.9) | copy-start | bytes 2752516

commit v8 on v7

--- a/solution.py
+++ b/solution.py
@@ -59,8 +59,6 @@
     w_gate, w_up = w_mine[:units].astype(jnp.float32), w_mine[units:].astype(jnp.float32)
     next_gate = hop(w_gate, dims, FIRST, -1)
     last_up = hop(w_up, dims, FIRST, 1)
-    next_up = hop(w_up, dims, FIRST, -1)
-    last_gate = hop(w_gate, dims, FIRST, 1)
     far_gate = hop(next_gate, dims, FIRST, -1)
     far_up = hop(last_up, dims, FIRST, 1)
 
@@ -68,6 +66,9 @@
     limit = jnp.where(position < slots, lengths[0, 0], slots + lengths[0, 1])
     is_alive = (position < limit)[None, :]
     gate_up = dot(w_t, x, 1, 1)
+    gate_up, w_gate, w_up = lax.optimization_barrier((gate_up, w_gate, w_up))
+    next_up = hop(w_up, dims, FIRST, -1)
+    last_gate = hop(w_gate, dims, FIRST, 1)
     gate, upward = gate_up[:units], gate_up[units:]
     sig = jax.nn.sigmoid(gate)
     activated = gate * sig
@@ -136,8 +137,9 @@
     near_up, near_down = b1 + ru[:, :half], b7 + rd[:, :half]
     far_up_sum = jnp.concatenate([b2[:, :cut] + ru[:, half:], b2[:, cut:]], axis=1)
     far_down_sum = jnp.concatenate([b6[:, :cut], b6[:, cut:] + rd[:, half:]], axis=1)
-    near_up, far_up_sum = lax.optimization_barrier((near_up, far_up_sum))
-    near_down, far_down_sum = lax.optimization_barrier((near_down, far_down_sum))
+    near_up, near_down, far_up_sum, far_down_sum = lax.optimization_barrier(
+        (near_up, near_down, far_up_sum, far_down_sum)
+    )
     s2 = hop(far_up_sum, dims, along, 2)
     s6 = hop(far_down_sum, dims, along, -2)
     s1 = hop(near_up, dims, along, 1)

time: 136 us -> 142 us (1.044)
  the two profiles are of different devices: /device:TPU:1 before, /device:TPU:81 now
where the time goes in v8:
time: 142 us; the launch traced here: 141 us
  starting transfers between devices  43.7 us (31%)
  waiting for transfers between devices  37.5 us (26%)
  matrix products  31.7 us (22%)
  other arithmetic  22.9 us (16%)
  local copies, waits for them, and re-layouts  3.01 us (2%)
  between operations  2.35 us (2%)
    ppermute x20, waiting for transfers between devices, hop(): return lax.ppermute(value, ALL, sorted(pairs))  37.5 us
    dot_general x13, matrix products, dot(): lax.dot_general(a, b, (((over_a,), (over_b,)), ((), ())), preferred_eleme...  31.7 us
    ppermute x20, starting transfers between devices, hop(): return lax.ppermute(value, ALL, sorted(pairs))  24.4 us
    ppermute x1, starting transfers between devices, per_device(): lax.ppermute(lax.dynamic_index_in_dim(total, 1 - rep, 0, False), 'rep', S...  11.8 us
    convert_element_type x6, other arithmetic, per_device(): arrived = lambda p: (p * one).astype(jnp.bfloat16)  7.47 us
    mul x1, other arithmetic, per_device(): shared = (kept + back) * GRAD_SCALE  5.44 us
    all_to_all x1, starting transfers between devices, exchange(): lax.all_to_all(value, ALL, 0, 0, tiled=True, axis_index_groups=groups)  4.44 us
    ppermute x1, starting transfers between devices, per_device(): theirs = lax.ppermute(away, 'rep', SWAP)  3.01 us
  transfers between devices with their start and end apart: 24, of which 11 were waited for; matrix products, arithmetic and copies ran while one was open for 37% of the time, Pallas kernels for 0%

profile of v8, /device:TPU:81, one launch (start us, length us, event | category | flops | bytes accessed | tf_op | source)
XLA Modules:
  0.0 141.2 jit_solution(17361396373086959247)
XLA Ops:
  0.7 2.8 %dynamic-slice_convert_fusion = (f32[112,2048]{1,0:T(8,128)}, f32[112,2048]{1,0:T(8,128)}) fusion(bf16[224,4096]{1,0:T(8,128)(2,1)} %bitcast.121, s32[]{:T(128)S(6)} %add.343, s32[]{:T(128)S(6)} %select_n.181), kind=kLoop, calls=%fused_computation.54 | loop fusion | flops 458752 | bytes 2752520 | tf_op jit(solution)/shard_map/convert_element_type | solution.py:59
  3.5 1.0 collective-permute-start.4
  4.9 6.9 %fusion.2 = f32[224,1024]{1,0:T(8,128)} fusion(bf16[224,4096]{1,0:T(8,128)(2,1)S(1)} %bitcast.122, bf16[1,1024,4096]{2,1,0:T(8,128)(2,1)} %param.5), kind=kOutput, calls=%fused_computation.2 | convolution fusion | flops 1879048192 | bytes 11141120 | tf_op jit(solution)/shard_map/dot_general | solution.py:38
  12.0 1.3 collective-permute-start.3
  13.3 0.6 fusion.87
  14.5 0.7 select_compare_fusion
  15.1 6.4 %multiply_convert_fusion.11 = (bf16[112,1024]{1,0:T(8,128)(2,1)S(1)}, bf16[112,1024]{1,0:T(8,128)(2,1)S(1)}) fusion(f32[224,1024]{1,0:T(8,128)} %fusion.2, bf16[112,4096]{1,0:T(8,128)(2,1)S(1)} %copy-done, bf16[1,1024,4096]{2,1,0:T(8,128)(2,1)} %param.6, pred[1024]{0:T(1024)(128)(4,1)S(1)} %select_compare_fusion), kind=kOutput, calls=%fused_computation.67 | convolution fusion | flops 941129728 | bytes 10683392 | tf_op jit(solution)/shard_map/dot_general | solution.py:38
  21.6 2.3 %convert_select_fusion.1 = (f32[224,1024]{1,0:T(8,128)}, f32[224,1024]{1,0:T(8,128)}) fusion(pred[]{:T(512)S(6)} %eq.19, bf16[112,1024]{1,0:T(8,128)(2,1)S(1)} %get-tuple-element.41, bf16[112,1024]{1,0:T(8,128)(2,1)S(1)} %get-tuple-element.40, s32[1024]{0:T(1024)S(1)} %fusion.70), kind=kOutput, calls=%fused_computation.26 | convolution fusion | flops 473104384 | bytes 2297857 | tf_op jit(solution)/shard_map/dot_general | solution.py:38
  23.9 3.0 %collective-permute-start = (f32[224,1024]{1,0:T(8,128)}, f32[224,1024]{1,0:T(8,128)S(1)}, u32[]{:S(2)}, u32[]{:S(2)}) collective-permute-start(f32[224,1024]{1,0:T(8,128)} %get-tuple-element.39), channel_id=1, source_target_pairs={{0,1},{1,0},{2,3},{3,2},{4,5},{5,4},{6,7},{7,6},{8,9},{9,8},{10,11... | collective-permute-start | bytes 2752520 | tf_op jit(solution)/shard_map/ppermute | solution.py:88
  27.5 7.2 %fusion = f32[224,4096]{1,0:T(8,128)} fusion(bf16[1,1024,4096]{2,1,0:T(8,128)(2,1)} %param.5, bf16[112,1024]{1,0:T(8,128)(2,1)S(1)} %get-tuple-element.41, bf16[112,1024]{1,0:T(8,128)(2,1)S(1)} %get-tuple-element.40), kind=kOutput, calls=%fused_computation | convolution fusion | flops 1879965696 | bytes 12517376 | tf_op jit(solution)/shard_map/dot_general | solution.py:38
  34.8 5.1 %fusion.4 = f32[112,4096]{1,0:T(8,128)S(1)} fusion(bf16[1,1024,4096]{2,1,0:T(8,128)(2,1)} %param.6, f32[224,1024]{1,0:T(8,128)} %fusion.2, pred[1024]{0:T(1024)(128)(4,1)S(1)} %select_compare_fusion), kind=kOutput, calls=%fused_computation.4 | convolution fusion | flops 940326912 | bytes 11142144 | tf_op jit(solution)/shard_map/dot_general | solution.py:38
  39.9 1.9 %broadcast_select_fusion = f32[336,2048]{1,0:T(8,128)} fusion(pred[]{:T(512)S(6)} %eq.19, f32[112,4096]{1,0:T(8,128)S(1)} %fusion.4, f32[224,4096]{1,0:T(8,128)S(1)} %copy-done.2), kind=kLoop, calls=%fused_computation.23 | loop fusion | flops 2064384 | bytes 8257537 | tf_op jit(solution)/shard_map/jit(_where)/select_n | solution.py:100
  42.2 1.4 pad_maximum_fusion.1
  43.6 4.4 %all-to-all-start = ((f32[4,448,256]{2,1,0:T(8,128)}), f32[4,448,256]{2,1,0:T(8,128)}, u32[]{:S(2)}, u32[]{:S(2)}) async-start(f32[4,448,256]{2,1,0:T(8,128)} %pad_maximum_fusion.1), calls=%async_computation | async-start | bytes 3670016 | tf_op jit(solution)/shard_map/all_to_all | solution.py:34
  48.0 1.1 collective-permute-start.6
  49.6 1.2 multiply_convert_fusion.2
  50.8 1.2 multiply_convert_fusion.5
  52.1 1.2 multiply_convert_fusion.4
  53.4 2.0 %multiply_convert_fusion.3 = bf16[112,2048]{1,0:T(8,128)(2,1)} fusion(f32[112,2048]{1,0:T(8,128)} %collective-permute-done.3, f32[]{:T(128)S(6)} %convert_element_type.54), kind=kLoop, calls=%fused_computation.33 | loop fusion | flops 458752 | bytes 1376260 | tf_op jit(solution)/shard_map/convert_element_type | solution.py:103
  55.4 14.0 %collective-permute-done.6 = f32[112,2048]{1,0:T(8,128)S(1)} collective-permute-done((f32[112,2048]{1,0:T(8,128)}, f32[112,2048]{1,0:T(8,128)S(1)}, u32[]{:S(2)}, u32[]{:S(2)}) %collective-permute-start.6) | collective-permute-done | bytes 917536 | tf_op jit(solution)/shard_map/ppermute | solution.py:29
  69.4 0.9 multiply_convert_fusion
  70.2 0.8 multiply_convert_fusion.1
  71.1 1.7 %multiply_convert_fusion.6 = (bf16[1,448,256]{2,1,0:T(8,128)(2,1)S(1)}, bf16[1,448,256]{2,1,0:T(8,128)(2,1)S(1)}, bf16[1,448,256]{2,1,0:T(8,128)(2,1)S(1)}, bf16[1,448,256]{2,1,0:T(8,128)(2,1)S(1)}) fusion(f32[4,448,256]{2,1,0:T(8,128)} %all-to-all-done, s32[]{:T(128)S(6)} %select_n.193, f32[]{:T(128)S(6)} %convert_element_type.54, s32[]{:T(128)S(6)} %select_n.192, ...), kind=kLoop, calls=%fused_computation.62 | loop fusion | flops 917504 | bytes 2752532 | tf_op jit(solution)/shard_map/convert_element_type | solution.py:94
  73.6 0.5 convolution_add_fusion.2
  74.1 0.5 copy-done.5
  75.1 0.5 copy-done.6
  76.8 2.7 %collective-permute-start.11 = (f32[64,2048]{1,0:T(8,128)S(1)}, f32[64,2048]{1,0:T(8,128)S(1)}, u32[]{:S(2)}, u32[]{:S(2)}) collective-permute-start(f32[64,2048]{1,0:T(8,128)S(1)} %pad_maximum_fusion.13), channel_id=1, source_target_pairs={{0,192},{1,49},{2,194},{3,51},{4,196},{5,53},{6,198},{7,55},{8,200... | collective-permute-start | bytes 1572872 | tf_op jit(solution)/shard_map/ppermute | solution.py:29
  80.0 0.5 convolution_add_fusion.5
  82.1 2.7 %collective-permute-start.7 = (f32[64,2048]{1,0:T(8,128)S(1)}, f32[64,2048]{1,0:T(8,128)S(1)}, u32[]{:S(2)}, u32[]{:S(2)}) collective-permute-start(f32[64,2048]{1,0:T(8,128)S(1)} %pad_maximum_fusion.11), channel_id=1, source_target_pairs={{0,192},{1,49},{2,194},{3,51},{4,196},{5,53},{6,198},{7,55},{8,200... | collective-permute-start | bytes 1572872 | tf_op jit(solution)/shard_map/ppermute | solution.py:29
  84.9 1.1 collective-permute-done.12
  86.0 1.1 collective-permute-start.13
  87.2 1.8 %collective-permute-start.14 = (f32[64,1024]{1,0:T(8,128)S(1)}, f32[64,1024]{1,0:T(8,128)S(1)}, u32[]{:S(2)}, u32[]{:S(2)}) collective-permute-start(f32[64,1024]{1,0:T(8,128)S(1)} %slice_add_fusion.1), channel_id=1, source_target_pairs={{0,192},{1,49},{2,194},{3,51},{4,196},{5,53},{6,198},{7,55},{8,200... | collective-permute-start | bytes 786440 | tf_op jit(solution)/shard_map/ppermute | solution.py:29
  88.9 2.6 %collective-permute-done.8 = f32[64,2048]{1,0:T(8,128)S(1)} collective-permute-done((f32[64,2048]{1,0:T(8,128)S(1)}, f32[64,2048]{1,0:T(8,128)S(1)}, u32[]{:S(2)}, u32[]{:S(2)}) %collective-permute-start.8) | collective-permute-done | bytes 524320 | tf_op jit(solution)/shard_map/ppermute | solution.py:29
  91.7 1.1 collective-permute-start.9
  92.8 1.8 %collective-permute-start.10 = (f32[64,1024]{1,0:T(8,128)S(1)}, f32[64,1024]{1,0:T(8,128)S(1)}, u32[]{:S(2)}, u32[]{:S(2)}) collective-permute-start(f32[64,1024]{1,0:T(8,128)S(1)} %slice_add_fusion.5), channel_id=1, source_target_pairs={{0,192},{1,49},{2,194},{3,51},{4,196},{5,53},{6,198},{7,55},{8,200... | collective-permute-start | bytes 786440 | tf_op jit(solution)/shard_map/ppermute | solution.py:29
  94.7 3.5 %collective-permute-done.9 = f32[64,1024]{1,0:T(8,128)S(1)} collective-permute-done((f32[64,1024]{1,0:T(8,128)S(1)}, f32[64,1024]{1,0:T(8,128)S(1)}, u32[]{:S(2)}, u32[]{:S(2)}) %collective-permute-start.9) | collective-permute-done | bytes 262176 | tf_op jit(solution)/shard_map/ppermute | solution.py:29
  98.6 4.3 %collective-permute-start.15 = (f32[16,3072]{1,0:T(8,128)S(1)}, f32[16,3072]{1,0:T(8,128)S(1)}, u32[]{:S(2)}, u32[]{:S(2)}) collective-permute-start(f32[16,3072]{1,0:T(8,128)S(1)} %pad_maximum_fusion.16), channel_id=1, source_target_pairs={{0,4},{1,5},{2,6},{3,7},{4,8},{5,9},{6,10},{7,11},{8,12},{9,13},{1... | collective-permute-start | bytes 589832 | tf_op jit(solution)/shard_map/ppermute | solution.py:29
  103.0 4.5 %collective-permute-done.15 = f32[16,3072]{1,0:T(8,128)S(1)} collective-permute-done((f32[16,3072]{1,0:T(8,128)S(1)}, f32[16,3072]{1,0:T(8,128)S(1)}, u32[]{:S(2)}, u32[]{:S(2)}) %collective-permute-start.15) | collective-permute-done | bytes 196640 | tf_op jit(solution)/shard_map/ppermute | solution.py:29
  107.5 4.2 %collective-permute-done.16 = f32[16,3072]{1,0:T(8,128)S(1)} collective-permute-done((f32[16,3072]{1,0:T(8,128)S(1)}, f32[16,3072]{1,0:T(8,128)S(1)}, u32[]{:S(2)}, u32[]{:S(2)}) %collective-permute-start.16) | collective-permute-done | bytes 196640 | tf_op jit(solution)/shard_map/ppermute | solution.py:29
  112.1 1.3 collective-permute-start.18
  113.3 1.3 collective-permute-start.19
  114.6 1.1 collective-permute-start.20
  116.0 1.4 %collective-permute-done.18 = f32[16,2048]{1,0:T(8,128)S(1)} collective-permute-done((f32[16,2048]{1,0:T(8,128)S(1)}, f32[16,2048]{1,0:T(8,128)S(1)}, u32[]{:S(2)}, u32[]{:S(2)}) %collective-permute-start.18) | collective-permute-done | bytes 131104 | tf_op jit(solution)/shard_map/ppermute | solution.py:29
  117.4 1.3 collective-permute-done.19
  118.7 4.5 %collective-permute-done.20 = f32[16,2048]{1,0:T(8,128)S(1)} collective-permute-done((f32[16,2048]{1,0:T(8,128)S(1)}, f32[16,2048]{1,0:T(8,128)S(1)}, u32[]{:S(2)}, u32[]{:S(2)}) %collective-permute-start.20) | collective-permute-done | bytes 131104 | tf_op jit(solution)/shard_map/ppermute | solution.py:29
  123.3 11.8 %collective-permute-start.21 = (f32[8,2048]{1,0:T(8,128)S(1)}, f32[8,2048]{1,0:T(8,128)S(1)}, u32[]{:S(2)}, u32[]{:S(2)}) collective-permute-start(f32[8,2048]{1,0:T(8,128)S(1)} %dynamic-slice_bitcast_fusion.8), channel_id=1, source_target_pairs={{0,1},{1,0},{2,3},{3,2},{4,5},{5,4},{6,7},{7,6},{8,9},{9,8},{10,11... | collective-permute-start | bytes 196616 | tf_op jit(solution)/shard_map/ppermute | solution.py:149
  135.0 5.4 %add_multiply_fusion = f32[336,2048]{1,0:T(8,128)} fusion(f32[336,2048]{1,0:T(8,128)} %collective-permute-done.22, pred[]{:T(512)S(6)} %eq.19, f32[112,4096]{1,0:T(8,128)S(1)} %fusion.4, f32[224,4096]{1,0:T(8,128)} %fusion), kind=kLoop, calls=%fused_computation.14 | loop fusion | flops 3440640 | bytes 11010049 | tf_op jit(solution)/shard_map/mul | solution.py:153
  140.5 0.7 maximum_bitcast_fusion.6
  (86 shorter events, 7.3 us)
Async XLA Ops:
  0.6 14.5 %copy-start = (bf16[112,4096]{1,0:T(8,128)(2,1)S(1)}, bf16[112,4096]{1,0:T(8,128)(2,1)}, u32[]{:S(2)}) copy-start(bf16[112,4096]{1,0:T(8,128)(2,1)} %param.9) | copy-start | bytes 2752516
  0.6 4.3 %copy-start.3 = (bf16[4096,2,112]{0,2,1:T(8,128)(2,1)S(1)}, bf16[4096,2,112]{0,2,1:T(8,128)(2,1)}, u32[]{:S(2)}) copy-start(bf16[4096,2,112]{0,2,1:T(8,128)(2,1)} %param.8) | copy-start | bytes 5505028
  3.5 44.6 %collective-permute-start.4 = (f32[112,2048]{1,0:T(8,128)}, f32[112,2048]{1,0:T(8,128)}, u32[]{:S(2)}, u32[]{:S(2)}) collective-permute-start(f32[112,2048]{1,0:T(8,128)} %get-tuple-element.14), channel_id=1, source_target_pairs={{0,16},{1,65},{2,18},{3,67},{4,20},{5,69},{6,22},{7,71},{8,24},{9,... | collective-permute-start | bytes 2752520 | tf_op jit(solution)/shard_map/ppermute | solution.py:29
  4.5 8.9 %copy-start.9 = (s32[1,2]{1,0:T(1,128)S(1)}, s32[1,2]{1,0:T(1,128)}, u32[]{:S(2)}) copy-start(s32[1,2]{1,0:T(1,128)} %param.7) | copy-start | bytes 28
  4.5 44.6 %collective-permute-start.1 = (f32[112,2048]{1,0:T(8,128)}, f32[112,2048]{1,0:T(8,128)}, u32[]{:S(2)}, u32[]{:S(2)}) collective-permute-start(f32[112,2048]{1,0:T(8,128)} %get-tuple-element.15), channel_id=1, source_target_pairs={{0,48},{1,193},{2,50},{3,195},{4,52},{5,197},{6,54},{7,199},{8,56}... | collective-permute-start | bytes 2752520 | tf_op jit(solution)/shard_map/ppermute | solution.py:29
  11.8 40.2 %collective-permute-start.2 = (f32[112,2048]{1,0:T(8,128)}, f32[112,2048]{1,0:T(8,128)}, u32[]{:S(2)}, u32[]{:S(2)}) collective-permute-start(f32[112,2048]{1,0:T(8,128)} %get-tuple-element.14), channel_id=1, source_target_pairs={{0,48},{1,193},{2,50},{3,195},{4,52},{5,197},{6,54},{7,199},{8,56}... | collective-permute-start | bytes 2752520 | tf_op jit(solution)/shard_map/ppermute | solution.py:29
  12.0 41.3 %collective-permute-start.3 = (f32[112,2048]{1,0:T(8,128)}, f32[112,2048]{1,0:T(8,128)}, u32[]{:S(2)}, u32[]{:S(2)}) collective-permute-start(f32[112,2048]{1,0:T(8,128)} %get-tuple-element.15), channel_id=1, source_target_pairs={{0,16},{1,65},{2,18},{3,67},{4,20},{5,69},{6,22},{7,71},{8,24},{9,... | collective-permute-start | bytes 2752520 | tf_op jit(solution)/shard_map/ppermute | solution.py:29
  23.9 18.0 %collective-permute-start = (f32[224,1024]{1,0:T(8,128)}, f32[224,1024]{1,0:T(8,128)S(1)}, u32[]{:S(2)}, u32[]{:S(2)}) collective-permute-start(f32[224,1024]{1,0:T(8,128)} %get-tuple-element.39), channel_id=1, source_target_pairs={{0,1},{1,0},{2,3},{3,2},{4,5},{5,4},{6,7},{7,6},{8,9},{9,8},{10,11... | collective-permute-start | bytes 2752520 | tf_op jit(solution)/shard_map/ppermute | solution.py:88
  34.8 5.1 %copy-start.2 = (f32[224,4096]{1,0:T(8,128)S(1)}, f32[224,4096]{1,0:T(8,128)}, u32[]{:S(2)}) copy-start(f32[224,4096]{1,0:T(8,128)} %fusion) | copy-start | bytes 11010052
  39.8 1.9 %copy-start.8 = (f32[224,1024]{1,0:T(8,128)S(1)}, f32[224,1024]{1,0:T(8,128)}, u32[]{:S(2)}) copy-start(f32[224,1024]{1,0:T(8,128)} %get-tuple-element.38) | copy-start | bytes 2752516
  41.9 93.1 %collective-permute-start.22 = (f32[336,2048]{1,0:T(8,128)}, f32[336,2048]{1,0:T(8,128)}, u32[]{:S(2)}, u32[]{:S(2)}) collective-permute-start(f32[336,2048]{1,0:T(8,128)} %broadcast_select_fusion), channel_id=1, source_target_pairs={{0,1},{1,0},{2,3},{3,2},{4,5},{5,4},{6,7},{7,6},{8,9},{9,8},{10,11... | collective-permute-start | bytes 8257544 | tf_op jit(solution)/shard_map/ppermute | solution.py:101
  43.6 27.5 %all-to-all-start = ((f32[4,448,256]{2,1,0:T(8,128)}), f32[4,448,256]{2,1,0:T(8,128)}, u32[]{:S(2)}, u32[]{:S(2)}) async-start(f32[4,448,256]{2,1,0:T(8,128)} %pad_maximum_fusion.1), calls=%async_computation | async-start | bytes 3670016 | tf_op jit(solution)/shard_map/all_to_all | solution.py:34
  48.0 21.4 %collective-permute-start.6 = (f32[112,2048]{1,0:T(8,128)}, f32[112,2048]{1,0:T(8,128)S(1)}, u32[]{:S(2)}, u32[]{:S(2)}) collective-permute-start(f32[112,2048]{1,0:T(8,128)} %collective-permute-done.4), channel_id=1, source_target_pairs={{0,16},{1,65},{2,18},{3,67},{4,20},{5,69},{6,22},{7,71},{8,24},{9,... | collective-permute-start | bytes 2752520 | tf_op jit(solution)/shard_map/ppermute | solution.py:29
  49.1 21.1 %collective-permute-start.5 = (f32[112,2048]{1,0:T(8,128)}, f32[112,2048]{1,0:T(8,128)S(1)}, u32[]{:S(2)}, u32[]{:S(2)}) collective-permute-start(f32[112,2048]{1,0:T(8,128)} %collective-permute-done.1), channel_id=1, source_target_pairs={{0,48},{1,193},{2,50},{3,195},{4,52},{5,197},{6,54},{7,199},{8,56}... | collective-permute-start | bytes 2752520 | tf_op jit(solution)/shard_map/ppermute | solution.py:29
  71.1 2.1 %copy-start.4 = (bf16[4096,2,112]{0,2,1:T(8,128)(2,1)S(1)}, bf16[4096,2,112]{0,2,1:T(8,128)(2,1)}, u32[]{:S(2)}) copy-start(bf16[4096,2,112]{0,2,1:T(8,128)(2,1)} %param.8) | copy-start | bytes 5505028
  73.6 1.0 copy-start.5
  74.6 1.0 copy-start.6
  74.6 1.2 copy-start.7
  76.6 9.3 %collective-permute-start.12 = (f32[64,2048]{1,0:T(8,128)S(1)}, f32[64,2048]{1,0:T(8,128)S(1)}, u32[]{:S(2)}, u32[]{:S(2)}) collective-permute-start(f32[64,2048]{1,0:T(8,128)S(1)} %pad_maximum_fusion.14), channel_id=1, source_target_pairs={{0,64},{1,17},{2,66},{3,19},{4,68},{5,21},{6,70},{7,23},{8,72},{9,... | collective-permute-start | bytes 1572872 | tf_op jit(solution)/shard_map/ppermute | solution.py:29
  76.8 9.2 %collective-permute-start.11 = (f32[64,2048]{1,0:T(8,128)S(1)}, f32[64,2048]{1,0:T(8,128)S(1)}, u32[]{:S(2)}, u32[]{:S(2)}) collective-permute-start(f32[64,2048]{1,0:T(8,128)S(1)} %pad_maximum_fusion.13), channel_id=1, source_target_pairs={{0,192},{1,49},{2,194},{3,51},{4,196},{5,53},{6,198},{7,55},{8,200... | collective-permute-start | bytes 1572872 | tf_op jit(solution)/shard_map/ppermute | solution.py:29
  81.8 9.8 %collective-permute-start.8 = (f32[64,2048]{1,0:T(8,128)S(1)}, f32[64,2048]{1,0:T(8,128)S(1)}, u32[]{:S(2)}, u32[]{:S(2)}) collective-permute-start(f32[64,2048]{1,0:T(8,128)S(1)} %pad_maximum_fusion.12), channel_id=1, source_target_pairs={{0,64},{1,17},{2,66},{3,19},{4,68},{5,21},{6,70},{7,23},{8,72},{9,... | collective-permute-start | bytes 1572872 | tf_op jit(solution)/shard_map/ppermute | solution.py:29
  82.1 9.5 %collective-permute-start.7 = (f32[64,2048]{1,0:T(8,128)S(1)}, f32[64,2048]{1,0:T(8,128)S(1)}, u32[]{:S(2)}, u32[]{:S(2)}) collective-permute-start(f32[64,2048]{1,0:T(8,128)S(1)} %pad_maximum_fusion.11), channel_id=1, source_target_pairs={{0,192},{1,49},{2,194},{3,51},{4,196},{5,53},{6,198},{7,55},{8,200... | collective-permute-start | bytes 1572872 | tf_op jit(solution)/shard_map/ppermute | solution.py:29
  86.0 8.5 %collective-permute-start.13 = (f32[64,1024]{1,0:T(8,128)S(1)}, f32[64,1024]{1,0:T(8,128)S(1)}, u32[]{:S(2)}, u32[]{:S(2)}) collective-permute-start(f32[64,1024]{1,0:T(8,128)S(1)} %slice_add_fusion.2), channel_id=1, source_target_pairs={{0,64},{1,17},{2,66},{3,19},{4,68},{5,21},{6,70},{7,23},{8,72},{9,... | collective-permute-start | bytes 786440 | tf_op jit(solution)/shard_map/ppermute | solution.py:29
  87.2 7.4 %collective-permute-start.14 = (f32[64,1024]{1,0:T(8,128)S(1)}, f32[64,1024]{1,0:T(8,128)S(1)}, u32[]{:S(2)}, u32[]{:S(2)}) collective-permute-start(f32[64,1024]{1,0:T(8,128)S(1)} %slice_add_fusion.1), channel_id=1, source_target_pairs={{0,192},{1,49},{2,194},{3,51},{4,196},{5,53},{6,198},{7,55},{8,200... | collective-permute-start | bytes 786440 | tf_op jit(solution)/shard_map/ppermute | solution.py:29
  91.7 6.6 %collective-permute-start.9 = (f32[64,1024]{1,0:T(8,128)S(1)}, f32[64,1024]{1,0:T(8,128)S(1)}, u32[]{:S(2)}, u32[]{:S(2)}) collective-permute-start(f32[64,1024]{1,0:T(8,128)S(1)} %slice_add_fusion.6), channel_id=1, source_target_pairs={{0,64},{1,17},{2,66},{3,19},{4,68},{5,21},{6,70},{7,23},{8,72},{9,... | collective-permute-start | bytes 786440 | tf_op jit(solution)/shard_map/ppermute | solution.py:29
  92.8 5.5 %collective-permute-start.10 = (f32[64,1024]{1,0:T(8,128)S(1)}, f32[64,1024]{1,0:T(8,128)S(1)}, u32[]{:S(2)}, u32[]{:S(2)}) collective-permute-start(f32[64,1024]{1,0:T(8,128)S(1)} %slice_add_fusion.5), channel_id=1, source_target_pairs={{0,192},{1,49},{2,194},{3,51},{4,196},{5,53},{6,198},{7,55},{8,200... | collective-permute-start | bytes 786440 | tf_op jit(solution)/shard_map/ppermute | solution.py:29
  98.6 8.9 %collective-permute-start.15 = (f32[16,3072]{1,0:T(8,128)S(1)}, f32[16,3072]{1,0:T(8,128)S(1)}, u32[]{:S(2)}, u32[]{:S(2)}) collective-permute-start(f32[16,3072]{1,0:T(8,128)S(1)} %pad_maximum_fusion.16), channel_id=1, source_target_pairs={{0,4},{1,5},{2,6},{3,7},{4,8},{5,9},{6,10},{7,11},{8,12},{9,13},{1... | collective-permute-start | bytes 589832 | tf_op jit(solution)/shard_map/ppermute | solution.py:29
  102.9 8.8 %collective-permute-start.16 = (f32[16,3072]{1,0:T(8,128)S(1)}, f32[16,3072]{1,0:T(8,128)S(1)}, u32[]{:S(2)}, u32[]{:S(2)}) collective-permute-start(f32[16,3072]{1,0:T(8,128)S(1)} %fusion.25), channel_id=1, source_target_pairs={{0,12},{1,13},{2,14},{3,15},{4,0},{5,1},{6,2},{7,3},{8,4},{9,5},{1... | collective-permute-start | bytes 589832 | tf_op jit(solution)/shard_map/ppermute | solution.py:29
  111.8 4.2 %collective-permute-start.17 = (f32[16,2048]{1,0:T(8,128)S(1)}, f32[16,2048]{1,0:T(8,128)S(1)}, u32[]{:S(2)}, u32[]{:S(2)}) collective-permute-start(f32[16,2048]{1,0:T(8,128)S(1)} %slice_add_fusion.9), channel_id=1, source_target_pairs={{0,2},{1,3},{2,4},{3,5},{4,6},{5,7},{6,8},{7,9},{8,10},{9,11},{10,... | collective-permute-start | bytes 393224 | tf_op jit(solution)/shard_map/ppermute | solution.py:29
  112.1 5.3 %collective-permute-start.18 = (f32[16,2048]{1,0:T(8,128)S(1)}, f32[16,2048]{1,0:T(8,128)S(1)}, u32[]{:S(2)}, u32[]{:S(2)}) collective-permute-start(f32[16,2048]{1,0:T(8,128)S(1)} %slice_add_fusion.8), channel_id=1, source_target_pairs={{0,14},{1,15},{2,0},{3,1},{4,2},{5,3},{6,4},{7,5},{8,6},{9,7},{10,... | collective-permute-start | bytes 393224 | tf_op jit(solution)/shard_map/ppermute | solution.py:29
  113.3 5.4 %collective-permute-start.19 = (f32[16,2048]{1,0:T(8,128)S(1)}, f32[16,2048]{1,0:T(8,128)S(1)}, u32[]{:S(2)}, u32[]{:S(2)}) collective-permute-start(f32[16,2048]{1,0:T(8,128)S(1)} %fusion.27), channel_id=1, source_target_pairs={{0,4},{1,5},{2,6},{3,7},{4,8},{5,9},{6,10},{7,11},{8,12},{9,13},{1... | collective-permute-start | bytes 393224 | tf_op jit(solution)/shard_map/ppermute | solution.py:29
  114.6 8.6 %collective-permute-start.20 = (f32[16,2048]{1,0:T(8,128)S(1)}, f32[16,2048]{1,0:T(8,128)S(1)}, u32[]{:S(2)}, u32[]{:S(2)}) collective-permute-start(f32[16,2048]{1,0:T(8,128)S(1)} %pad_maximum_fusion.17), channel_id=1, source_target_pairs={{0,12},{1,13},{2,14},{3,15},{4,0},{5,1},{6,2},{7,3},{8,4},{9,5},{1... | collective-permute-start | bytes 393224 | tf_op jit(solution)/shard_map/ppermute | solution.py:29
  123.3 17.2 %collective-permute-start.21 = (f32[8,2048]{1,0:T(8,128)S(1)}, f32[8,2048]{1,0:T(8,128)S(1)}, u32[]{:S(2)}, u32[]{:S(2)}) collective-permute-start(f32[8,2048]{1,0:T(8,128)S(1)} %dynamic-slice_bitcast_fusion.8), channel_id=1, source_target_pairs={{0,1},{1,0},{2,3},{3,2},{4,5},{5,4},{6,7},{7,6},{8,9},{9,8},{10,11... | collective-permute-start | bytes 196616 | tf_op jit(solution)/shard_map/ppermute | solution.py:149
  135.0 6.1 %copy-start.1 = (bf16[112,4096]{1,0:T(8,128)(2,1)S(1)}, bf16[112,4096]{1,0:T(8,128)(2,1)}, u32[]{:S(2)}) copy-start(bf16[112,4096]{1,0:T(8,128)(2,1)} %param.9) | copy-start | bytes 2752516
